TPU v7x, 128 devices: a whole 4x4x4 slice. The times are simulated.
128 devices in a mesh: dp: 16 (over x_hi, z, core), tensor: 8 (over y, x_lo).
Axes of the slice: x: 4 (x_hi: 2, x_lo: 2; x = x_hi * 2 + x_lo), y: 4, z: 4, core: 2. Of those that a mesh axis runs over, the one named last changes fastest.
Arguments:
- latents: bfloat16 [176, 256, 640], P('dp', 'tensor'), may hold values from -6 to 6
- cotangent: bfloat16 [176, 256, 640], P('dp', 'tensor'), may hold values from -6 to 6
- trunc_steps: int32 [16], replicated, may hold values from 30 to 40, as said below
- timesteps: int32 [176], replicated, may hold values from 100 to 900
- tile_map: int32 [176], replicated, may hold values from 0 to 175, as said below
- gain: float32 [640], replicated, may hold values from 0.5 to 1.5
- w_value: bfloat16 [640, 2560], P(None, 'tensor'), may hold values from -0.25 to 0.25
- w_gate: bfloat16 [640, 2560], P(None, 'tensor'), may hold values from -0.25 to 0.25
- w_out: bfloat16 [640, 2560], P(None, 'tensor'), may hold values from -0.125 to 0.125
Outputs:
- placed_grad: bfloat16 [176, 256, 640], P('dp', 'tensor')
- grad_value: float32 [640, 2560], P('dp', 'tensor')
- grad_gate: float32 [640, 2560], P('dp', 'tensor')
- grad_out_proj: float32 [640, 2560], P('dp', 'tensor')
- grad_gain: float32 [640], replicated
Inputs may be any that keep to these rules, and one draw needn't show every extreme that they name: trunc_steps lies in 30 to 40, so a prompt has 1 to 11 live slots, its lowest ones. tile_map is a permutation of 0 to 175. Output slots g * 11 to g * 11 + 10 form group g; the live items go to the lowest slots of the groups, and each group receives the floor or the ceiling of (number of live items) / 16 of them.
All inputs are finite; a program needn't handle non-finite values.
Results may differ from a plain program's by a relative error of at most 0.0068.
Values may be sent and summed in bfloat16 or wider, within the bound.
No kernel may reach another device: no remote copies, remote signals or barrier semaphores. Data moves between devices by JAX's collectives and lax.ppermute only.
A program may use at most 64 MiB of HBM per device.

v0:
```python
import jax
import jax.numpy as jnp
import numpy as np
from jax import lax
from jax.experimental import pallas as pl
from jax.experimental.pallas import tpu as pltpu
from jax.sharding import Mesh
from jax.sharding import PartitionSpec as P


TENSOR = ("y", "xl")
DP = ("xh", "z", "c")
EPS = 1e-05
PLACES = 3
BF = jnp.bfloat16
F32 = jnp.float32

VMEM = pltpu.MemorySpace.VMEM
SMEM = pltpu.MemorySpace.SMEM


def noise_table():
    betas = np.linspace(0.00085**0.5, 0.012**0.5, 1000) ** 2
    abar = np.exp(np.cumsum(np.log1p(-betas)))
    return jnp.asarray(np.sqrt(1.0 - abar), F32)


def swap(x, axis):
    return lax.ppermute(x, axis, [(0, 1), (1, 0)])


def ring(x, axis, step):
    return lax.ppermute(x, axis, [(i, (i + step) % 4) for i in range(4)])


def vmem(n):
    return [pl.BlockSpec(memory_space=VMEM)] * n


def smem(n):
    return [pl.BlockSpec(memory_space=SMEM)] * n


def index_kernel(meta, trunc, tmap, dest_g, dest_r, src_p, src_r, most, cnt):
    me = meta[0]

    def clear(i, _):
        cnt[i] = 0
        return 0

    lax.fori_loop(0, 256, clear, 0)

    def prompt(p, top):
        alive = trunc[p] - 29

        def slot(k, top):
            m = tmap[p * 11 + k]
            g = lax.div(m, 11)
            s = m - g * 11
            live = k < alive
            at = p * 16 + g
            r = cnt[at]

            @pl.when(live)
            def _():
                cnt[at] = r + 1

            rank = jnp.where(live, r, -1)

            @pl.when(p == me)
            def _():
                dest_g[k] = g
                dest_r[k] = rank

            @pl.when(g == me)
            def _():
                src_p[s] = p
                src_r[s] = rank

            return jnp.maximum(top, rank + 1)

        return lax.fori_loop(0, 11, slot, top)

    most[0] = lax.fori_loop(0, 16, prompt, jnp.int32(0))


def index_work(meta, trunc, tmap):
    i11 = jax.ShapeDtypeStruct((11,), jnp.int32)
    return pl.pallas_call(
        index_kernel,
        out_shape=(i11, i11, i11, i11, jax.ShapeDtypeStruct((1,), jnp.int32)),
        in_specs=smem(3),
        out_specs=tuple(smem(5)),
        scratch_shapes=[pltpu.SMEM((256,), jnp.int32)],
        name="routes",
    )(meta, trunc, tmap)


def halves_kernel(meta, wv, wg, wo, half):
    for j, w in enumerate((wv, wg, wo)):
        half[j] = w[...]


def halves(meta, wv, wg, wo):
    mine = pl.BlockSpec((160, 640), lambda i, meta: (meta[1], 0))
    return pl.pallas_call(
        halves_kernel,
        grid_spec=pltpu.PrefetchScalarGridSpec(
            num_scalar_prefetch=1,
            grid=(1,),
            in_specs=[mine] * 3,
            out_specs=pl.BlockSpec((3, 160, 640), lambda i, meta: (0, 0, 0)),
        ),
        out_shape=jax.ShapeDtypeStruct((3, 160, 640), BF),
        name="halves",
    )(meta, wv, wg, wo)


def normalise(tile):
    x = tile.astype(F32)
    centred = x - jnp.mean(x, axis=-1, keepdims=True)
    inv_std = lax.rsqrt(jnp.mean(centred * centred, axis=-1, keepdims=True) + EPS)
    return centred * inv_std, inv_std


def prologue_kernel(meta, trunc, times, table, lat, cot, gain, rows):
    me = meta[0]
    alive = trunc[me] - 29
    for k in range(11):
        scale = jnp.where(k < alive, table[times[me * 11 + k]], 0.0)
        x_hat, _ = normalise(lat[k])
        rows[0, k] = (x_hat * gain[...]).astype(BF)
        rows[1, k] = (cot[k].astype(F32) * scale).astype(BF)


def prologue(meta, trunc, times, table, lat, cot, gain):
    return pl.pallas_call(
        prologue_kernel,
        out_shape=jax.ShapeDtypeStruct((2, 11, 32, 640), BF),
        in_specs=smem(4) + vmem(3),
        out_specs=vmem(1)[0],
        name="prologue",
    )(meta, trunc, times, table, lat, cot, gain)


LAST = (((1,), (1,)), ((), ()))
PLAIN = (((1,), (0,)), ((), ()))


def dot(a, b, dims=PLAIN):
    return lax.dot_general(a, b, dims, preferred_element_type=F32)


def load_rows(own, other, rows, turned):
    for j in range(2):
        rows[j, :352] = own[j]
        rows[j, 352:] = other[j]
        turned[j] = rows[j].T


def hidden_part(rows, w, acts, start, width):
    span = slice(start, start + width)
    value = dot(rows[0], w[0, span], LAST)
    gate = dot(rows[0], w[1, span], LAST)
    d_hidden = dot(rows[1], w[2, span], LAST)
    cdf = 0.5 * (1.0 + lax.erf(gate * 0.7071067811865476))
    density = jnp.exp(-0.5 * gate * gate) * 0.3989422804014327
    gelu = gate * cdf
    acts[0, :, span] = (d_hidden * gelu).astype(BF)
    acts[1, :, span] = (d_hidden * value * (cdf + gate * density)).astype(BF)
    acts[2, :, span] = (value * gelu).astype(BF)


def near_kernel(meta, own, other, wv, wg, wo, below, below2, above, above2, dn, mine, send,
                rows, turned, w, acts, keep):
    c = meta[1]
    here = pl.multiple_of(c * 160, 16)
    there = pl.multiple_of((1 - c) * 160, 16)
    load_rows(own, other, rows, turned)
    for j, ref in enumerate((wv, wg, wo)):
        w[j, :320] = ref[...]
        w[j, pl.ds(320 + here, 160)] = above[j]
        w[j, pl.ds(320 + there, 160)] = above2[j]
        w[j, pl.ds(640 + here, 160)] = below[j]
        w[j, pl.ds(640 + there, 160)] = below2[j]
    for start, width in ((0, 256), (256, 256), (512, 256), (768, 192)):
        hidden_part(rows, w, acts, start, width)
    dn[...] = dot(acts[0], w[0]) + dot(acts[1], w[1])
    for j in range(3):
        keep[...] = dot(turned[j // 2], acts[j]).reshape(8, 2, 40, 960)
        for out, side in ((mine, c), (send, 1 - c)):
            both = keep[:, side].reshape(320, 960)
            out[0, j] = both[:, :320].reshape(8, 40, 320).astype(BF)
            mid = pltpu.roll(both[:, 256:640], 320, 1)[:, :320]
            out[1, j] = mid.reshape(8, 40, 320).astype(BF)
            out[2, j] = both[:, 640:].reshape(8, 40, 320).astype(BF)


def near_block(meta, own, other, wv, wg, wo, below, below2, above, above2):
    grads = jax.ShapeDtypeStruct((3, 3, 8, 40, 320), BF)
    return pl.pallas_call(
        near_kernel,
        out_shape=(jax.ShapeDtypeStruct((704, 640), F32), grads, grads),
        in_specs=smem(1) + vmem(9),
        out_specs=tuple(vmem(3)),
        scratch_shapes=[
            pltpu.VMEM((2, 704, 640), BF),
            pltpu.VMEM((2, 640, 704), BF),
            pltpu.VMEM((3, 960, 640), BF),
            pltpu.VMEM((3, 704, 960), BF),
            pltpu.VMEM((8, 2, 40, 960), F32),
        ],
        compiler_params=pltpu.CompilerParams(vmem_limit_bytes=56 * 2**20),
        name="near_block",
    )(meta, own, other, wv, wg, wo, below, below2, above, above2)


def split_gain(g):
    g = jnp.broadcast_to(g, (8, 640))
    low = g[:, :320]
    high = pltpu.roll(g[:, 256:], 320, 1)[:, :320]
    row = lax.broadcasted_iota(jnp.int32, (8, 320), 0)
    value = jnp.where(row % 2 == 0, low, high)
    top = value.astype(BF).astype(F32)
    return jnp.where(row < 2, top, jnp.where(row < 4, value - top, 0.0))


def resplit(g):
    row = lax.broadcasted_iota(jnp.int32, (8, 320), 0)
    value = jnp.where(row < 2, g, pltpu.roll(g, 2, 0))
    top = value.astype(BF).astype(F32)
    return jnp.where(row < 2, top, jnp.where(row < 4, value - top, 0.0))


def joined(rows):
    rows = rows.astype(F32)
    return rows + pltpu.roll(rows, 6, 0)


def far_kernel(meta, own, other, gain, near_dn, first, second, dn, dn_send, mine, send,
               rows, turned, w, acts, keep):
    c = meta[1]
    here = pl.multiple_of(c * 160, 16)
    there = pl.multiple_of((1 - c) * 160, 16)
    load_rows(own, other, rows, turned)
    for j in range(3):
        w[j, pl.ds(here, 160)] = first[j]
        w[j, pl.ds(there, 160)] = second[j]
    hidden_part(rows, w, acts, 0, 320)
    total = near_dn[...] + dot(acts[0], w[0]) + dot(acts[1], w[1])
    dn[...] = total[:352]
    dn_send[...] = total[352:].astype(BF)
    gsum = jnp.sum(total * rows[0].astype(F32), axis=0, keepdims=True) / gain[...]
    tail = split_gain(gsum).astype(BF)
    for j in range(3):
        keep[...] = dot(turned[j // 2], acts[j]).reshape(8, 2, 40, 320)
        for out, side in ((mine, c), (send, 1 - c)):
            out[8 * j : 8 * j + 8] = keep[:, side].astype(BF)
    for out in (mine, send):
        out[24] = jnp.zeros((40, 320), BF)
        out[24, :8] = tail


def far_block(meta, own, other, gain, near_dn, first, second):
    grads = jax.ShapeDtypeStruct((25, 40, 320), BF)
    return pl.pallas_call(
        far_kernel,
        out_shape=(
            jax.ShapeDtypeStruct((352, 640), F32),
            jax.ShapeDtypeStruct((352, 640), BF),
            grads,
            grads,
        ),
        in_specs=smem(1) + vmem(6),
        out_specs=tuple(vmem(4)),
        scratch_shapes=[
            pltpu.VMEM((2, 704, 640), BF),
            pltpu.VMEM((2, 640, 704), BF),
            pltpu.VMEM((3, 320, 640), BF),
            pltpu.VMEM((3, 704, 320), BF),
            pltpu.VMEM((8, 2, 40, 320), F32),
        ],
        compiler_params=pltpu.CompilerParams(vmem_limit_bytes=56 * 2**20),
        name="far_block",
    )(meta, own, other, gain, near_dn, first, second)


def finish_kernel(dest_g, dest_r, dn, got, lat, grad, gain, own, packed, sems):
    def sent(k):
        rank = dest_r[k]
        return (rank >= 0) & (rank < PLACES)

    for k in range(11):
        x_hat, inv_std = normalise(lat[k])
        d_hat = (dn[k] + got[k].astype(F32)) * gain[...]
        out = grad[1, k].astype(F32) + inv_std * (
            d_hat
            - jnp.mean(d_hat, axis=-1, keepdims=True)
            - x_hat * jnp.mean(d_hat * x_hat, axis=-1, keepdims=True)
        )
        own[k] = jnp.where(dest_r[k] >= 0, out, 0.0).astype(BF)

        @pl.when(sent(k))
        def _():
            place = dest_g[k] * PLACES + dest_r[k]
            pltpu.make_async_copy(own.at[k], packed.at[place], sems.at[k]).start()

    for k in range(11):

        @pl.when(sent(k))
        def _():
            pltpu.make_async_copy(own.at[k], packed.at[0], sems.at[k]).wait()


def finish(dest_g, dest_r, dn, got, lat, grad, gain):
    return pl.pallas_call(
        finish_kernel,
        out_shape=(
            jax.ShapeDtypeStruct((11, 32, 640), BF),
            jax.ShapeDtypeStruct((16 * PLACES, 32, 640), BF),
        ),
        in_specs=smem(2) + vmem(5),
        out_specs=(vmem(1)[0], pl.BlockSpec(memory_space=pl.ANY)),
        scratch_shapes=[pltpu.SemaphoreType.DMA((11,))],
        name="finish",
    )(dest_g, dest_r, dn, got, lat, grad, gain)


def unpack_kernel(src_p, src_r, came, placed, blank, sems):
    blank[...] = jnp.zeros_like(blank)
    for s in range(11):
        rank = src_r[s]

        @pl.when((rank >= 0) & (rank < PLACES))
        def _():
            pltpu.make_async_copy(
                came.at[src_p[s] * PLACES + rank], placed.at[s], sems.at[s]
            ).start()

        @pl.when((rank < 0) | (rank >= PLACES))
        def _():
            pltpu.make_async_copy(blank, placed.at[s], sems.at[s]).start()

    for s in range(11):
        pltpu.make_async_copy(blank, placed.at[s], sems.at[s]).wait()


def unpack(src_p, src_r, came):
    return pl.pallas_call(
        unpack_kernel,
        out_shape=jax.ShapeDtypeStruct((11, 32, 640), BF),
        in_specs=smem(2) + [pl.BlockSpec(memory_space=pl.ANY)],
        out_specs=pl.BlockSpec(memory_space=pl.ANY),
        scratch_shapes=[pltpu.VMEM((32, 640), BF), pltpu.SemaphoreType.DMA((11,))],
        name="unpack",
    )(src_p, src_r, came)


def local(kernel, out_shapes, *arrays):
    return pl.pallas_call(
        kernel,
        out_shape=tuple(jax.ShapeDtypeStruct(s, d) for s, d in out_shapes),
        in_specs=vmem(len(arrays)),
        out_specs=tuple(vmem(len(out_shapes))),
        compiler_params=pltpu.CompilerParams(vmem_limit_bytes=32 * 2**20),
    )(*arrays)


def near_sums_kernel(mine, got, own, up, down):
    own[...] = mine[0].astype(F32) + got[0].astype(F32)
    up[...] = (mine[1].astype(F32) + got[1].astype(F32)).astype(BF)
    down[...] = (mine[2].astype(F32) + got[2].astype(F32)).astype(BF)


def far_sums_kernel(mine, got, lower, upper, tail):
    for j in range(3):
        for out, at in ((lower, 8 * j), (upper, 8 * j + 4)):
            out[j] = (mine[at : at + 4].astype(F32) + got[at : at + 4].astype(F32)).astype(BF)
    tail[...] = joined(mine[24, :8]) + joined(got[24, :8])


def over_y_kernel(own, from_down, from_up, far_lower, far_upper, g0, g1, g2, g3, out):
    for j in range(3):
        for half, far in ((0, far_lower), (4, far_upper)):
            at = slice(half, half + 4)
            x = own[j, at] + from_down[j, at].astype(F32)
            x = x + (from_up[j, at].astype(F32) + far[j].astype(F32))
            out[at, 5 * j : 5 * j + 5] = x.astype(BF).reshape(4, 5, 8, 320)
    tail = resplit((g0[...] + g1[...]) + (g2[...] + g3[...])).astype(BF)
    for k in range(8):
        out[k, 15] = tail


def last_kernel(parts, value, gate, out, tail):
    total = parts[0].astype(F32)
    for k in range(1, 8):
        total = total + parts[k].astype(F32)
    for j, ref in enumerate((value, gate, out)):
        ref[...] = total[5 * j : 5 * j + 5].reshape(40, 320)
    tail[...] = joined(total[15])


def reduce_weights(near_mine, near_got, far_mine, far_got):
    grads = (3, 8, 40, 320)
    half = (3, 4, 40, 320)
    row = ((8, 320), F32)
    own, up, down = local(
        near_sums_kernel, ((grads, F32), (grads, BF), (grads, BF)), near_mine, near_got
    )
    from_down = ring(up, "y", 1)
    from_up = ring(down, "y", -1)
    lower, upper, tail = local(
        far_sums_kernel, ((half, BF), (half, BF), row), far_mine, far_got
    )
    lower = ring(lower, "y", 1)
    upper = ring(upper, "y", -1)
    lower = ring(lower, "y", 1)
    upper = ring(upper, "y", -1)
    tail = tail + swap(tail, "xl")
    tails = [tail] + [ring(tail, "y", d) for d in (2, 1, -1)]
    (parts,) = local(
        over_y_kernel, (((8, 16, 8, 320), BF),),
        own, from_down, from_up, lower, upper, *tails,
    )
    parts = lax.all_to_all(parts, ("xh", "z"), 0, 0, tiled=True)
    out = ((40, 320), F32)
    value, gate, proj, tail = local(last_kernel, (out, out, out, row), parts)
    return value, gate, proj, tail[:2].reshape(640)


def route(packed):
    return lax.all_to_all(packed, DP, 0, 0, tiled=True)


def more_rounds(placed, own, most, dest_g, dest_r, src_p, src_r):
    def more(state):
        return state[0] * PLACES < most[0]

    def one(state):
        t, placed = state
        rank = dest_r - t * PLACES
        here = (rank >= 0) & (rank < PLACES) & (dest_r >= 0)
        place = jnp.where(here, dest_g * PLACES + rank, -1)
        hit = place[None, :] == jnp.arange(16 * PLACES, dtype=jnp.int32)[:, None]
        pick = jnp.sum(jnp.where(hit, jnp.arange(11, dtype=jnp.int32)[None, :], 0), axis=1)
        came = route(jnp.take(own, pick, axis=0))
        rank = src_r - t * PLACES
        here = (rank >= 0) & (rank < PLACES) & (src_r >= 0)
        new = jnp.take(came, jnp.where(here, src_p * PLACES + rank, 0), axis=0)
        return t + 1, jnp.where(here[:, None, None], new, placed)

    return lax.while_loop(more, one, (jnp.int32(1), placed))[1]


def per_device(latents, cotangent, trunc, times, tmap, gain, w_value, w_gate, w_out):
    meta = jnp.stack([lax.axis_index(a) for a in (DP, "c")]).astype(jnp.int32)
    gain = gain[None, :]
    wv, wg, wo = w_value.T, w_gate.T, w_out.T
    rows = prologue(meta, trunc, times, noise_table(), latents, cotangent, gain)
    other = swap(rows, "xl")
    half = halves(meta, wv, wg, wo)
    below = ring(half, "y", 1)
    above = ring(half, "y", -1)
    dest_g, dest_r, src_p, src_r, most = index_work(meta, trunc, tmap)
    below2 = swap(below, "c")
    above2 = swap(above, "c")
    first = ring(below, "y", 1)
    second = ring(above2, "y", -1)
    rows2 = rows.reshape(2, 352, 640)
    other = other.reshape(2, 352, 640)
    near_dn, near_mine, near_send = near_block(
        meta, rows2, other, wv, wg, wo, below, below2, above, above2
    )
    near_got = swap(near_send, "c")
    dn, dn_send, far_mine, far_send = far_block(meta, rows2, other, gain, near_dn, first, second)
    got = swap(dn_send, "xl")
    far_got = swap(far_send, "c")
    tiles = (11, 32, 640)
    own, packed = finish(
        dest_g, dest_r, dn.reshape(tiles), got.reshape(tiles), latents, rows, gain
    )
    came = route(packed)
    placed = unpack(src_p, src_r, came)
    placed = more_rounds(placed, own, most, dest_g, dest_r, src_p, src_r)
    grads = reduce_weights(near_mine, near_got, far_mine, far_got)
    return placed, *grads


def solution(mesh):
    split = Mesh(mesh.devices.reshape(2, 4, 2, 4, 2), ("xh", "z", "c", "y", "xl"))
    tiles = P(DP, TENSOR, None)
    weights = P(None, TENSOR)

    def step(*args):
        return per_device(*args)

    step = jax.shard_map(
        step,
        mesh=split,
        in_specs=(tiles, tiles, P(), P(), P(), P(), weights, weights, weights),
        out_specs=(tiles, P(DP, TENSOR), P(DP, TENSOR), P(DP, TENSOR), P()),
        check_vma=False,
    )
    return step
```

profile of v0, /device:TPU:0, one launch (start us, length us, event | category | flops | bytes accessed | tf_op | source)
XLA Modules:
  0.0 167.5 jit_solution(17354749357373329751)
XLA Ops:
  0.6 0.6 pad_add_fusion.meta
  1.2 2.7 %halves.1 = bf16[3,160,640]{2,1,0:T(8,128)(2,1)} custom-call(s32[2]{0:T(128)} %pad_add_fusion.meta, bf16[320,640]{1,0:T(8,128)(2,1)} %bitcast.31, bf16[320,640]{1,0:T(8,128)(2,1)} %bitcast.33, bf16[320,640]{1,0:T(8,128)(2,1)} %bitcast.35), custom_call_target="tpu_custom_call" | custom-call | tf_op jit(solution)/shard_map/halves/pallas_call | solution.py:106
  3.9 3.1 %collective-permute-start.3 = (bf16[3,160,640]{2,1,0:T(8,128)(2,1)}, bf16[3,160,640]{2,1,0:T(8,128)(2,1)S(1)}, u32[]{:S(2)}, u32[]{:S(2)}) collective-permute-start(bf16[3,160,640]{2,1,0:T(8,128)(2,1)} %halves.1), channel_id=1, source_target_pairs={{0,6},{2,0},{4,2},{6,4},{1,7},{3,1},{5,3},{7,5},{8,14},{10,8},{12,... | collective-permute-start | bytes 1843208 | tf_op jit(solution)/shard_map/ppermute | solution.py:33
  7.0 13.4 %collective-permute-done.3.above = bf16[3,160,640]{2,1,0:T(8,128)(2,1)S(1)} collective-permute-done((bf16[3,160,640]{2,1,0:T(8,128)(2,1)}, bf16[3,160,640]{2,1,0:T(8,128)(2,1)S(1)}, u32[]{:S(2)}, u32[]{:S(2)}) %collective-permute-start.3) | collective-permute-done | bytes 614432 | tf_op jit(solution)/shard_map/ppermute | solution.py:33
  20.5 1.3 broadcast_in_dim.52.gain
  21.8 2.5 %prologue.1.grad = bf16[2,11,32,640]{3,2,1,0:T(8,128)(2,1)} custom-call(s32[2]{0:T(128)} %pad_add_fusion.meta, s32[16]{0:T(128)} %trunc.3, s32[176]{0:T(256)} %times.1, f32[1000]{0:T(1024)} %constant.64.clone.table, bf16[11,32,640]{2,1,0:T(8,128)(2,1)} %lat.3, bf16[11,32,640]{2,1,0:T(8,128)(2,1)} %cot.1, f32[1,640]{1,0:T(1,128)} %broadcast_in_dim.52.gain), custom_call_target="tpu_custom_call" | custom-call | tf_op jit(solution)/shard_map/prologue/pallas_call | solution.py:137
  24.3 1.5 collective-permute-start
  25.7 0.2 collective-permute-start.2
  26.0 0.9 collective-permute-start.5
  26.9 2.7 %collective-permute-start.6 = (bf16[3,160,640]{2,1,0:T(8,128)(2,1)S(1)}, bf16[3,160,640]{2,1,0:T(8,128)(2,1)S(1)}, u32[]{:S(2)}, u32[]{:S(2)}) collective-permute-start(bf16[3,160,640]{2,1,0:T(8,128)(2,1)S(1)} %collective-permute-done.4.above2), channel_id=1, source_target_pairs={{0,6},{2,0},{4,2},{6,4},{1,7},{3,1},{5,3},{7,5},{8,14},{10,8},{12,... | collective-permute-start | bytes 1843208 | tf_op jit(solution)/shard_map/ppermute | solution.py:33
  29.6 17.2 %collective-permute-done = bf16[2,11,32,640]{3,2,1,0:T(8,128)(2,1)S(1)} collective-permute-done((bf16[2,11,32,640]{3,2,1,0:T(8,128)(2,1)}, bf16[2,11,32,640]{3,2,1,0:T(8,128)(2,1)S(1)}, u32[]{:S(2)}, u32[]{:S(2)}) %collective-permute-start) | collective-permute-done | bytes 901152 | tf_op jit(solution)/shard_map/ppermute | solution.py:29
  46.9 0.9 copy-done.3
  47.8 0.2 copy-done.9
  48.0 14.5 %near_block.1 = (f32[704,640]{1,0:T(8,128)}, bf16[3,3,8,40,320]{4,3,2,1,0:T(8,128)(2,1)}, bf16[3,3,8,40,320]{4,3,2,1,0:T(8,128)(2,1)}) custom-call(s32[2]{0:T(128)} %pad_add_fusion.meta, bf16[2,352,640]{2,1,0:T(8,128)(2,1)} %bitcast.27, bf16[2,352,640]{2,1,0:T(8,128)(2,1)} %bitcast.29, bf16[320,640]{1,0:T(8,128)(2,1)} %bitcast.32, ...), custom_call_target="tpu_custom_call" | custom-call | tf_op jit(solution)/shard_map/near_block/pallas_call | solution.py:201
  62.6 0.8 copy-done.4
  63.4 0.2 copy-done.5
  63.6 8.0 %far_block.1 = (f32[352,640]{1,0:T(8,128)}, bf16[352,640]{1,0:T(8,128)(2,1)}, bf16[25,40,320]{2,1,0:T(8,128)(2,1)}, bf16[25,40,320]{2,1,0:T(8,128)(2,1)}) custom-call(s32[2]{0:T(128)} %pad_add_fusion.meta, bf16[2,352,640]{2,1,0:T(8,128)(2,1)} %bitcast.28, bf16[2,352,640]{2,1,0:T(8,128)(2,1)} %bitcast.30, f32[1,640]{1,0:T(1,128)} %broadcast_in_dim.52.gain, ...), custom_call_target="tpu_custom_call" | custom-call | tf_op jit(solution)/shard_map/far_block/pallas_call | solution.py:266
  71.6 1.5 collective-permute-start.7
  73.1 6.1 %routes.1 = (s32[11]{0:T(128)S(1)}, s32[11]{0:T(128)S(1)}, s32[11]{0:T(128)S(1)}, s32[11]{0:T(128)S(1)}, s32[1]{0:T(128)}) custom-call(s32[2]{0:T(128)} %pad_add_fusion.meta, s32[16]{0:T(128)} %trunc.3, s32[176]{0:T(256)} %tmap.1), custom_call_target="tpu_custom_call" | custom-call | tf_op jit(solution)/shard_map/routes/pallas_call | solution.py:89
  79.2 5.4 %collective-permute-done.7 = bf16[352,640]{1,0:T(8,128)(2,1)S(1)} collective-permute-done((bf16[352,640]{1,0:T(8,128)(2,1)}, bf16[352,640]{1,0:T(8,128)(2,1)S(1)}, u32[]{:S(2)}, u32[]{:S(2)}) %collective-permute-start.7) | collective-permute-done | bytes 450592 | tf_op jit(solution)/shard_map/ppermute | solution.py:29
  84.6 0.8 copy-done.10
  85.3 3.0 %finish.1 = (bf16[11,32,640]{2,1,0:T(8,128)(2,1)S(1)}, bf16[48,32,640]{2,1,0:T(8,128)(2,1)}) custom-call(s32[11]{0:T(128)S(1)} %get-tuple-element.178.dest_g, s32[11]{0:T(128)S(1)} %get-tuple-element.177.dest_r, f32[11,32,640]{2,1,0:T(8,128)} %bitcast.37, bf16[11,32,640]{2,1,0:T(8,128)(2,1)} %bitcast.38, bf16[11,32,640]{2,1,0:T(8,128)(2,1)} %lat.3, ...), custom_call_target="tpu_custom_call" | custom-call | tf_op jit(solution)/shard_map/finish/pallas_call | solution.py:316
  88.4 8.2 %all-to-all-start.1 = ((bf16[48,32,640]{2,1,0:T(8,128)(2,1)}), bf16[48,32,640]{2,1,0:T(8,128)(2,1)}, u32[]{:S(2)}, u32[]{:S(2)}) async-start(bf16[48,32,640]{2,1,0:T(8,128)(2,1)} %get-tuple-element.79), calls=%async_computation.1 | async-start | bytes 3932160 | tf_op jit(solution)/shard_map/all_to_all | solution.py:432
  96.6 0.4 collective-permute-start.11
  97.0 2.2 %collective-permute-done.11.got = bf16[25,40,320]{2,1,0:T(8,128)(2,1)S(1)} collective-permute-done((bf16[25,40,320]{2,1,0:T(8,128)(2,1)}, bf16[25,40,320]{2,1,0:T(8,128)(2,1)S(1)}, u32[]{:S(2)}, u32[]{:S(2)}) %collective-permute-start.11) | collective-permute-done | bytes 640032 | tf_op jit(solution)/shard_map/ppermute | solution.py:29
  99.2 0.2 shard_map.138
  99.3 1.0 collective-permute-start.12
  100.4 2.7 %collective-permute-start.14 = (bf16[3,4,40,320]{3,2,1,0:T(8,128)(2,1)S(1)}, bf16[3,4,40,320]{3,2,1,0:T(8,128)(2,1)S(1)}, u32[]{:S(2)}, u32[]{:S(2)}) collective-permute-start(bf16[3,4,40,320]{3,2,1,0:T(8,128)(2,1)S(1)} %get-tuple-element.91), channel_id=1, source_target_pairs={{0,6},{2,0},{4,2},{6,4},{1,7},{3,1},{5,3},{7,5},{8,14},{10,8},{12,... | collective-permute-start | bytes 921608 | tf_op jit(solution)/shard_map/ppermute | solution.py:33
  103.1 2.2 %shard_map.137 = (f32[3,8,40,320]{3,2,1,0:T(8,128)S(1)}, bf16[3,8,40,320]{3,2,1,0:T(8,128)(2,1)S(1)}, bf16[3,8,40,320]{3,2,1,0:T(8,128)(2,1)S(1)}) custom-call(bf16[3,3,8,40,320]{4,3,2,1,0:T(8,128)(2,1)S(1)} %copy-done, bf16[3,3,8,40,320]{4,3,2,1,0:T(8,128)(2,1)} %collective-permute-done.8.got), custom_call_target="tpu_custom_call" | custom-call | tf_op jit(solution)/shard_map/pallas_call | solution.py:360
  105.3 2.0 %collective-permute-start.10 = (bf16[3,8,40,320]{3,2,1,0:T(8,128)(2,1)S(1)}, bf16[3,8,40,320]{3,2,1,0:T(8,128)(2,1)S(1)}, u32[]{:S(2)}, u32[]{:S(2)}) collective-permute-start(bf16[3,8,40,320]{3,2,1,0:T(8,128)(2,1)S(1)} %get-tuple-element.87), channel_id=1, source_target_pairs={{0,6},{2,0},{4,2},{6,4},{1,7},{3,1},{5,3},{7,5},{8,14},{10,8},{12,... | collective-permute-start | bytes 1843208 | tf_op jit(solution)/shard_map/ppermute | solution.py:33
  107.3 0.1 collective-permute-start.9
  107.4 5.0 %collective-permute-done.12 = bf16[3,4,40,320]{3,2,1,0:T(8,128)(2,1)S(1)} collective-permute-done((bf16[3,4,40,320]{3,2,1,0:T(8,128)(2,1)S(1)}, bf16[3,4,40,320]{3,2,1,0:T(8,128)(2,1)S(1)}, u32[]{:S(2)}, u32[]{:S(2)}) %collective-permute-start.12) | collective-permute-done | bytes 307232 | tf_op jit(solution)/shard_map/ppermute | solution.py:33
  112.4 3.3 %collective-permute-start.15 = (bf16[3,4,40,320]{3,2,1,0:T(8,128)(2,1)S(1)}, bf16[3,4,40,320]{3,2,1,0:T(8,128)(2,1)S(1)}, u32[]{:S(2)}, u32[]{:S(2)}) collective-permute-start(bf16[3,4,40,320]{3,2,1,0:T(8,128)(2,1)S(1)} %collective-permute-done.14), channel_id=1, source_target_pairs={{0,6},{2,0},{4,2},{6,4},{1,7},{3,1},{5,3},{7,5},{8,14},{10,8},{12,... | collective-permute-start | bytes 921608 | tf_op jit(solution)/shard_map/ppermute | solution.py:33
  115.7 0.6 collective-permute-start.16
  116.3 3.7 %collective-permute-done.16 = f32[8,320]{1,0:T(8,128)S(1)} collective-permute-done((f32[8,320]{1,0:T(8,128)S(1)}, f32[8,320]{1,0:T(8,128)S(1)}, u32[]{:S(2)}, u32[]{:S(2)}) %collective-permute-start.16) | collective-permute-done | bytes 10272 | tf_op jit(solution)/shard_map/ppermute | solution.py:29
  120.0 2.5 %collective-permute-start.17 = (f32[8,320]{1,0:T(8,128)S(1)}, f32[8,320]{1,0:T(8,128)S(1)}, u32[]{:S(2)}, u32[]{:S(2)}) collective-permute-start(f32[8,320]{1,0:T(8,128)S(1)} %add.72.g0), channel_id=1, source_target_pairs={{0,4},{2,6},{4,0},{6,2},{1,5},{3,7},{5,1},{7,3},{8,12},{10,14},{12... | collective-permute-start | bytes 30728 | tf_op jit(solution)/shard_map/ppermute | solution.py:33
  122.6 14.6 %collective-permute-done.17.g1 = f32[8,320]{1,0:T(8,128)S(1)} collective-permute-done((f32[8,320]{1,0:T(8,128)S(1)}, f32[8,320]{1,0:T(8,128)S(1)}, u32[]{:S(2)}, u32[]{:S(2)}) %collective-permute-start.17) | collective-permute-done | bytes 10272 | tf_op jit(solution)/shard_map/ppermute | solution.py:33
  137.2 1.1 collective-permute-start.18
  138.3 3.8 %collective-permute-done.18.g2 = f32[8,320]{1,0:T(8,128)S(1)} collective-permute-done((f32[8,320]{1,0:T(8,128)S(1)}, f32[8,320]{1,0:T(8,128)S(1)}, u32[]{:S(2)}, u32[]{:S(2)}) %collective-permute-start.18) | collective-permute-done | bytes 10272 | tf_op jit(solution)/shard_map/ppermute | solution.py:33
  142.1 3.7 %collective-permute-done.19.g3 = f32[8,320]{1,0:T(8,128)S(1)} collective-permute-done((f32[8,320]{1,0:T(8,128)S(1)}, f32[8,320]{1,0:T(8,128)S(1)}, u32[]{:S(2)}, u32[]{:S(2)}) %collective-permute-start.19) | collective-permute-done | bytes 10272 | tf_op jit(solution)/shard_map/ppermute | solution.py:33
  145.8 1.3 shard_map.139
  147.1 6.9 %all-to-all-start.2 = ((bf16[8,16,8,320]{3,2,1,0:T(8,128)(2,1)}), bf16[8,16,8,320]{3,2,1,0:T(8,128)(2,1)S(1)}, u32[]{:S(2)}, u32[]{:S(2)}) async-start(bf16[8,16,8,320]{3,2,1,0:T(8,128)(2,1)} %shard_map.139), calls=%async_computation.2 | async-start | bytes 1572864 | tf_op jit(solution)/shard_map/all_to_all | solution.py:425
  154.0 1.6 unpack.1
  155.5 9.3 %all-to-all-done.2.parts = bf16[8,16,8,320]{3,2,1,0:T(8,128)(2,1)S(1)} async-done(((bf16[8,16,8,320]{3,2,1,0:T(8,128)(2,1)}), bf16[8,16,8,320]{3,2,1,0:T(8,128)(2,1)S(1)}, u32[]{:S(2)}, u32[]{:S(2)}) %all-to-all-start.2) | async-done | bytes 655392 | tf_op jit(solution)/shard_map/all_to_all | solution.py:425
  164.8 0.7 shard_map.140
  165.5 0.7 reshape.131
  166.2 0.6 while.10
  166.8 0.8 copy-done.2
  (35 shorter events, 0.1 us)
Async XLA Ops:
  3.9 16.6 %collective-permute-start.3 = (bf16[3,160,640]{2,1,0:T(8,128)(2,1)}, bf16[3,160,640]{2,1,0:T(8,128)(2,1)S(1)}, u32[]{:S(2)}, u32[]{:S(2)}) collective-permute-start(bf16[3,160,640]{2,1,0:T(8,128)(2,1)} %halves.1), channel_id=1, source_target_pairs={{0,6},{2,0},{4,2},{6,4},{1,7},{3,1},{5,3},{7,5},{8,14},{10,8},{12,... | collective-permute-start | bytes 1843208 | tf_op jit(solution)/shard_map/ppermute | solution.py:33
  7.0 18.7 %collective-permute-start.1 = (bf16[3,160,640]{2,1,0:T(8,128)(2,1)}, bf16[3,160,640]{2,1,0:T(8,128)(2,1)S(1)}, u32[]{:S(2)}, u32[]{:S(2)}) collective-permute-start(bf16[3,160,640]{2,1,0:T(8,128)(2,1)} %halves.1), channel_id=1, source_target_pairs={{0,2},{2,4},{4,6},{6,0},{1,3},{3,5},{5,7},{7,1},{8,10},{10,12},{12... | collective-permute-start | bytes 1843208 | tf_op jit(solution)/shard_map/ppermute | solution.py:33
  20.5 26.4 %copy-start.7 = (bf16[3,160,640]{2,1,0:T(8,128)(2,1)}, bf16[3,160,640]{2,1,0:T(8,128)(2,1)S(1)}, u32[]{:S(2)}) copy-start(bf16[3,160,640]{2,1,0:T(8,128)(2,1)S(1)} %collective-permute-done.3.above) | copy-start | bytes 1843204
  20.5 6.4 %collective-permute-start.4 = (bf16[3,160,640]{2,1,0:T(8,128)(2,1)S(1)}, bf16[3,160,640]{2,1,0:T(8,128)(2,1)S(1)}, u32[]{:S(2)}, u32[]{:S(2)}) collective-permute-start(bf16[3,160,640]{2,1,0:T(8,128)(2,1)S(1)} %collective-permute-done.3.above), channel_id=1, source_target_pairs={{0,8},{8,0},{1,9},{9,1},{2,10},{10,2},{3,11},{11,3},{4,12},{12,4},... | collective-permute-start | bytes 1843208 | tf_op jit(solution)/shard_map/ppermute | solution.py:29
  24.3 22.6 %collective-permute-start = (bf16[2,11,32,640]{3,2,1,0:T(8,128)(2,1)}, bf16[2,11,32,640]{3,2,1,0:T(8,128)(2,1)S(1)}, u32[]{:S(2)}, u32[]{:S(2)}) collective-permute-start(bf16[2,11,32,640]{3,2,1,0:T(8,128)(2,1)} %prologue.1.grad), channel_id=1, source_target_pairs={{0,1},{1,0},{2,3},{3,2},{4,5},{5,4},{6,7},{7,6},{8,9},{9,8},{10,11... | collective-permute-start | bytes 2703368 | tf_op jit(solution)/shard_map/ppermute | solution.py:29
  25.7 21.1 %copy-start.6 = (bf16[3,160,640]{2,1,0:T(8,128)(2,1)}, bf16[3,160,640]{2,1,0:T(8,128)(2,1)S(1)}, u32[]{:S(2)}) copy-start(bf16[3,160,640]{2,1,0:T(8,128)(2,1)S(1)} %collective-permute-done.1.below) | copy-start | bytes 1843204
  25.7 21.1 %collective-permute-start.2 = (bf16[3,160,640]{2,1,0:T(8,128)(2,1)S(1)}, bf16[3,160,640]{2,1,0:T(8,128)(2,1)S(1)}, u32[]{:S(2)}, u32[]{:S(2)}) collective-permute-start(bf16[3,160,640]{2,1,0:T(8,128)(2,1)S(1)} %collective-permute-done.1.below), channel_id=1, source_target_pairs={{0,8},{8,0},{1,9},{9,1},{2,10},{10,2},{3,11},{11,3},{4,12},{12,4},... | collective-permute-start | bytes 1843208 | tf_op jit(solution)/shard_map/ppermute | solution.py:29
  26.0 36.6 %collective-permute-start.5 = (bf16[3,160,640]{2,1,0:T(8,128)(2,1)S(1)}, bf16[3,160,640]{2,1,0:T(8,128)(2,1)S(1)}, u32[]{:S(2)}, u32[]{:S(2)}) collective-permute-start(bf16[3,160,640]{2,1,0:T(8,128)(2,1)S(1)} %collective-permute-done.1.below), channel_id=1, source_target_pairs={{0,2},{2,4},{4,6},{6,0},{1,3},{3,5},{5,7},{7,1},{8,10},{10,12},{12... | collective-permute-start | bytes 1843208 | tf_op jit(solution)/shard_map/ppermute | solution.py:33
  26.9 20.0 %copy-start.8 = (bf16[3,160,640]{2,1,0:T(8,128)(2,1)}, bf16[3,160,640]{2,1,0:T(8,128)(2,1)S(1)}, u32[]{:S(2)}) copy-start(bf16[3,160,640]{2,1,0:T(8,128)(2,1)S(1)} %collective-permute-done.4.above2) | copy-start | bytes 1843204
  26.9 35.7 %collective-permute-start.6 = (bf16[3,160,640]{2,1,0:T(8,128)(2,1)S(1)}, bf16[3,160,640]{2,1,0:T(8,128)(2,1)S(1)}, u32[]{:S(2)}, u32[]{:S(2)}) collective-permute-start(bf16[3,160,640]{2,1,0:T(8,128)(2,1)S(1)} %collective-permute-done.4.above2), channel_id=1, source_target_pairs={{0,6},{2,0},{4,2},{6,4},{1,7},{3,1},{5,3},{7,5},{8,14},{10,8},{12,... | collective-permute-start | bytes 1843208 | tf_op jit(solution)/shard_map/ppermute | solution.py:33
  46.9 1.0 copy-start.3
  46.9 1.2 copy-start.9
  62.6 40.5 %collective-permute-start.8 = (bf16[3,3,8,40,320]{4,3,2,1,0:T(8,128)(2,1)}, bf16[3,3,8,40,320]{4,3,2,1,0:T(8,128)(2,1)}, u32[]{:S(2)}, u32[]{:S(2)}) collective-permute-start(bf16[3,3,8,40,320]{4,3,2,1,0:T(8,128)(2,1)} %get-tuple-element.84), channel_id=1, source_target_pairs={{0,8},{8,0},{1,9},{9,1},{2,10},{10,2},{3,11},{11,3},{4,12},{12,4},... | collective-permute-start | bytes 5529608 | tf_op jit(solution)/shard_map/ppermute | solution.py:29
  62.6 0.8 copy-start.4
  62.6 1.0 copy-start.5
  71.6 13.0 %collective-permute-start.7 = (bf16[352,640]{1,0:T(8,128)(2,1)}, bf16[352,640]{1,0:T(8,128)(2,1)S(1)}, u32[]{:S(2)}, u32[]{:S(2)}) collective-permute-start(bf16[352,640]{1,0:T(8,128)(2,1)} %get-tuple-element.78), channel_id=1, source_target_pairs={{0,1},{1,0},{2,3},{3,2},{4,5},{5,4},{6,7},{7,6},{8,9},{9,8},{10,11... | collective-permute-start | bytes 1351688 | tf_op jit(solution)/shard_map/ppermute | solution.py:29
  84.6 0.8 copy-start.10
  88.3 10.8 %copy-start.1 = (bf16[25,40,320]{2,1,0:T(8,128)(2,1)S(1)}, bf16[25,40,320]{2,1,0:T(8,128)(2,1)}, u32[]{:S(2)}) copy-start(bf16[25,40,320]{2,1,0:T(8,128)(2,1)} %get-tuple-element.88.mine) | copy-start | bytes 1920004
  88.4 14.7 %copy-start = (bf16[3,3,8,40,320]{4,3,2,1,0:T(8,128)(2,1)S(1)}, bf16[3,3,8,40,320]{4,3,2,1,0:T(8,128)(2,1)}, u32[]{:S(2)}) copy-start(bf16[3,3,8,40,320]{4,3,2,1,0:T(8,128)(2,1)} %get-tuple-element.83.mine) | copy-start | bytes 5529604
  88.4 58.7 %all-to-all-start.1 = ((bf16[48,32,640]{2,1,0:T(8,128)(2,1)}), bf16[48,32,640]{2,1,0:T(8,128)(2,1)}, u32[]{:S(2)}, u32[]{:S(2)}) async-start(bf16[48,32,640]{2,1,0:T(8,128)(2,1)} %get-tuple-element.79), calls=%async_computation.1 | async-start | bytes 3932160 | tf_op jit(solution)/shard_map/all_to_all | solution.py:432
  96.6 2.5 %collective-permute-start.11 = (bf16[25,40,320]{2,1,0:T(8,128)(2,1)}, bf16[25,40,320]{2,1,0:T(8,128)(2,1)S(1)}, u32[]{:S(2)}, u32[]{:S(2)}) collective-permute-start(bf16[25,40,320]{2,1,0:T(8,128)(2,1)} %get-tuple-element.89), channel_id=1, source_target_pairs={{0,8},{8,0},{1,9},{9,1},{2,10},{10,2},{3,11},{11,3},{4,12},{12,4},... | collective-permute-start | bytes 1920008 | tf_op jit(solution)/shard_map/ppermute | solution.py:29
  99.3 13.1 %collective-permute-start.12 = (bf16[3,4,40,320]{3,2,1,0:T(8,128)(2,1)S(1)}, bf16[3,4,40,320]{3,2,1,0:T(8,128)(2,1)S(1)}, u32[]{:S(2)}, u32[]{:S(2)}) collective-permute-start(bf16[3,4,40,320]{3,2,1,0:T(8,128)(2,1)S(1)} %get-tuple-element.90), channel_id=1, source_target_pairs={{0,2},{2,4},{4,6},{6,0},{1,3},{3,5},{5,7},{7,1},{8,10},{10,12},{12... | collective-permute-start | bytes 921608 | tf_op jit(solution)/shard_map/ppermute | solution.py:33
  100.4 12.1 %collective-permute-start.14 = (bf16[3,4,40,320]{3,2,1,0:T(8,128)(2,1)S(1)}, bf16[3,4,40,320]{3,2,1,0:T(8,128)(2,1)S(1)}, u32[]{:S(2)}, u32[]{:S(2)}) collective-permute-start(bf16[3,4,40,320]{3,2,1,0:T(8,128)(2,1)S(1)} %get-tuple-element.91), channel_id=1, source_target_pairs={{0,6},{2,0},{4,2},{6,4},{1,7},{3,1},{5,3},{7,5},{8,14},{10,8},{12,... | collective-permute-start | bytes 921608 | tf_op jit(solution)/shard_map/ppermute | solution.py:33
  105.3 40.5 %collective-permute-start.10 = (bf16[3,8,40,320]{3,2,1,0:T(8,128)(2,1)S(1)}, bf16[3,8,40,320]{3,2,1,0:T(8,128)(2,1)S(1)}, u32[]{:S(2)}, u32[]{:S(2)}) collective-permute-start(bf16[3,8,40,320]{3,2,1,0:T(8,128)(2,1)S(1)} %get-tuple-element.87), channel_id=1, source_target_pairs={{0,6},{2,0},{4,2},{6,4},{1,7},{3,1},{5,3},{7,5},{8,14},{10,8},{12,... | collective-permute-start | bytes 1843208 | tf_op jit(solution)/shard_map/ppermute | solution.py:33
  107.3 38.5 %collective-permute-start.9 = (bf16[3,8,40,320]{3,2,1,0:T(8,128)(2,1)S(1)}, bf16[3,8,40,320]{3,2,1,0:T(8,128)(2,1)S(1)}, u32[]{:S(2)}, u32[]{:S(2)}) collective-permute-start(bf16[3,8,40,320]{3,2,1,0:T(8,128)(2,1)S(1)} %get-tuple-element.86), channel_id=1, source_target_pairs={{0,2},{2,4},{4,6},{6,0},{1,3},{3,5},{5,7},{7,1},{8,10},{10,12},{12... | collective-permute-start | bytes 1843208 | tf_op jit(solution)/shard_map/ppermute | solution.py:33
  112.4 33.3 %collective-permute-start.13 = (bf16[3,4,40,320]{3,2,1,0:T(8,128)(2,1)S(1)}, bf16[3,4,40,320]{3,2,1,0:T(8,128)(2,1)S(1)}, u32[]{:S(2)}, u32[]{:S(2)}) collective-permute-start(bf16[3,4,40,320]{3,2,1,0:T(8,128)(2,1)S(1)} %collective-permute-done.12), channel_id=1, source_target_pairs={{0,2},{2,4},{4,6},{6,0},{1,3},{3,5},{5,7},{7,1},{8,10},{10,12},{12... | collective-permute-start | bytes 921608 | tf_op jit(solution)/shard_map/ppermute | solution.py:33
  112.4 33.3 %collective-permute-start.15 = (bf16[3,4,40,320]{3,2,1,0:T(8,128)(2,1)S(1)}, bf16[3,4,40,320]{3,2,1,0:T(8,128)(2,1)S(1)}, u32[]{:S(2)}, u32[]{:S(2)}) collective-permute-start(bf16[3,4,40,320]{3,2,1,0:T(8,128)(2,1)S(1)} %collective-permute-done.14), channel_id=1, source_target_pairs={{0,6},{2,0},{4,2},{6,4},{1,7},{3,1},{5,3},{7,5},{8,14},{10,8},{12,... | collective-permute-start | bytes 921608 | tf_op jit(solution)/shard_map/ppermute | solution.py:33
  115.7 4.3 %collective-permute-start.16 = (f32[8,320]{1,0:T(8,128)S(1)}, f32[8,320]{1,0:T(8,128)S(1)}, u32[]{:S(2)}, u32[]{:S(2)}) collective-permute-start(f32[8,320]{1,0:T(8,128)S(1)} %get-tuple-element.92), channel_id=1, source_target_pairs={{0,1},{1,0},{2,3},{3,2},{4,5},{5,4},{6,7},{7,6},{8,9},{9,8},{10,11... | collective-permute-start | bytes 30728 | tf_op jit(solution)/shard_map/ppermute | solution.py:29
  120.0 17.2 %collective-permute-start.17 = (f32[8,320]{1,0:T(8,128)S(1)}, f32[8,320]{1,0:T(8,128)S(1)}, u32[]{:S(2)}, u32[]{:S(2)}) collective-permute-start(f32[8,320]{1,0:T(8,128)S(1)} %add.72.g0), channel_id=1, source_target_pairs={{0,4},{2,6},{4,0},{6,2},{1,5},{3,7},{5,1},{7,3},{8,12},{10,14},{12... | collective-permute-start | bytes 30728 | tf_op jit(solution)/shard_map/ppermute | solution.py:33
  137.2 4.9 %collective-permute-start.18 = (f32[8,320]{1,0:T(8,128)S(1)}, f32[8,320]{1,0:T(8,128)S(1)}, u32[]{:S(2)}, u32[]{:S(2)}) collective-permute-start(f32[8,320]{1,0:T(8,128)S(1)} %add.72.g0), channel_id=1, source_target_pairs={{0,2},{2,4},{4,6},{6,0},{1,3},{3,5},{5,7},{7,1},{8,10},{10,12},{12... | collective-permute-start | bytes 30728 | tf_op jit(solution)/shard_map/ppermute | solution.py:33
  142.1 3.7 %collective-permute-start.19 = (f32[8,320]{1,0:T(8,128)S(1)}, f32[8,320]{1,0:T(8,128)S(1)}, u32[]{:S(2)}, u32[]{:S(2)}) collective-permute-start(f32[8,320]{1,0:T(8,128)S(1)} %add.72.g0), channel_id=1, source_target_pairs={{0,6},{2,0},{4,2},{6,4},{1,7},{3,1},{5,3},{7,5},{8,14},{10,8},{12,... | collective-permute-start | bytes 30728 | tf_op jit(solution)/shard_map/ppermute | solution.py:33
  147.1 17.7 %all-to-all-start.2 = ((bf16[8,16,8,320]{3,2,1,0:T(8,128)(2,1)}), bf16[8,16,8,320]{3,2,1,0:T(8,128)(2,1)S(1)}, u32[]{:S(2)}, u32[]{:S(2)}) async-start(bf16[8,16,8,320]{3,2,1,0:T(8,128)(2,1)} %shard_map.139), calls=%async_computation.2 | async-start | bytes 1572864 | tf_op jit(solution)/shard_map/all_to_all | solution.py:425
  166.8 0.8 copy-start.2
where the time goes:
time: 168 us
  waiting for transfers between devices  78.3 us (47%)
  Pallas kernels  42.8 us (25%)
  starting transfers between devices  38.9 us (23%)
  local copies, waits for them, and re-layouts  5.66 us (3%)
    ppermute x13, waiting for transfers between devices, ring(): return lax.ppermute(x, axis, [(i, (i + step) % 4) for i in range(4)])  40.5 us
    ppermute x7, waiting for transfers between devices, swap(): return lax.ppermute(x, axis, [(0, 1), (1, 0)])  28.5 us
    ppermute x13, starting transfers between devices, ring(): return lax.ppermute(x, axis, [(i, (i + step) % 4) for i in range(4)])  19.6 us
    pallas_call x1, Pallas kernels, near_block(): pl.pallas_call(near_kernel, out_shape=(jax.ShapeDtypeStruct((704, 640), F...  14.5 us
    all_to_all x1, waiting for transfers between devices, reduce_weights(): parts = lax.all_to_all(parts, ('xh', 'z'), 0, 0, tiled=True)  9.27 us
    all_to_all x1, starting transfers between devices, route(): return lax.all_to_all(packed, DP, 0, 0, tiled=True)  8.22 us
    pallas_call x1, Pallas kernels, far_block(): pl.pallas_call(far_kernel, out_shape=(jax.ShapeDtypeStruct((352, 640), F3...  8 us
    all_to_all x1, starting transfers between devices, reduce_weights(): parts = lax.all_to_all(parts, ('xh', 'z'), 0, 0, tiled=True)  6.88 us
  transfers between devices with their start and end apart: 22, of which 10 were waited for; matrix products, arithmetic and copies ran while one was open for 1% of the time, Pallas kernels for 24%

commit v1 on v0

--- a/solution.py
+++ b/solution.py
@@ -149,13 +149,6 @@
 
 def dot(a, b, dims=PLAIN):
     return lax.dot_general(a, b, dims, preferred_element_type=F32)
-
-
-def load_rows(own, other, rows, turned):
-    for j in range(2):
-        rows[j, :352] = own[j]
-        rows[j, 352:] = other[j]
-        turned[j] = rows[j].T
 
 
 def hidden_part(rows, w, acts, start, width):
@@ -171,48 +164,99 @@
     acts[2, :, span] = (value * gelu).astype(BF)
 
 
-def near_kernel(meta, own, other, wv, wg, wo, below, below2, above, above2, dn, mine, send,
-                rows, turned, w, acts, keep):
+def pallas(kernel, out_shapes, scalars, arrays, scratch):
+    return pl.pallas_call(
+        kernel,
+        out_shape=tuple(jax.ShapeDtypeStruct(s, d) for s, d in out_shapes),
+        in_specs=smem(1) + vmem(len(arrays)),
+        out_specs=tuple(vmem(len(out_shapes))),
+        scratch_shapes=[pltpu.VMEM(s, d) for s, d in scratch],
+        compiler_params=pltpu.CompilerParams(vmem_limit_bytes=56 * 2**20),
+    )(scalars, *arrays)
+
+
+def first_kernel(meta, rows, wv, wg, wo, dn, turned, grads, w, acts):
+    for j, ref in enumerate((wv, wg, wo)):
+        w[j] = ref[...]
+    for j in range(2):
+        turned[j] = rows[j].T
+    hidden_part(rows, w, acts, 0, 320)
+    dn[...] = dot(acts[0], w[0]) + dot(acts[1], w[1])
+    for j in range(3):
+        grads[j] = dot(turned[j // 2], acts[j])
+
+
+def first_block(meta, rows, wv, wg, wo):
+    return pallas(
+        first_kernel,
+        (((352, 640), F32), ((2, 640, 352), BF), ((3, 640, 320), F32)),
+        meta, (rows, wv, wg, wo),
+        [((3, 320, 640), BF), ((3, 352, 320), BF)],
+    )
+
+
+def second_kernel(meta, rows, wv, wg, wo, before, dn, turned, mine, send, w, acts, keep):
+    for j, ref in enumerate((wv, wg, wo)):
+        w[j] = ref[...]
+    for j in range(2):
+        turned[j] = rows[j].T
+    hidden_part(rows, w, acts, 0, 320)
+    dn[...] = dot(acts[0], w[0]) + dot(acts[1], w[1])
+    c = meta[1]
+    for j in range(3):
+        keep[...] = (before[j] + dot(turned[j // 2], acts[j])).reshape(8, 2, 40, 320)
+        mine[j] = keep[:, c].astype(BF)
+        send[j] = keep[:, 1 - c].astype(BF)
+
+
+def second_block(meta, rows, wv, wg, wo, before):
+    grads = ((3, 8, 40, 320), BF)
+    return pallas(
+        second_kernel,
+        (((352, 640), F32), ((2, 640, 352), BF), grads, grads),
+        meta, (rows, wv, wg, wo, before),
+        [((3, 320, 640), BF), ((3, 352, 320), BF), ((8, 2, 40, 320), F32)],
+    )
+
+
+def near_kernel(meta, own, other, below, below2, above, above2, own_dn, other_dn,
+                own_turned, other_turned, dn, mine, send, rows, w, acts, keep):
     c = meta[1]
     here = pl.multiple_of(c * 160, 16)
     there = pl.multiple_of((1 - c) * 160, 16)
-    load_rows(own, other, rows, turned)
-    for j, ref in enumerate((wv, wg, wo)):
-        w[j, :320] = ref[...]
-        w[j, pl.ds(320 + here, 160)] = above[j]
-        w[j, pl.ds(320 + there, 160)] = above2[j]
-        w[j, pl.ds(640 + here, 160)] = below[j]
-        w[j, pl.ds(640 + there, 160)] = below2[j]
-    for start, width in ((0, 256), (256, 256), (512, 256), (768, 192)):
+    for j in range(2):
+        rows[j, :352] = own[j]
+        rows[j, 352:] = other[j]
+    for j in range(3):
+        w[j, pl.ds(here, 160)] = above[j]
+        w[j, pl.ds(there, 160)] = above2[j]
+        w[j, pl.ds(320 + here, 160)] = below[j]
+        w[j, pl.ds(320 + there, 160)] = below2[j]
+    for start, width in ((0, 256), (256, 256), (512, 128)):
         hidden_part(rows, w, acts, start, width)
-    dn[...] = dot(acts[0], w[0]) + dot(acts[1], w[1])
-    for j in range(3):
-        keep[...] = dot(turned[j // 2], acts[j]).reshape(8, 2, 40, 960)
+    for before, at in ((own_dn, slice(0, 352)), (other_dn, slice(352, 704))):
+        dn[at] = before[...] + dot(acts[0, at], w[0]) + dot(acts[1, at], w[1])
+    for j in range(3):
+        grad = dot(own_turned[j // 2], acts[j, :352]) + dot(other_turned[j // 2], acts[j, 352:])
+        keep[...] = grad.reshape(8, 2, 40, 640)
         for out, side in ((mine, c), (send, 1 - c)):
-            both = keep[:, side].reshape(320, 960)
+            both = keep[:, side].reshape(320, 640)
             out[0, j] = both[:, :320].reshape(8, 40, 320).astype(BF)
-            mid = pltpu.roll(both[:, 256:640], 320, 1)[:, :320]
-            out[1, j] = mid.reshape(8, 40, 320).astype(BF)
-            out[2, j] = both[:, 640:].reshape(8, 40, 320).astype(BF)
-
-
-def near_block(meta, own, other, wv, wg, wo, below, below2, above, above2):
-    grads = jax.ShapeDtypeStruct((3, 3, 8, 40, 320), BF)
-    return pl.pallas_call(
+            high = pltpu.roll(both[:, 256:640], 320, 1)[:, :320]
+            out[1, j] = high.reshape(8, 40, 320).astype(BF)
+
+
+def near_block(meta, *arrays):
+    grads = ((2, 3, 8, 40, 320), BF)
+    return pallas(
         near_kernel,
-        out_shape=(jax.ShapeDtypeStruct((704, 640), F32), grads, grads),
-        in_specs=smem(1) + vmem(9),
-        out_specs=tuple(vmem(3)),
-        scratch_shapes=[
-            pltpu.VMEM((2, 704, 640), BF),
-            pltpu.VMEM((2, 640, 704), BF),
-            pltpu.VMEM((3, 960, 640), BF),
-            pltpu.VMEM((3, 704, 960), BF),
-            pltpu.VMEM((8, 2, 40, 960), F32),
+        (((704, 640), F32), grads, grads),
+        meta, arrays,
+        [
+            ((2, 704, 640), BF), ((3, 640, 640), BF), ((3, 704, 640), BF),
+            ((8, 2, 40, 640), F32),
         ],
-        compiler_params=pltpu.CompilerParams(vmem_limit_bytes=56 * 2**20),
-        name="near_block",
-    )(meta, own, other, wv, wg, wo, below, below2, above, above2)
+    )
 
 
 def split_gain(g):
@@ -237,12 +281,14 @@
     return rows + pltpu.roll(rows, 6, 0)
 
 
-def far_kernel(meta, own, other, gain, near_dn, first, second, dn, dn_send, mine, send,
-               rows, turned, w, acts, keep):
+def far_kernel(meta, own, other, gain, near_dn, first, second, own_turned, other_turned,
+               dn, dn_send, mine, send, rows, w, acts, keep):
     c = meta[1]
     here = pl.multiple_of(c * 160, 16)
     there = pl.multiple_of((1 - c) * 160, 16)
-    load_rows(own, other, rows, turned)
+    for j in range(2):
+        rows[j, :352] = own[j]
+        rows[j, 352:] = other[j]
     for j in range(3):
         w[j, pl.ds(here, 160)] = first[j]
         w[j, pl.ds(there, 160)] = second[j]
@@ -253,7 +299,8 @@
     gsum = jnp.sum(total * rows[0].astype(F32), axis=0, keepdims=True) / gain[...]
     tail = split_gain(gsum).astype(BF)
     for j in range(3):
-        keep[...] = dot(turned[j // 2], acts[j]).reshape(8, 2, 40, 320)
+        grad = dot(own_turned[j // 2], acts[j, :352]) + dot(other_turned[j // 2], acts[j, 352:])
+        keep[...] = grad.reshape(8, 2, 40, 320)
         for out, side in ((mine, c), (send, 1 - c)):
             out[8 * j : 8 * j + 8] = keep[:, side].astype(BF)
     for out in (mine, send):
@@ -261,28 +308,17 @@
         out[24, :8] = tail
 
 
-def far_block(meta, own, other, gain, near_dn, first, second):
-    grads = jax.ShapeDtypeStruct((25, 40, 320), BF)
-    return pl.pallas_call(
+def far_block(meta, *arrays):
+    grads = ((25, 40, 320), BF)
+    return pallas(
         far_kernel,
-        out_shape=(
-            jax.ShapeDtypeStruct((352, 640), F32),
-            jax.ShapeDtypeStruct((352, 640), BF),
-            grads,
-            grads,
-        ),
-        in_specs=smem(1) + vmem(6),
-        out_specs=tuple(vmem(4)),
-        scratch_shapes=[
-            pltpu.VMEM((2, 704, 640), BF),
-            pltpu.VMEM((2, 640, 704), BF),
-            pltpu.VMEM((3, 320, 640), BF),
-            pltpu.VMEM((3, 704, 320), BF),
-            pltpu.VMEM((8, 2, 40, 320), F32),
+        (((352, 640), F32), ((352, 640), BF), grads, grads),
+        meta, arrays,
+        [
+            ((2, 704, 640), BF), ((3, 320, 640), BF), ((3, 704, 320), BF),
+            ((8, 2, 40, 320), F32),
         ],
-        compiler_params=pltpu.CompilerParams(vmem_limit_bytes=56 * 2**20),
-        name="far_block",
-    )(meta, own, other, gain, near_dn, first, second)
+    )
 
 
 def finish_kernel(dest_g, dest_r, dn, got, lat, grad, gain, own, packed, sems):
@@ -366,10 +402,9 @@
     )(*arrays)
 
 
-def near_sums_kernel(mine, got, own, up, down):
-    own[...] = mine[0].astype(F32) + got[0].astype(F32)
-    up[...] = (mine[1].astype(F32) + got[1].astype(F32)).astype(BF)
-    down[...] = (mine[2].astype(F32) + got[2].astype(F32)).astype(BF)
+def near_sums_kernel(mine, got, up, down):
+    up[...] = (mine[0].astype(F32) + got[0].astype(F32)).astype(BF)
+    down[...] = (mine[1].astype(F32) + got[1].astype(F32)).astype(BF)
 
 
 def far_sums_kernel(mine, got, lower, upper, tail):
@@ -379,11 +414,12 @@
     tail[...] = joined(mine[24, :8]) + joined(got[24, :8])
 
 
-def over_y_kernel(own, from_down, from_up, far_lower, far_upper, g0, g1, g2, g3, out):
+def over_y_kernel(mine, got, from_down, from_up, far_lower, far_upper, g0, g1, g2, g3, out):
     for j in range(3):
         for half, far in ((0, far_lower), (4, far_upper)):
             at = slice(half, half + 4)
-            x = own[j, at] + from_down[j, at].astype(F32)
+            x = mine[j, at].astype(F32) + got[j, at].astype(F32)
+            x = x + from_down[j, at].astype(F32)
             x = x + (from_up[j, at].astype(F32) + far[j].astype(F32))
             out[at, 5 * j : 5 * j + 5] = x.astype(BF).reshape(4, 5, 8, 320)
     tail = resplit((g0[...] + g1[...]) + (g2[...] + g3[...])).astype(BF)
@@ -400,13 +436,11 @@
     tail[...] = joined(total[15])
 
 
-def reduce_weights(near_mine, near_got, far_mine, far_got):
+def reduce_weights(own_mine, own_got, near_mine, near_got, far_mine, far_got):
     grads = (3, 8, 40, 320)
     half = (3, 4, 40, 320)
     row = ((8, 320), F32)
-    own, up, down = local(
-        near_sums_kernel, ((grads, F32), (grads, BF), (grads, BF)), near_mine, near_got
-    )
+    up, down = local(near_sums_kernel, ((grads, BF), (grads, BF)), near_mine, near_got)
     from_down = ring(up, "y", 1)
     from_up = ring(down, "y", -1)
     lower, upper, tail = local(
@@ -420,7 +454,7 @@
     tails = [tail] + [ring(tail, "y", d) for d in (2, 1, -1)]
     (parts,) = local(
         over_y_kernel, (((8, 16, 8, 320), BF),),
-        own, from_down, from_up, lower, upper, *tails,
+        own_mine, own_got, from_down, from_up, lower, upper, *tails,
     )
     parts = lax.all_to_all(parts, ("xh", "z"), 0, 0, tiled=True)
     out = ((40, 320), F32)
@@ -468,11 +502,16 @@
     second = ring(above2, "y", -1)
     rows2 = rows.reshape(2, 352, 640)
     other = other.reshape(2, 352, 640)
+    own_dn, own_turned, partial = first_block(meta, rows2, wv, wg, wo)
+    other_dn, other_turned, own_mine, own_send = second_block(meta, other, wv, wg, wo, partial)
+    own_got = swap(own_send, "c")
     near_dn, near_mine, near_send = near_block(
-        meta, rows2, other, wv, wg, wo, below, below2, above, above2
+        meta, rows2, other, below, below2, above, above2, own_dn, other_dn, own_turned, other_turned
     )
     near_got = swap(near_send, "c")
-    dn, dn_send, far_mine, far_send = far_block(meta, rows2, other, gain, near_dn, first, second)
+    dn, dn_send, far_mine, far_send = far_block(
+        meta, rows2, other, gain, near_dn, first, second, own_turned, other_turned
+    )
     got = swap(dn_send, "xl")
     far_got = swap(far_send, "c")
     tiles = (11, 32, 640)
@@ -482,7 +521,7 @@
     came = route(packed)
     placed = unpack(src_p, src_r, came)
     placed = more_rounds(placed, own, most, dest_g, dest_r, src_p, src_r)
-    grads = reduce_weights(near_mine, near_got, far_mine, far_got)
+    grads = reduce_weights(own_mine, own_got, near_mine, near_got, far_mine, far_got)
     return placed, *grads
 
 

time: 168 us -> 185 us (1.10)
  the two profiles are of different devices: /device:TPU:0 before, /device:TPU:1 now
where the time goes in v1:
time: 185 us
  waiting for transfers between devices  79.1 us (43%)
  Pallas kernels  52.3 us (28%)
  starting transfers between devices  42.6 us (23%)
  local copies, waits for them, and re-layouts  8.67 us (5%)
    ppermute x13, waiting for transfers between devices, ring(): return lax.ppermute(x, axis, [(i, (i + step) % 4) for i in range(4)])  43.3 us
    pallas_call x4, Pallas kernels, pallas(): pl.pallas_call(kernel, out_shape=tuple((jax.ShapeDtypeStruct(s, d) for s,...  33.8 us
    all_to_all x1, waiting for transfers between devices, route(): return lax.all_to_all(packed, DP, 0, 0, tiled=True)  25.5 us
    ppermute x13, starting transfers between devices, ring(): return lax.ppermute(x, axis, [(i, (i + step) % 4) for i in range(4)])  15.5 us
    all_to_all x1, starting transfers between devices, route(): return lax.all_to_all(packed, DP, 0, 0, tiled=True)  13 us
    ppermute x8, waiting for transfers between devices, swap(): return lax.ppermute(x, axis, [(0, 1), (1, 0)])  10.2 us
    all_to_all x1, starting transfers between devices, reduce_weights(): parts = lax.all_to_all(parts, ('xh', 'z'), 0, 0, tiled=True)  7.22 us
    ppermute x8, starting transfers between devices, swap(): return lax.ppermute(x, axis, [(0, 1), (1, 0)])  6.97 us
  transfers between devices with their start and end apart: 23, of which 9 were waited for; matrix products, arithmetic and copies ran while one was open for 1% of the time, Pallas kernels for 25%

profile of v1, /device:TPU:1, one launch (start us, length us, event | category | flops | bytes accessed | tf_op | source)
XLA Modules:
  0.0 184.8 jit_solution(1923391181676942495)
XLA Ops:
  0.6 0.6 pad_add_fusion.meta
  1.2 2.7 %halves.1 = bf16[3,160,640]{2,1,0:T(8,128)(2,1)} custom-call(s32[2]{0:T(128)} %pad_add_fusion.meta, bf16[320,640]{1,0:T(8,128)(2,1)} %bitcast.33, bf16[320,640]{1,0:T(8,128)(2,1)} %bitcast.36, bf16[320,640]{1,0:T(8,128)(2,1)} %bitcast.39), custom_call_target="tpu_custom_call" | custom-call | tf_op jit(solution)/shard_map/halves/pallas_call | solution.py:106
  3.9 3.6 %collective-permute-start.3 = (bf16[3,160,640]{2,1,0:T(8,128)(2,1)}, bf16[3,160,640]{2,1,0:T(8,128)(2,1)S(1)}, u32[]{:S(2)}, u32[]{:S(2)}) collective-permute-start(bf16[3,160,640]{2,1,0:T(8,128)(2,1)} %halves.1), channel_id=1, source_target_pairs={{0,6},{2,0},{4,2},{6,4},{1,7},{3,1},{5,3},{7,5},{8,14},{10,8},{12,... | collective-permute-start | bytes 1843208 | tf_op jit(solution)/shard_map/ppermute | solution.py:33
  7.4 1.3 broadcast_in_dim.52.gain
  8.7 2.5 %prologue.1.grad = bf16[2,11,32,640]{3,2,1,0:T(8,128)(2,1)} custom-call(s32[2]{0:T(128)} %pad_add_fusion.meta, s32[16]{0:T(128)} %trunc.3, s32[176]{0:T(256)} %times.1, f32[1000]{0:T(1024)} %constant.64.clone.table, bf16[11,32,640]{2,1,0:T(8,128)(2,1)} %lat.3, bf16[11,32,640]{2,1,0:T(8,128)(2,1)} %cot.1, f32[1,640]{1,0:T(1,128)} %broadcast_in_dim.52.gain), custom_call_target="tpu_custom_call" | custom-call | tf_op jit(solution)/shard_map/prologue/pallas_call | solution.py:137
  11.2 1.2 collective-permute-start
  12.4 7.9 %collective-permute-done.3.above = bf16[3,160,640]{2,1,0:T(8,128)(2,1)S(1)} collective-permute-done((bf16[3,160,640]{2,1,0:T(8,128)(2,1)}, bf16[3,160,640]{2,1,0:T(8,128)(2,1)S(1)}, u32[]{:S(2)}, u32[]{:S(2)}) %collective-permute-start.3) | collective-permute-done | bytes 614432 | tf_op jit(solution)/shard_map/ppermute | solution.py:33
  20.3 1.5 collective-permute-start.4
  21.8 1.5 collective-permute-done.1.below
  23.3 1.8 collective-permute-start.2
  25.1 2.7 %collective-permute-start.6 = (bf16[3,160,640]{2,1,0:T(8,128)(2,1)S(1)}, bf16[3,160,640]{2,1,0:T(8,128)(2,1)S(1)}, u32[]{:S(2)}, u32[]{:S(2)}) collective-permute-start(bf16[3,160,640]{2,1,0:T(8,128)(2,1)S(1)} %collective-permute-done.4.above2), channel_id=1, source_target_pairs={{0,6},{2,0},{4,2},{6,4},{1,7},{3,1},{5,3},{7,5},{8,14},{10,8},{12,... | collective-permute-start | bytes 1843208 | tf_op jit(solution)/shard_map/ppermute | solution.py:33
  27.8 5.7 %shard_map.137 = (f32[352,640]{1,0:T(8,128)}, bf16[2,640,352]{2,1,0:T(8,128)(2,1)}, f32[3,640,320]{2,1,0:T(8,128)}) custom-call(s32[2]{0:T(128)} %pad_add_fusion.meta, bf16[2,352,640]{2,1,0:T(8,128)(2,1)} %bitcast.27, bf16[320,640]{1,0:T(8,128)(2,1)} %bitcast.34, bf16[320,640]{1,0:T(8,128)(2,1)} %bitcast.37, bf16[320,640]{1,0:T(8,128)(2,1)} %bitcast.40), custom_call_target="tpu_custom_call" | custom-call | tf_op jit(solution)/shard_map/pallas_call | solution.py:168
  33.5 0.9 copy-done.4
  34.5 6.3 %shard_map.138 = (f32[352,640]{1,0:T(8,128)}, bf16[2,640,352]{2,1,0:T(8,128)(2,1)}, bf16[3,8,40,320]{3,2,1,0:T(8,128)(2,1)}, bf16[3,8,40,320]{3,2,1,0:T(8,128)(2,1)}) custom-call(s32[2]{0:T(128)} %pad_add_fusion.meta, bf16[2,352,640]{2,1,0:T(8,128)(2,1)} %bitcast.30, bf16[320,640]{1,0:T(8,128)(2,1)} %bitcast.35, bf16[320,640]{1,0:T(8,128)(2,1)} %bitcast.38, ...), custom_call_target="tpu_custom_call" | custom-call | tf_op jit(solution)/shard_map/pallas_call | solution.py:168
  40.8 0.8 copy-done.11
  41.6 12.6 %shard_map.139 = (f32[704,640]{1,0:T(8,128)}, bf16[2,3,8,40,320]{4,3,2,1,0:T(8,128)(2,1)}, bf16[2,3,8,40,320]{4,3,2,1,0:T(8,128)(2,1)}) custom-call(s32[2]{0:T(128)} %pad_add_fusion.meta, bf16[2,352,640]{2,1,0:T(8,128)(2,1)} %bitcast.28, bf16[2,352,640]{2,1,0:T(8,128)(2,1)} %bitcast.31, bf16[3,160,640]{2,1,0:T(8,128)(2,1)} %copy-done.6, ...), custom_call_target="tpu_custom_call" | custom-call | tf_op jit(solution)/shard_map/pallas_call | solution.py:168
  54.3 0.5 collective-permute-start.9
  54.8 0.8 copy-done.9
  55.8 9.1 %shard_map.140 = (f32[352,640]{1,0:T(8,128)}, bf16[352,640]{1,0:T(8,128)(2,1)}, bf16[25,40,320]{2,1,0:T(8,128)(2,1)}, bf16[25,40,320]{2,1,0:T(8,128)(2,1)}) custom-call(s32[2]{0:T(128)} %pad_add_fusion.meta, bf16[2,352,640]{2,1,0:T(8,128)(2,1)} %bitcast.29, bf16[2,352,640]{2,1,0:T(8,128)(2,1)} %bitcast.32, f32[1,640]{1,0:T(1,128)} %broadcast_in_dim.52.gain, ...), custom_call_target="tpu_custom_call" | custom-call | tf_op jit(solution)/shard_map/pallas_call | solution.py:168
  65.0 0.5 collective-permute-start.8
  65.5 2.0 %collective-permute-done.12.got = bf16[25,40,320]{2,1,0:T(8,128)(2,1)S(1)} collective-permute-done((bf16[25,40,320]{2,1,0:T(8,128)(2,1)}, bf16[25,40,320]{2,1,0:T(8,128)(2,1)S(1)}, u32[]{:S(2)}, u32[]{:S(2)}) %collective-permute-start.12) | collective-permute-done | bytes 640032 | tf_op jit(solution)/shard_map/ppermute | solution.py:29
  67.5 1.1 copy-done.1
  68.6 0.2 shard_map.142
  68.8 1.3 collective-permute-start.17
  70.1 0.4 shard_map.141
  70.5 2.7 %collective-permute-start.11 = (bf16[3,8,40,320]{3,2,1,0:T(8,128)(2,1)S(1)}, bf16[3,8,40,320]{3,2,1,0:T(8,128)(2,1)S(1)}, u32[]{:S(2)}, u32[]{:S(2)}) collective-permute-start(bf16[3,8,40,320]{3,2,1,0:T(8,128)(2,1)S(1)} %get-tuple-element.99), channel_id=1, source_target_pairs={{0,6},{2,0},{4,2},{6,4},{1,7},{3,1},{5,3},{7,5},{8,14},{10,8},{12,... | collective-permute-start | bytes 1843208 | tf_op jit(solution)/shard_map/ppermute | solution.py:33
  73.2 2.7 %collective-permute-start.15 = (bf16[3,4,40,320]{3,2,1,0:T(8,128)(2,1)S(1)}, bf16[3,4,40,320]{3,2,1,0:T(8,128)(2,1)S(1)}, u32[]{:S(2)}, u32[]{:S(2)}) collective-permute-start(bf16[3,4,40,320]{3,2,1,0:T(8,128)(2,1)S(1)} %get-tuple-element.103), channel_id=1, source_target_pairs={{0,6},{2,0},{4,2},{6,4},{1,7},{3,1},{5,3},{7,5},{8,14},{10,8},{12,... | collective-permute-start | bytes 921608 | tf_op jit(solution)/shard_map/ppermute | solution.py:33
  75.9 21.4 %collective-permute-done.13 = bf16[3,4,40,320]{3,2,1,0:T(8,128)(2,1)S(1)} collective-permute-done((bf16[3,4,40,320]{3,2,1,0:T(8,128)(2,1)S(1)}, bf16[3,4,40,320]{3,2,1,0:T(8,128)(2,1)S(1)}, u32[]{:S(2)}, u32[]{:S(2)}) %collective-permute-start.13) | collective-permute-done | bytes 307232 | tf_op jit(solution)/shard_map/ppermute | solution.py:33
  97.2 2.7 %collective-permute-start.16 = (bf16[3,4,40,320]{3,2,1,0:T(8,128)(2,1)S(1)}, bf16[3,4,40,320]{3,2,1,0:T(8,128)(2,1)S(1)}, u32[]{:S(2)}, u32[]{:S(2)}) collective-permute-start(bf16[3,4,40,320]{3,2,1,0:T(8,128)(2,1)S(1)} %collective-permute-done.15), channel_id=1, source_target_pairs={{0,6},{2,0},{4,2},{6,4},{1,7},{3,1},{5,3},{7,5},{8,14},{10,8},{12,... | collective-permute-start | bytes 921608 | tf_op jit(solution)/shard_map/ppermute | solution.py:33
  99.9 7.1 %collective-permute-done.18.g1 = f32[8,320]{1,0:T(8,128)S(1)} collective-permute-done((f32[8,320]{1,0:T(8,128)S(1)}, f32[8,320]{1,0:T(8,128)S(1)}, u32[]{:S(2)}, u32[]{:S(2)}) %collective-permute-start.18) | collective-permute-done | bytes 10272 | tf_op jit(solution)/shard_map/ppermute | solution.py:33
  107.0 0.6 collective-permute-start.19
  107.6 3.2 %collective-permute-done.19.g2 = f32[8,320]{1,0:T(8,128)S(1)} collective-permute-done((f32[8,320]{1,0:T(8,128)S(1)}, f32[8,320]{1,0:T(8,128)S(1)}, u32[]{:S(2)}, u32[]{:S(2)}) %collective-permute-start.19) | collective-permute-done | bytes 10272 | tf_op jit(solution)/shard_map/ppermute | solution.py:33
  110.8 0.5 collective-permute-start.20
  111.3 2.3 %collective-permute-done.20.g3 = f32[8,320]{1,0:T(8,128)S(1)} collective-permute-done((f32[8,320]{1,0:T(8,128)S(1)}, f32[8,320]{1,0:T(8,128)S(1)}, u32[]{:S(2)}, u32[]{:S(2)}) %collective-permute-start.20) | collective-permute-done | bytes 10272 | tf_op jit(solution)/shard_map/ppermute | solution.py:33
  113.7 1.4 shard_map.143
  115.0 7.2 %all-to-all-start.2 = ((bf16[8,16,8,320]{3,2,1,0:T(8,128)(2,1)}), bf16[8,16,8,320]{3,2,1,0:T(8,128)(2,1)S(1)}, u32[]{:S(2)}, u32[]{:S(2)}) async-start(bf16[8,16,8,320]{3,2,1,0:T(8,128)(2,1)} %shard_map.143), calls=%async_computation.2 | async-start | bytes 1572864 | tf_op jit(solution)/shard_map/all_to_all | solution.py:459
  122.4 6.1 %routes.1 = (s32[11]{0:T(128)S(1)}, s32[11]{0:T(128)S(1)}, s32[11]{0:T(128)S(1)}, s32[11]{0:T(128)S(1)}, s32[1]{0:T(128)}) custom-call(s32[2]{0:T(128)} %pad_add_fusion.meta, s32[16]{0:T(128)} %trunc.3, s32[176]{0:T(256)} %tmap.1), custom_call_target="tpu_custom_call" | custom-call | tf_op jit(solution)/shard_map/routes/pallas_call | solution.py:89
  128.5 8.3 %collective-permute-done.7 = bf16[352,640]{1,0:T(8,128)(2,1)S(1)} collective-permute-done((bf16[352,640]{1,0:T(8,128)(2,1)S(1)}, bf16[352,640]{1,0:T(8,128)(2,1)S(1)}, u32[]{:S(2)}, u32[]{:S(2)}) %collective-permute-start.7) | collective-permute-done | bytes 450592 | tf_op jit(solution)/shard_map/ppermute | solution.py:29
  136.7 0.8 copy-done.12
  137.5 3.0 %finish.1 = (bf16[11,32,640]{2,1,0:T(8,128)(2,1)S(1)}, bf16[48,32,640]{2,1,0:T(8,128)(2,1)}) custom-call(s32[11]{0:T(128)S(1)} %get-tuple-element.190.dest_g, s32[11]{0:T(128)S(1)} %get-tuple-element.189.dest_r, f32[11,32,640]{2,1,0:T(8,128)} %bitcast.42, bf16[11,32,640]{2,1,0:T(8,128)(2,1)} %bitcast.43, bf16[11,32,640]{2,1,0:T(8,128)(2,1)} %lat.3, ...), custom_call_target="tpu_custom_call" | custom-call | tf_op jit(solution)/shard_map/finish/pallas_call | solution.py:352
  140.6 13.0 %all-to-all-start.1 = ((bf16[48,32,640]{2,1,0:T(8,128)(2,1)}), bf16[48,32,640]{2,1,0:T(8,128)(2,1)S(1)}, u32[]{:S(2)}, u32[]{:S(2)}) async-start(bf16[48,32,640]{2,1,0:T(8,128)(2,1)} %get-tuple-element.90), calls=%async_computation.1 | async-start | bytes 3932160 | tf_op jit(solution)/shard_map/all_to_all | solution.py:466
  153.5 0.7 shard_map.144
  154.3 0.7 reshape.131
  154.9 25.5 %all-to-all-done.1.came = bf16[48,32,640]{2,1,0:T(8,128)(2,1)S(1)} async-done(((bf16[48,32,640]{2,1,0:T(8,128)(2,1)}), bf16[48,32,640]{2,1,0:T(8,128)(2,1)S(1)}, u32[]{:S(2)}, u32[]{:S(2)}) %all-to-all-start.1) | async-done | bytes 1966112 | tf_op jit(solution)/shard_map/all_to_all | solution.py:466
  180.5 1.3 copy-done.5
  181.7 1.6 unpack.1
  183.3 0.7 while.10
  184.0 0.8 copy-done.3
  (47 shorter events, 0.5 us)
Async XLA Ops:
  3.9 16.4 %collective-permute-start.3 = (bf16[3,160,640]{2,1,0:T(8,128)(2,1)}, bf16[3,160,640]{2,1,0:T(8,128)(2,1)S(1)}, u32[]{:S(2)}, u32[]{:S(2)}) collective-permute-start(bf16[3,160,640]{2,1,0:T(8,128)(2,1)} %halves.1), channel_id=1, source_target_pairs={{0,6},{2,0},{4,2},{6,4},{1,7},{3,1},{5,3},{7,5},{8,14},{10,8},{12,... | collective-permute-start | bytes 1843208 | tf_op jit(solution)/shard_map/ppermute | solution.py:33
  7.4 15.9 %collective-permute-start.1 = (bf16[3,160,640]{2,1,0:T(8,128)(2,1)}, bf16[3,160,640]{2,1,0:T(8,128)(2,1)S(1)}, u32[]{:S(2)}, u32[]{:S(2)}) collective-permute-start(bf16[3,160,640]{2,1,0:T(8,128)(2,1)} %halves.1), channel_id=1, source_target_pairs={{0,2},{2,4},{4,6},{6,0},{1,3},{3,5},{5,7},{7,1},{8,10},{10,12},{12... | collective-permute-start | bytes 1843208 | tf_op jit(solution)/shard_map/ppermute | solution.py:33
  11.2 22.3 %collective-permute-start = (bf16[2,11,32,640]{3,2,1,0:T(8,128)(2,1)}, bf16[2,11,32,640]{3,2,1,0:T(8,128)(2,1)S(1)}, u32[]{:S(2)}, u32[]{:S(2)}) collective-permute-start(bf16[2,11,32,640]{3,2,1,0:T(8,128)(2,1)} %prologue.1.grad), channel_id=1, source_target_pairs={{0,1},{1,0},{2,3},{3,2},{4,5},{5,4},{6,7},{7,6},{8,9},{9,8},{10,11... | collective-permute-start | bytes 2703368 | tf_op jit(solution)/shard_map/ppermute | solution.py:29
  20.3 20.5 %copy-start.7 = (bf16[3,160,640]{2,1,0:T(8,128)(2,1)}, bf16[3,160,640]{2,1,0:T(8,128)(2,1)S(1)}, u32[]{:S(2)}) copy-start(bf16[3,160,640]{2,1,0:T(8,128)(2,1)S(1)} %collective-permute-done.3.above) | copy-start | bytes 1843204
  20.3 4.8 %collective-permute-start.4 = (bf16[3,160,640]{2,1,0:T(8,128)(2,1)S(1)}, bf16[3,160,640]{2,1,0:T(8,128)(2,1)S(1)}, u32[]{:S(2)}, u32[]{:S(2)}) collective-permute-start(bf16[3,160,640]{2,1,0:T(8,128)(2,1)S(1)} %collective-permute-done.3.above), channel_id=1, source_target_pairs={{0,8},{8,0},{1,9},{9,1},{2,10},{10,2},{3,11},{11,3},{4,12},{12,4},... | collective-permute-start | bytes 1843208 | tf_op jit(solution)/shard_map/ppermute | solution.py:29
  23.3 17.5 %copy-start.6 = (bf16[3,160,640]{2,1,0:T(8,128)(2,1)}, bf16[3,160,640]{2,1,0:T(8,128)(2,1)S(1)}, u32[]{:S(2)}) copy-start(bf16[3,160,640]{2,1,0:T(8,128)(2,1)S(1)} %collective-permute-done.1.below) | copy-start | bytes 1843204
  23.3 17.5 %collective-permute-start.2 = (bf16[3,160,640]{2,1,0:T(8,128)(2,1)S(1)}, bf16[3,160,640]{2,1,0:T(8,128)(2,1)S(1)}, u32[]{:S(2)}, u32[]{:S(2)}) collective-permute-start(bf16[3,160,640]{2,1,0:T(8,128)(2,1)S(1)} %collective-permute-done.1.below), channel_id=1, source_target_pairs={{0,8},{8,0},{1,9},{9,1},{2,10},{10,2},{3,11},{11,3},{4,12},{12,4},... | collective-permute-start | bytes 1843208 | tf_op jit(solution)/shard_map/ppermute | solution.py:29
  25.1 29.7 %collective-permute-start.5 = (bf16[3,160,640]{2,1,0:T(8,128)(2,1)S(1)}, bf16[3,160,640]{2,1,0:T(8,128)(2,1)S(1)}, u32[]{:S(2)}, u32[]{:S(2)}) collective-permute-start(bf16[3,160,640]{2,1,0:T(8,128)(2,1)S(1)} %collective-permute-done.1.below), channel_id=1, source_target_pairs={{0,2},{2,4},{4,6},{6,0},{1,3},{3,5},{5,7},{7,1},{8,10},{10,12},{12... | collective-permute-start | bytes 1843208 | tf_op jit(solution)/shard_map/ppermute | solution.py:33
  25.1 15.7 %copy-start.8 = (bf16[3,160,640]{2,1,0:T(8,128)(2,1)}, bf16[3,160,640]{2,1,0:T(8,128)(2,1)S(1)}, u32[]{:S(2)}) copy-start(bf16[3,160,640]{2,1,0:T(8,128)(2,1)S(1)} %collective-permute-done.4.above2) | copy-start | bytes 1843204
  25.1 29.7 %collective-permute-start.6 = (bf16[3,160,640]{2,1,0:T(8,128)(2,1)S(1)}, bf16[3,160,640]{2,1,0:T(8,128)(2,1)S(1)}, u32[]{:S(2)}, u32[]{:S(2)}) collective-permute-start(bf16[3,160,640]{2,1,0:T(8,128)(2,1)S(1)} %collective-permute-done.4.above2), channel_id=1, source_target_pairs={{0,6},{2,0},{4,2},{6,4},{1,7},{3,1},{5,3},{7,5},{8,14},{10,8},{12,... | collective-permute-start | bytes 1843208 | tf_op jit(solution)/shard_map/ppermute | solution.py:33
  33.5 0.9 copy-start.4
  40.8 0.8 copy-start.11
  54.3 15.8 %collective-permute-start.9 = (bf16[2,3,8,40,320]{4,3,2,1,0:T(8,128)(2,1)}, bf16[2,3,8,40,320]{4,3,2,1,0:T(8,128)(2,1)S(1)}, u32[]{:S(2)}, u32[]{:S(2)}) collective-permute-start(bf16[2,3,8,40,320]{4,3,2,1,0:T(8,128)(2,1)} %get-tuple-element.97), channel_id=1, source_target_pairs={{0,8},{8,0},{1,9},{9,1},{2,10},{10,2},{3,11},{11,3},{4,12},{12,4},... | collective-permute-start | bytes 3686408 | tf_op jit(solution)/shard_map/ppermute | solution.py:29
  54.8 0.9 copy-start.9
  54.8 1.0 copy-start.10
  55.8 9.2 %copy-start.13 = (bf16[3,8,40,320]{3,2,1,0:T(8,128)(2,1)S(1)}, bf16[3,8,40,320]{3,2,1,0:T(8,128)(2,1)}, u32[]{:S(2)}) copy-start(bf16[3,8,40,320]{3,2,1,0:T(8,128)(2,1)} %get-tuple-element.95) | copy-start | bytes 1843204
  65.0 5.1 %copy-start = (bf16[2,3,8,40,320]{4,3,2,1,0:T(8,128)(2,1)S(1)}, bf16[2,3,8,40,320]{4,3,2,1,0:T(8,128)(2,1)}, u32[]{:S(2)}) copy-start(bf16[2,3,8,40,320]{4,3,2,1,0:T(8,128)(2,1)} %get-tuple-element.96.mine) | copy-start | bytes 3686404
  65.0 2.5 %collective-permute-start.12 = (bf16[25,40,320]{2,1,0:T(8,128)(2,1)}, bf16[25,40,320]{2,1,0:T(8,128)(2,1)S(1)}, u32[]{:S(2)}, u32[]{:S(2)}) collective-permute-start(bf16[25,40,320]{2,1,0:T(8,128)(2,1)} %get-tuple-element.101), channel_id=1, source_target_pairs={{0,8},{8,0},{1,9},{9,1},{2,10},{10,2},{3,11},{11,3},{4,12},{12,4},... | collective-permute-start | bytes 1920008 | tf_op jit(solution)/shard_map/ppermute | solution.py:29
  65.0 34.9 %collective-permute-start.8 = (bf16[3,8,40,320]{3,2,1,0:T(8,128)(2,1)S(1)}, bf16[3,8,40,320]{3,2,1,0:T(8,128)(2,1)S(1)}, u32[]{:S(2)}, u32[]{:S(2)}) collective-permute-start(bf16[3,8,40,320]{3,2,1,0:T(8,128)(2,1)S(1)} %copy-done.13), channel_id=1, source_target_pairs={{0,8},{8,0},{1,9},{9,1},{2,10},{10,2},{3,11},{11,3},{4,12},{12,4},... | collective-permute-start | bytes 1843208 | tf_op jit(solution)/shard_map/ppermute | solution.py:29
  67.5 1.1 copy-start.1
  68.6 45.1 %copy-start.2 = (bf16[3,8,40,320]{3,2,1,0:T(8,128)(2,1)S(1)}, bf16[3,8,40,320]{3,2,1,0:T(8,128)(2,1)}, u32[]{:S(2)}) copy-start(bf16[3,8,40,320]{3,2,1,0:T(8,128)(2,1)} %get-tuple-element.94.mine) | copy-start | bytes 1843204
  68.8 4.4 %collective-permute-start.17 = (f32[8,320]{1,0:T(8,128)S(1)}, f32[8,320]{1,0:T(8,128)S(1)}, u32[]{:S(2)}, u32[]{:S(2)}) collective-permute-start(f32[8,320]{1,0:T(8,128)S(1)} %get-tuple-element.104), channel_id=1, source_target_pairs={{0,1},{1,0},{2,3},{3,2},{4,5},{5,4},{6,7},{7,6},{8,9},{9,8},{10,11... | collective-permute-start | bytes 30728 | tf_op jit(solution)/shard_map/ppermute | solution.py:29
  70.4 43.2 %collective-permute-start.10 = (bf16[3,8,40,320]{3,2,1,0:T(8,128)(2,1)S(1)}, bf16[3,8,40,320]{3,2,1,0:T(8,128)(2,1)S(1)}, u32[]{:S(2)}, u32[]{:S(2)}) collective-permute-start(bf16[3,8,40,320]{3,2,1,0:T(8,128)(2,1)S(1)} %get-tuple-element.98), channel_id=1, source_target_pairs={{0,2},{2,4},{4,6},{6,0},{1,3},{3,5},{5,7},{7,1},{8,10},{10,12},{12... | collective-permute-start | bytes 1843208 | tf_op jit(solution)/shard_map/ppermute | solution.py:33
  70.5 43.1 %collective-permute-start.11 = (bf16[3,8,40,320]{3,2,1,0:T(8,128)(2,1)S(1)}, bf16[3,8,40,320]{3,2,1,0:T(8,128)(2,1)S(1)}, u32[]{:S(2)}, u32[]{:S(2)}) collective-permute-start(bf16[3,8,40,320]{3,2,1,0:T(8,128)(2,1)S(1)} %get-tuple-element.99), channel_id=1, source_target_pairs={{0,6},{2,0},{4,2},{6,4},{1,7},{3,1},{5,3},{7,5},{8,14},{10,8},{12,... | collective-permute-start | bytes 1843208 | tf_op jit(solution)/shard_map/ppermute | solution.py:33
  73.2 24.1 %collective-permute-start.13 = (bf16[3,4,40,320]{3,2,1,0:T(8,128)(2,1)S(1)}, bf16[3,4,40,320]{3,2,1,0:T(8,128)(2,1)S(1)}, u32[]{:S(2)}, u32[]{:S(2)}) collective-permute-start(bf16[3,4,40,320]{3,2,1,0:T(8,128)(2,1)S(1)} %get-tuple-element.102), channel_id=1, source_target_pairs={{0,2},{2,4},{4,6},{6,0},{1,3},{3,5},{5,7},{7,1},{8,10},{10,12},{12... | collective-permute-start | bytes 921608 | tf_op jit(solution)/shard_map/ppermute | solution.py:33
  73.2 24.1 %collective-permute-start.15 = (bf16[3,4,40,320]{3,2,1,0:T(8,128)(2,1)S(1)}, bf16[3,4,40,320]{3,2,1,0:T(8,128)(2,1)S(1)}, u32[]{:S(2)}, u32[]{:S(2)}) collective-permute-start(bf16[3,4,40,320]{3,2,1,0:T(8,128)(2,1)S(1)} %get-tuple-element.103), channel_id=1, source_target_pairs={{0,6},{2,0},{4,2},{6,4},{1,7},{3,1},{5,3},{7,5},{8,14},{10,8},{12,... | collective-permute-start | bytes 921608 | tf_op jit(solution)/shard_map/ppermute | solution.py:33
  97.2 16.4 %collective-permute-start.14 = (bf16[3,4,40,320]{3,2,1,0:T(8,128)(2,1)S(1)}, bf16[3,4,40,320]{3,2,1,0:T(8,128)(2,1)S(1)}, u32[]{:S(2)}, u32[]{:S(2)}) collective-permute-start(bf16[3,4,40,320]{3,2,1,0:T(8,128)(2,1)S(1)} %collective-permute-done.13), channel_id=1, source_target_pairs={{0,2},{2,4},{4,6},{6,0},{1,3},{3,5},{5,7},{7,1},{8,10},{10,12},{12... | collective-permute-start | bytes 921608 | tf_op jit(solution)/shard_map/ppermute | solution.py:33
  97.2 16.4 %collective-permute-start.16 = (bf16[3,4,40,320]{3,2,1,0:T(8,128)(2,1)S(1)}, bf16[3,4,40,320]{3,2,1,0:T(8,128)(2,1)S(1)}, u32[]{:S(2)}, u32[]{:S(2)}) collective-permute-start(bf16[3,4,40,320]{3,2,1,0:T(8,128)(2,1)S(1)} %collective-permute-done.15), channel_id=1, source_target_pairs={{0,6},{2,0},{4,2},{6,4},{1,7},{3,1},{5,3},{7,5},{8,14},{10,8},{12,... | collective-permute-start | bytes 921608 | tf_op jit(solution)/shard_map/ppermute | solution.py:33
  99.9 7.1 %collective-permute-start.18 = (f32[8,320]{1,0:T(8,128)S(1)}, f32[8,320]{1,0:T(8,128)S(1)}, u32[]{:S(2)}, u32[]{:S(2)}) collective-permute-start(f32[8,320]{1,0:T(8,128)S(1)} %add.72.g0), channel_id=1, source_target_pairs={{0,4},{2,6},{4,0},{6,2},{1,5},{3,7},{5,1},{7,3},{8,12},{10,14},{12... | collective-permute-start | bytes 30728 | tf_op jit(solution)/shard_map/ppermute | solution.py:33
  107.0 3.8 %collective-permute-start.19 = (f32[8,320]{1,0:T(8,128)S(1)}, f32[8,320]{1,0:T(8,128)S(1)}, u32[]{:S(2)}, u32[]{:S(2)}) collective-permute-start(f32[8,320]{1,0:T(8,128)S(1)} %add.72.g0), channel_id=1, source_target_pairs={{0,2},{2,4},{4,6},{6,0},{1,3},{3,5},{5,7},{7,1},{8,10},{10,12},{12... | collective-permute-start | bytes 30728 | tf_op jit(solution)/shard_map/ppermute | solution.py:33
  110.8 2.8 %collective-permute-start.20 = (f32[8,320]{1,0:T(8,128)S(1)}, f32[8,320]{1,0:T(8,128)S(1)}, u32[]{:S(2)}, u32[]{:S(2)}) collective-permute-start(f32[8,320]{1,0:T(8,128)S(1)} %add.72.g0), channel_id=1, source_target_pairs={{0,6},{2,0},{4,2},{6,4},{1,7},{3,1},{5,3},{7,5},{8,14},{10,8},{12,... | collective-permute-start | bytes 30728 | tf_op jit(solution)/shard_map/ppermute | solution.py:33
  113.7 8.6 %copy-start.14 = (bf16[352,640]{1,0:T(8,128)(2,1)S(1)}, bf16[352,640]{1,0:T(8,128)(2,1)}, u32[]{:S(2)}) copy-start(bf16[352,640]{1,0:T(8,128)(2,1)} %get-tuple-element.89) | copy-start | bytes 1351684
  115.0 25.5 %all-to-all-start.2 = ((bf16[8,16,8,320]{3,2,1,0:T(8,128)(2,1)}), bf16[8,16,8,320]{3,2,1,0:T(8,128)(2,1)S(1)}, u32[]{:S(2)}, u32[]{:S(2)}) async-start(bf16[8,16,8,320]{3,2,1,0:T(8,128)(2,1)} %shard_map.143), calls=%async_computation.2 | async-start | bytes 1572864 | tf_op jit(solution)/shard_map/all_to_all | solution.py:459
  122.3 14.5 %collective-permute-start.7 = (bf16[352,640]{1,0:T(8,128)(2,1)S(1)}, bf16[352,640]{1,0:T(8,128)(2,1)S(1)}, u32[]{:S(2)}, u32[]{:S(2)}) collective-permute-start(bf16[352,640]{1,0:T(8,128)(2,1)S(1)} %copy-done.14), channel_id=1, source_target_pairs={{0,1},{1,0},{2,3},{3,2},{4,5},{5,4},{6,7},{7,6},{8,9},{9,8},{10,11... | collective-permute-start | bytes 1351688 | tf_op jit(solution)/shard_map/ppermute | solution.py:29
  136.7 0.8 copy-start.12
  140.6 39.9 %all-to-all-start.1 = ((bf16[48,32,640]{2,1,0:T(8,128)(2,1)}), bf16[48,32,640]{2,1,0:T(8,128)(2,1)S(1)}, u32[]{:S(2)}, u32[]{:S(2)}) async-start(bf16[48,32,640]{2,1,0:T(8,128)(2,1)} %get-tuple-element.90), calls=%async_computation.1 | async-start | bytes 3932160 | tf_op jit(solution)/shard_map/all_to_all | solution.py:466
  180.5 1.3 copy-start.5
  184.0 0.8 copy-start.3

commit v2 on v0

--- a/solution.py
+++ b/solution.py
@@ -33,6 +33,10 @@
     return lax.ppermute(x, axis, [(i, (i + step) % 4) for i in range(4)])
 
 
+def grant(mib):
+    return pltpu.CompilerParams(vmem_limit_bytes=mib * 2**20)
+
+
 def vmem(n):
     return [pl.BlockSpec(memory_space=VMEM)] * n
 
@@ -92,6 +96,7 @@
         in_specs=smem(3),
         out_specs=tuple(smem(5)),
         scratch_shapes=[pltpu.SMEM((256,), jnp.int32)],
+        compiler_params=grant(1),
         name="routes",
     )(meta, trunc, tmap)
 
@@ -112,6 +117,7 @@
             out_specs=pl.BlockSpec((3, 160, 640), lambda i, meta: (0, 0, 0)),
         ),
         out_shape=jax.ShapeDtypeStruct((3, 160, 640), BF),
+        compiler_params=grant(6),
         name="halves",
     )(meta, wv, wg, wo)
 
@@ -139,6 +145,7 @@
         out_shape=jax.ShapeDtypeStruct((2, 11, 32, 640), BF),
         in_specs=smem(4) + vmem(3),
         out_specs=vmem(1)[0],
+        compiler_params=grant(10),
         name="prologue",
     )(meta, trunc, times, table, lat, cot, gain)
 
@@ -149,13 +156,6 @@
 
 def dot(a, b, dims=PLAIN):
     return lax.dot_general(a, b, dims, preferred_element_type=F32)
-
-
-def load_rows(own, other, rows, turned):
-    for j in range(2):
-        rows[j, :352] = own[j]
-        rows[j, 352:] = other[j]
-        turned[j] = rows[j].T
 
 
 def hidden_part(rows, w, acts, start, width):
@@ -171,12 +171,27 @@
     acts[2, :, span] = (value * gelu).astype(BF)
 
 
-def near_kernel(meta, own, other, wv, wg, wo, below, below2, above, above2, dn, mine, send,
-                rows, turned, w, acts, keep):
+def local(kernel, mib, out_shapes, arrays, scratch=(), scalars=()):
+    out = pl.pallas_call(
+        kernel,
+        out_shape=tuple(jax.ShapeDtypeStruct(s, d) for s, d in out_shapes),
+        in_specs=smem(len(scalars)) + vmem(len(arrays)),
+        out_specs=tuple(vmem(len(out_shapes))),
+        scratch_shapes=[pltpu.VMEM(s, d) for s, d in scratch],
+        compiler_params=grant(mib),
+    )(*scalars, *arrays)
+    return out
+
+
+def near_kernel(meta, own, other, wv, wg, wo, below, below2, above, above2,
+                dn, acts, rows, turned, w):
     c = meta[1]
     here = pl.multiple_of(c * 160, 16)
     there = pl.multiple_of((1 - c) * 160, 16)
-    load_rows(own, other, rows, turned)
+    for j in range(2):
+        rows[j, :352] = own[j]
+        rows[j, 352:] = other[j]
+        turned[j] = rows[j].T
     for j, ref in enumerate((wv, wg, wo)):
         w[j, :320] = ref[...]
         w[j, pl.ds(320 + here, 160)] = above[j]
@@ -186,6 +201,20 @@
     for start, width in ((0, 256), (256, 256), (512, 256), (768, 192)):
         hidden_part(rows, w, acts, start, width)
     dn[...] = dot(acts[0], w[0]) + dot(acts[1], w[1])
+
+
+def near_forward(meta, *arrays):
+    return local(
+        near_kernel, 18,
+        (
+            ((704, 640), F32), ((3, 704, 960), BF), ((2, 704, 640), BF), ((2, 640, 704), BF),
+        ),
+        arrays, [((3, 960, 640), BF)], (meta,),
+    )
+
+
+def near_grads_kernel(meta, turned, acts, mine, send, keep):
+    c = meta[1]
     for j in range(3):
         keep[...] = dot(turned[j // 2], acts[j]).reshape(8, 2, 40, 960)
         for out, side in ((mine, c), (send, 1 - c)):
@@ -196,23 +225,12 @@
             out[2, j] = both[:, 640:].reshape(8, 40, 320).astype(BF)
 
 
-def near_block(meta, own, other, wv, wg, wo, below, below2, above, above2):
-    grads = jax.ShapeDtypeStruct((3, 3, 8, 40, 320), BF)
-    return pl.pallas_call(
-        near_kernel,
-        out_shape=(jax.ShapeDtypeStruct((704, 640), F32), grads, grads),
-        in_specs=smem(1) + vmem(9),
-        out_specs=tuple(vmem(3)),
-        scratch_shapes=[
-            pltpu.VMEM((2, 704, 640), BF),
-            pltpu.VMEM((2, 640, 704), BF),
-            pltpu.VMEM((3, 960, 640), BF),
-            pltpu.VMEM((3, 704, 960), BF),
-            pltpu.VMEM((8, 2, 40, 960), F32),
-        ],
-        compiler_params=pltpu.CompilerParams(vmem_limit_bytes=56 * 2**20),
-        name="near_block",
-    )(meta, own, other, wv, wg, wo, below, below2, above, above2)
+def near_grads(meta, turned, acts):
+    grads = ((3, 3, 8, 40, 320), BF)
+    return local(
+        near_grads_kernel, 14, (grads, grads), (turned, acts),
+        [((8, 2, 40, 960), F32)], (meta,),
+    )
 
 
 def split_gain(g):
@@ -237,12 +255,10 @@
     return rows + pltpu.roll(rows, 6, 0)
 
 
-def far_kernel(meta, own, other, gain, near_dn, first, second, dn, dn_send, mine, send,
-               rows, turned, w, acts, keep):
+def far_kernel(meta, rows, gain, near_dn, first, second, dn, dn_send, acts, tail, w):
     c = meta[1]
     here = pl.multiple_of(c * 160, 16)
     there = pl.multiple_of((1 - c) * 160, 16)
-    load_rows(own, other, rows, turned)
     for j in range(3):
         w[j, pl.ds(here, 160)] = first[j]
         w[j, pl.ds(there, 160)] = second[j]
@@ -251,38 +267,34 @@
     dn[...] = total[:352]
     dn_send[...] = total[352:].astype(BF)
     gsum = jnp.sum(total * rows[0].astype(F32), axis=0, keepdims=True) / gain[...]
-    tail = split_gain(gsum).astype(BF)
+    tail[...] = split_gain(gsum)
+
+
+def far_forward(meta, *arrays):
+    return local(
+        far_kernel, 14,
+        (((352, 640), F32), ((352, 640), BF), ((3, 704, 320), BF), ((8, 320), F32)),
+        arrays, [((3, 320, 640), BF)], (meta,),
+    )
+
+
+def far_grads_kernel(meta, turned, acts, tail, mine, send, keep):
+    c = meta[1]
     for j in range(3):
         keep[...] = dot(turned[j // 2], acts[j]).reshape(8, 2, 40, 320)
         for out, side in ((mine, c), (send, 1 - c)):
             out[8 * j : 8 * j + 8] = keep[:, side].astype(BF)
     for out in (mine, send):
         out[24] = jnp.zeros((40, 320), BF)
-        out[24, :8] = tail
-
-
-def far_block(meta, own, other, gain, near_dn, first, second):
-    grads = jax.ShapeDtypeStruct((25, 40, 320), BF)
-    return pl.pallas_call(
-        far_kernel,
-        out_shape=(
-            jax.ShapeDtypeStruct((352, 640), F32),
-            jax.ShapeDtypeStruct((352, 640), BF),
-            grads,
-            grads,
-        ),
-        in_specs=smem(1) + vmem(6),
-        out_specs=tuple(vmem(4)),
-        scratch_shapes=[
-            pltpu.VMEM((2, 704, 640), BF),
-            pltpu.VMEM((2, 640, 704), BF),
-            pltpu.VMEM((3, 320, 640), BF),
-            pltpu.VMEM((3, 704, 320), BF),
-            pltpu.VMEM((8, 2, 40, 320), F32),
-        ],
-        compiler_params=pltpu.CompilerParams(vmem_limit_bytes=56 * 2**20),
-        name="far_block",
-    )(meta, own, other, gain, near_dn, first, second)
+        out[24, :8] = tail[...].astype(BF)
+
+
+def far_grads(meta, turned, acts, tail):
+    grads = ((25, 40, 320), BF)
+    return local(
+        far_grads_kernel, 10, (grads, grads), (turned, acts, tail),
+        [((8, 2, 40, 320), F32)], (meta,),
+    )
 
 
 def finish_kernel(dest_g, dest_r, dn, got, lat, grad, gain, own, packed, sems):
@@ -320,8 +332,9 @@
             jax.ShapeDtypeStruct((16 * PLACES, 32, 640), BF),
         ),
         in_specs=smem(2) + vmem(5),
-        out_specs=(vmem(1)[0], pl.BlockSpec(memory_space=pl.ANY)),
+        out_specs=(vmem(1)[0], pl.BlockSpec(memory_space=pltpu.MemorySpace.HBM)),
         scratch_shapes=[pltpu.SemaphoreType.DMA((11,))],
+        compiler_params=grant(10),
         name="finish",
     )(dest_g, dest_r, dn, got, lat, grad, gain)
 
@@ -352,18 +365,9 @@
         in_specs=smem(2) + [pl.BlockSpec(memory_space=pl.ANY)],
         out_specs=pl.BlockSpec(memory_space=pl.ANY),
         scratch_shapes=[pltpu.VMEM((32, 640), BF), pltpu.SemaphoreType.DMA((11,))],
+        compiler_params=grant(2),
         name="unpack",
     )(src_p, src_r, came)
-
-
-def local(kernel, out_shapes, *arrays):
-    return pl.pallas_call(
-        kernel,
-        out_shape=tuple(jax.ShapeDtypeStruct(s, d) for s, d in out_shapes),
-        in_specs=vmem(len(arrays)),
-        out_specs=tuple(vmem(len(out_shapes))),
-        compiler_params=pltpu.CompilerParams(vmem_limit_bytes=32 * 2**20),
-    )(*arrays)
 
 
 def near_sums_kernel(mine, got, own, up, down):
@@ -379,38 +383,50 @@
     tail[...] = joined(mine[24, :8]) + joined(got[24, :8])
 
 
-def over_y_kernel(own, from_down, from_up, far_lower, far_upper, g0, g1, g2, g3, out):
+def over_y_kernel(meta, own, from_down, from_up, far_lower, far_upper, g0, g1, g2, g3,
+                  keep, up, down, far, parts):
     for j in range(3):
-        for half, far in ((0, far_lower), (4, far_upper)):
+        for half, came in ((0, far_lower), (4, far_upper)):
             at = slice(half, half + 4)
             x = own[j, at] + from_down[j, at].astype(F32)
-            x = x + (from_up[j, at].astype(F32) + far[j].astype(F32))
-            out[at, 5 * j : 5 * j + 5] = x.astype(BF).reshape(4, 5, 8, 320)
-    tail = resplit((g0[...] + g1[...]) + (g2[...] + g3[...])).astype(BF)
-    for k in range(8):
-        out[k, 15] = tail
-
-
-def last_kernel(parts, value, gate, out, tail):
-    total = parts[0].astype(F32)
-    for k in range(1, 8):
-        total = total + parts[k].astype(F32)
+            x = x + (from_up[j, at].astype(F32) + came[j].astype(F32))
+            parts[half // 4, :, 5 * j : 5 * j + 5] = x.reshape(4, 5, 8, 320)
+    tail = resplit((g0[...] + g1[...]) + (g2[...] + g3[...]))
+    for k in range(2):
+        for z in range(4):
+            parts[k, z, 15] = tail
+    z = meta[2]
+    for out, step in ((keep, 0), (up, 1), (down, 3), (far, 2)):
+        out[...] = parts[:, lax.rem(z + step, 4)].astype(out.dtype)
+
+
+def over_z_kernel(meta, own, down, up, far, keep, give, sums):
+    sums[...] = (own[...] + far[...].astype(F32)) + (down[...].astype(F32) + up[...].astype(F32))
+    for k in range(2):
+        sums[k, 15] = resplit(joined(sums[k, 15]))
+    keep[...] = sums[meta[3]]
+    give[...] = sums[1 - meta[3]].astype(BF)
+
+
+def last_kernel(keep, got, value, gate, out, tail):
+    total = keep[...] + got[...].astype(F32)
     for j, ref in enumerate((value, gate, out)):
         ref[...] = total[5 * j : 5 * j + 5].reshape(40, 320)
     tail[...] = joined(total[15])
 
 
-def reduce_weights(near_mine, near_got, far_mine, far_got):
+def reduce_weights(meta, near_mine, near_got, far_mine, far_got):
     grads = (3, 8, 40, 320)
     half = (3, 4, 40, 320)
     row = ((8, 320), F32)
     own, up, down = local(
-        near_sums_kernel, ((grads, F32), (grads, BF), (grads, BF)), near_mine, near_got
+        near_sums_kernel, 4, ((grads, F32), (grads, BF), (grads, BF)),
+        (near_mine, near_got),
     )
     from_down = ring(up, "y", 1)
     from_up = ring(down, "y", -1)
     lower, upper, tail = local(
-        far_sums_kernel, ((half, BF), (half, BF), row), far_mine, far_got
+        far_sums_kernel, 4, ((half, BF), (half, BF), row), (far_mine, far_got)
     )
     lower = ring(lower, "y", 1)
     upper = ring(upper, "y", -1)
@@ -418,13 +434,19 @@
     upper = ring(upper, "y", -1)
     tail = tail + swap(tail, "xl")
     tails = [tail] + [ring(tail, "y", d) for d in (2, 1, -1)]
-    (parts,) = local(
-        over_y_kernel, (((8, 16, 8, 320), BF),),
-        own, from_down, from_up, lower, upper, *tails,
-    )
-    parts = lax.all_to_all(parts, ("xh", "z"), 0, 0, tiled=True)
+    part = (2, 16, 8, 320)
+    own, up, down, far = local(
+        over_y_kernel, 6, ((part, F32), (part, BF), (part, BF), (part, BF)),
+        (own, from_down, from_up, lower, upper, *tails), [((2, 4, 16, 8, 320), F32)], (meta,),
+    )
+    came = ring(up, "z", 1), ring(down, "z", -1), ring(far, "z", 2)
+    keep, give = local(
+        over_z_kernel, 4, ((part[1:], F32), (part[1:], BF)), (own, *came),
+        [(part, F32)], (meta,),
+    )
+    got = swap(give, "xh")
     out = ((40, 320), F32)
-    value, gate, proj, tail = local(last_kernel, (out, out, out, row), parts)
+    value, gate, proj, tail = local(last_kernel, 2, (out, out, out, row), (keep, got))
     return value, gate, proj, tail[:2].reshape(640)
 
 
@@ -434,33 +456,30 @@
 
 def more_rounds(placed, own, most, dest_g, dest_r, src_p, src_r):
     def more(state):
-        return state[0] * PLACES < most[0]
+        return state[0] < most[0]
 
     def one(state):
         t, placed = state
-        rank = dest_r - t * PLACES
-        here = (rank >= 0) & (rank < PLACES) & (dest_r >= 0)
-        place = jnp.where(here, dest_g * PLACES + rank, -1)
-        hit = place[None, :] == jnp.arange(16 * PLACES, dtype=jnp.int32)[:, None]
+        groups = jnp.arange(16, dtype=jnp.int32)
+        hit = (dest_g[None, :] == groups[:, None]) & (dest_r[None, :] == t)
         pick = jnp.sum(jnp.where(hit, jnp.arange(11, dtype=jnp.int32)[None, :], 0), axis=1)
         came = route(jnp.take(own, pick, axis=0))
-        rank = src_r - t * PLACES
-        here = (rank >= 0) & (rank < PLACES) & (src_r >= 0)
-        new = jnp.take(came, jnp.where(here, src_p * PLACES + rank, 0), axis=0)
+        here = src_r == t
+        new = jnp.take(came, jnp.where(here, src_p, 0), axis=0)
         return t + 1, jnp.where(here[:, None, None], new, placed)
 
-    return lax.while_loop(more, one, (jnp.int32(1), placed))[1]
+    return lax.while_loop(more, one, (jnp.int32(PLACES), placed))[1]
 
 
 def per_device(latents, cotangent, trunc, times, tmap, gain, w_value, w_gate, w_out):
-    meta = jnp.stack([lax.axis_index(a) for a in (DP, "c")]).astype(jnp.int32)
+    meta = jnp.stack([lax.axis_index(a) for a in (DP, "c", "z", "xh")]).astype(jnp.int32)
     gain = gain[None, :]
     wv, wg, wo = w_value.T, w_gate.T, w_out.T
-    rows = prologue(meta, trunc, times, noise_table(), latents, cotangent, gain)
-    other = swap(rows, "xl")
     half = halves(meta, wv, wg, wo)
     below = ring(half, "y", 1)
     above = ring(half, "y", -1)
+    rows = prologue(meta, trunc, times, noise_table(), latents, cotangent, gain)
+    other = swap(rows, "xl")
     dest_g, dest_r, src_p, src_r, most = index_work(meta, trunc, tmap)
     below2 = swap(below, "c")
     above2 = swap(above, "c")
@@ -468,12 +487,14 @@
     second = ring(above2, "y", -1)
     rows2 = rows.reshape(2, 352, 640)
     other = other.reshape(2, 352, 640)
-    near_dn, near_mine, near_send = near_block(
+    near_dn, near_acts, both, turned = near_forward(
         meta, rows2, other, wv, wg, wo, below, below2, above, above2
     )
+    near_mine, near_send = near_grads(meta, turned, near_acts)
     near_got = swap(near_send, "c")
-    dn, dn_send, far_mine, far_send = far_block(meta, rows2, other, gain, near_dn, first, second)
+    dn, dn_send, far_acts, tail = far_forward(meta, both, gain, near_dn, first, second)
     got = swap(dn_send, "xl")
+    far_mine, far_send = far_grads(meta, turned, far_acts, tail)
     far_got = swap(far_send, "c")
     tiles = (11, 32, 640)
     own, packed = finish(
@@ -482,7 +503,7 @@
     came = route(packed)
     placed = unpack(src_p, src_r, came)
     placed = more_rounds(placed, own, most, dest_g, dest_r, src_p, src_r)
-    grads = reduce_weights(near_mine, near_got, far_mine, far_got)
+    grads = reduce_weights(meta, near_mine, near_got, far_mine, far_got)
     return placed, *grads
 
 

time: 168 us -> 155 us (0.923)
  the two profiles are of different devices: /device:TPU:0 before, /device:TPU:6 now
where the time goes in v2:
time: 155 us
  waiting for transfers between devices  69.6 us (45%)
  Pallas kernels  36.9 us (24%)
  starting transfers between devices  33.1 us (21%)
  local copies, waits for them, and re-layouts  13.9 us (9%)
    ppermute x16, waiting for transfers between devices, ring(): return lax.ppermute(x, axis, [(i, (i + step) % 4) for i in range(4)])  46.3 us
    pallas_call x9, Pallas kernels, local(): pl.pallas_call(kernel, out_shape=tuple((jax.ShapeDtypeStruct(s, d) for s,...  24.1 us
    ppermute x8, waiting for transfers between devices, swap(): return lax.ppermute(x, axis, [(0, 1), (1, 0)])  23.2 us
    ppermute x16, starting transfers between devices, ring(): return lax.ppermute(x, axis, [(i, (i + step) % 4) for i in range(4)])  21.2 us
    unnamed x42, local copies, waits for them, and re-layouts  12.5 us
    all_to_all x1, starting transfers between devices, route(): return lax.all_to_all(packed, DP, 0, 0, tiled=True)  8.64 us
    pallas_call x1, Pallas kernels, index_work(): pl.pallas_call(index_kernel, out_shape=(i11, i11, i11, i11, jax.ShapeDtyp...  5.96 us
    pallas_call x1, Pallas kernels, finish(): pl.pallas_call(finish_kernel, out_shape=(jax.ShapeDtypeStruct((11, 32, 64...  3.79 us
  transfers between devices with their start and end apart: 25, of which 14 were waited for; matrix products, arithmetic and copies ran while one was open for 1% of the time, Pallas kernels for 23%

profile of v2, /device:TPU:6, one launch (start us, length us, event | category | flops | bytes accessed | tf_op | source)
XLA Modules:
  0.0 155.0 jit_solution(16879366298837380447)
XLA Ops:
  0.7 1.0 copy-done.6
  1.8 1.0 copy-done.8
  2.8 1.0 copy-done.10
  4.4 3.1 %collective-permute-start.3 = (bf16[3,160,640]{2,1,0:T(8,128)(2,1)S(1)}, bf16[3,160,640]{2,1,0:T(8,128)(2,1)S(1)}, u32[]{:S(2)}, u32[]{:S(2)}) collective-permute-start(bf16[3,160,640]{2,1,0:T(8,128)(2,1)S(1)} %halves.1), channel_id=1, source_target_pairs={{0,6},{2,0},{4,2},{6,4},{1,7},{3,1},{5,3},{7,5},{8,14},{10,8},{12,... | collective-permute-start | bytes 1843208 | tf_op jit(solution)/shard_map/ppermute | solution.py:33
  8.2 1.0 copy-done.14
  11.2 1.0 prologue.1.grad
  12.2 0.9 collective-permute-start
  13.1 7.4 %collective-permute-done.3.above = bf16[3,160,640]{2,1,0:T(8,128)(2,1)S(1)} collective-permute-done((bf16[3,160,640]{2,1,0:T(8,128)(2,1)S(1)}, bf16[3,160,640]{2,1,0:T(8,128)(2,1)S(1)}, u32[]{:S(2)}, u32[]{:S(2)}) %collective-permute-start.3) | collective-permute-done | bytes 614432 | tf_op jit(solution)/shard_map/ppermute | solution.py:33
  20.6 3.4 %collective-permute-done.1.below = bf16[3,160,640]{2,1,0:T(8,128)(2,1)S(1)} collective-permute-done((bf16[3,160,640]{2,1,0:T(8,128)(2,1)S(1)}, bf16[3,160,640]{2,1,0:T(8,128)(2,1)S(1)}, u32[]{:S(2)}, u32[]{:S(2)}) %collective-permute-start.1) | collective-permute-done | bytes 614432 | tf_op jit(solution)/shard_map/ppermute | solution.py:33
  24.0 3.2 %collective-permute-start.6 = (bf16[3,160,640]{2,1,0:T(8,128)(2,1)S(1)}, bf16[3,160,640]{2,1,0:T(8,128)(2,1)S(1)}, u32[]{:S(2)}, u32[]{:S(2)}) collective-permute-start(bf16[3,160,640]{2,1,0:T(8,128)(2,1)S(1)} %collective-permute-done.4.above2), channel_id=1, source_target_pairs={{0,6},{2,0},{4,2},{6,4},{1,7},{3,1},{5,3},{7,5},{8,14},{10,8},{12,... | collective-permute-start | bytes 1843208 | tf_op jit(solution)/shard_map/ppermute | solution.py:33
  27.2 6.5 %collective-permute-done = bf16[2,11,32,640]{3,2,1,0:T(8,128)(2,1)S(1)} collective-permute-done((bf16[2,11,32,640]{3,2,1,0:T(8,128)(2,1)S(1)}, bf16[2,11,32,640]{3,2,1,0:T(8,128)(2,1)S(1)}, u32[]{:S(2)}, u32[]{:S(2)}) %collective-permute-start) | collective-permute-done | bytes 901152 | tf_op jit(solution)/shard_map/ppermute | solution.py:29
  33.8 7.7 %shard_map.137 = (f32[704,640]{1,0:T(8,128)S(1)}, bf16[3,704,960]{2,1,0:T(8,128)(2,1)S(1)}, bf16[2,704,640]{2,1,0:T(8,128)(2,1)S(1)}, bf16[2,640,704]{2,1,0:T(8,128)(2,1)S(1)}) custom-call(s32[4]{0:T(128)S(1)} %pad_add_fusion.meta, bf16[2,352,640]{2,1,0:T(8,128)(2,1)S(1)} %bitcast.29, bf16[2,352,640]{2,1,0:T(8,128)(2,1)S(1)} %bitcast.37, ...), custom_call_target="tpu_custom_call" | custom-call | tf_op jit(solution)/shard_map/pallas_call | solution.py:175
  41.5 5.7 %shard_map.139 = (bf16[3,3,8,40,320]{4,3,2,1,0:T(8,128)(2,1)S(1)}, bf16[3,3,8,40,320]{4,3,2,1,0:T(8,128)(2,1)}) custom-call(s32[4]{0:T(128)S(1)} %pad_add_fusion.meta, bf16[2,640,704]{2,1,0:T(8,128)(2,1)S(1)} %get-tuple-element.95.turned, bf16[3,704,960]{2,1,0:T(8,128)(2,1)S(1)} %get-tuple-element.96.acts), custom_call_target="tpu_custom_call" | custom-call | tf_op jit(solution)/shard_map/pallas_call | solution.py:175
  47.1 1.4 copy-done.2
  48.6 3.7 %shard_map.138 = (f32[352,640]{1,0:T(8,128)S(1)}, bf16[352,640]{1,0:T(8,128)(2,1)S(1)}, bf16[3,704,320]{2,1,0:T(8,128)(2,1)S(1)}, f32[8,320]{1,0:T(8,128)S(1)}) custom-call(s32[4]{0:T(128)S(1)} %pad_add_fusion.meta, bf16[2,704,640]{2,1,0:T(8,128)(2,1)S(1)} %get-tuple-element.87.rows, f32[1,640]{1,0:T(1,128)S(1)} %broadcast_in_dim.54.gain, ...), custom_call_target="tpu_custom_call" | custom-call | tf_op jit(solution)/shard_map/pallas_call | solution.py:175
  52.2 0.9 collective-permute-start.7
  53.1 6.0 %routes.1 = (s32[11]{0:T(128)S(1)}, s32[11]{0:T(128)S(1)}, s32[11]{0:T(128)S(1)}, s32[11]{0:T(128)S(1)}, s32[1]{0:T(128)}) custom-call(s32[4]{0:T(128)S(1)} %pad_add_fusion.meta, s32[16]{0:T(128)S(1)} %copy-done.17, s32[176]{0:T(256)S(1)} %copy-done.19), custom_call_target="tpu_custom_call" | custom-call | tf_op jit(solution)/shard_map/routes/pallas_call | solution.py:93
  59.1 5.9 %collective-permute-done.7 = bf16[352,640]{1,0:T(8,128)(2,1)S(1)} collective-permute-done((bf16[352,640]{1,0:T(8,128)(2,1)S(1)}, bf16[352,640]{1,0:T(8,128)(2,1)S(1)}, u32[]{:S(2)}, u32[]{:S(2)}) %collective-permute-start.7) | collective-permute-done | bytes 450592 | tf_op jit(solution)/shard_map/ppermute | solution.py:29
  65.0 3.8 %finish.1 = (bf16[11,32,640]{2,1,0:T(8,128)(2,1)S(1)}, bf16[48,32,640]{2,1,0:T(8,128)(2,1)S(1)}) custom-call(s32[11]{0:T(128)S(1)} %get-tuple-element.196.dest_g, s32[11]{0:T(128)S(1)} %get-tuple-element.197.dest_r, f32[11,32,640]{2,1,0:T(8,128)S(1)} %bitcast.36, bf16[11,32,640]{2,1,0:T(8,128)(2,1)S(1)} %bitcast.38, bf16[11,32,640]{2,1,0:T(8,128)(2,1)S(1)} %copy-done.5, ...), custom_call_target="tpu_custom_call" | custom-call | tf_op jit(solution)/shard_map/finish/pallas_call | solution.py:328
  68.8 1.3 copy-done.4
  70.1 8.6 %all-to-all-start.1 = ((bf16[48,32,640]{2,1,0:T(8,128)(2,1)}), bf16[48,32,640]{2,1,0:T(8,128)(2,1)S(1)}, u32[]{:S(2)}, u32[]{:S(2)}) async-start(bf16[48,32,640]{2,1,0:T(8,128)(2,1)} %copy-done.4), calls=%async_computation.1 | async-start | bytes 3932160 | tf_op jit(solution)/shard_map/all_to_all | solution.py:454
  78.7 1.5 copy-done.1
  80.3 1.4 copy-done.13
  81.7 2.3 %shard_map.141 = (bf16[25,40,320]{2,1,0:T(8,128)(2,1)S(1)}, bf16[25,40,320]{2,1,0:T(8,128)(2,1)S(1)}) custom-call(s32[4]{0:T(128)S(1)} %pad_add_fusion.meta, bf16[2,640,704]{2,1,0:T(8,128)(2,1)S(1)} %copy-done.1, bf16[3,704,320]{2,1,0:T(8,128)(2,1)S(1)} %copy-done.13, f32[8,320]{1,0:T(8,128)S(1)} %get-tuple-element.103.tail), custom_call_target="tpu_custom_call" | custom-call | tf_op jit(solution)/shard_map/pallas_call | solution.py:175
  84.2 2.1 %collective-permute-done.11.got = bf16[25,40,320]{2,1,0:T(8,128)(2,1)S(1)} collective-permute-done((bf16[25,40,320]{2,1,0:T(8,128)(2,1)S(1)}, bf16[25,40,320]{2,1,0:T(8,128)(2,1)S(1)}, u32[]{:S(2)}, u32[]{:S(2)}) %collective-permute-start.11) | collective-permute-done | bytes 640032 | tf_op jit(solution)/shard_map/ppermute | solution.py:29
  86.9 2.9 %collective-permute-start.14 = (bf16[3,4,40,320]{3,2,1,0:T(8,128)(2,1)S(1)}, bf16[3,4,40,320]{3,2,1,0:T(8,128)(2,1)S(1)}, u32[]{:S(2)}, u32[]{:S(2)}) collective-permute-start(bf16[3,4,40,320]{3,2,1,0:T(8,128)(2,1)S(1)} %get-tuple-element.107), channel_id=1, source_target_pairs={{0,6},{2,0},{4,2},{6,4},{1,7},{3,1},{5,3},{7,5},{8,14},{10,8},{12,... | collective-permute-start | bytes 921608 | tf_op jit(solution)/shard_map/ppermute | solution.py:33
  89.8 2.1 %shard_map.140 = (f32[3,8,40,320]{3,2,1,0:T(8,128)S(1)}, bf16[3,8,40,320]{3,2,1,0:T(8,128)(2,1)S(1)}, bf16[3,8,40,320]{3,2,1,0:T(8,128)(2,1)S(1)}) custom-call(bf16[3,3,8,40,320]{4,3,2,1,0:T(8,128)(2,1)S(1)} %copy-done.3, bf16[3,3,8,40,320]{4,3,2,1,0:T(8,128)(2,1)} %collective-permute-done.8.got), custom_call_target="tpu_custom_call" | custom-call | tf_op jit(solution)/shard_map/pallas_call | solution.py:175
  92.0 1.8 %collective-permute-start.10 = (bf16[3,8,40,320]{3,2,1,0:T(8,128)(2,1)S(1)}, bf16[3,8,40,320]{3,2,1,0:T(8,128)(2,1)S(1)}, u32[]{:S(2)}, u32[]{:S(2)}) collective-permute-start(bf16[3,8,40,320]{3,2,1,0:T(8,128)(2,1)S(1)} %get-tuple-element.101), channel_id=1, source_target_pairs={{0,6},{2,0},{4,2},{6,4},{1,7},{3,1},{5,3},{7,5},{8,14},{10,8},{12,... | collective-permute-start | bytes 1843208 | tf_op jit(solution)/shard_map/ppermute | solution.py:33
  94.1 5.2 %collective-permute-done.12 = bf16[3,4,40,320]{3,2,1,0:T(8,128)(2,1)S(1)} collective-permute-done((bf16[3,4,40,320]{3,2,1,0:T(8,128)(2,1)S(1)}, bf16[3,4,40,320]{3,2,1,0:T(8,128)(2,1)S(1)}, u32[]{:S(2)}, u32[]{:S(2)}) %collective-permute-start.12) | collective-permute-done | bytes 307232 | tf_op jit(solution)/shard_map/ppermute | solution.py:33
  99.3 3.2 %collective-permute-start.15 = (bf16[3,4,40,320]{3,2,1,0:T(8,128)(2,1)S(1)}, bf16[3,4,40,320]{3,2,1,0:T(8,128)(2,1)S(1)}, u32[]{:S(2)}, u32[]{:S(2)}) collective-permute-start(bf16[3,4,40,320]{3,2,1,0:T(8,128)(2,1)S(1)} %collective-permute-done.14), channel_id=1, source_target_pairs={{0,6},{2,0},{4,2},{6,4},{1,7},{3,1},{5,3},{7,5},{8,14},{10,8},{12,... | collective-permute-start | bytes 921608 | tf_op jit(solution)/shard_map/ppermute | solution.py:33
  102.5 0.8 collective-permute-start.16
  103.3 2.9 %collective-permute-done.16 = f32[8,320]{1,0:T(8,128)S(1)} collective-permute-done((f32[8,320]{1,0:T(8,128)S(1)}, f32[8,320]{1,0:T(8,128)S(1)}, u32[]{:S(2)}, u32[]{:S(2)}) %collective-permute-start.16) | collective-permute-done | bytes 10272 | tf_op jit(solution)/shard_map/ppermute | solution.py:29
  106.2 17.4 %collective-permute-done.17.g1 = f32[8,320]{1,0:T(8,128)S(1)} collective-permute-done((f32[8,320]{1,0:T(8,128)S(1)}, f32[8,320]{1,0:T(8,128)S(1)}, u32[]{:S(2)}, u32[]{:S(2)}) %collective-permute-start.17) | collective-permute-done | bytes 10272 | tf_op jit(solution)/shard_map/ppermute | solution.py:33
  123.6 1.1 collective-permute-start.18
  124.7 3.8 %collective-permute-done.18.g2 = f32[8,320]{1,0:T(8,128)S(1)} collective-permute-done((f32[8,320]{1,0:T(8,128)S(1)}, f32[8,320]{1,0:T(8,128)S(1)}, u32[]{:S(2)}, u32[]{:S(2)}) %collective-permute-start.18) | collective-permute-done | bytes 10272 | tf_op jit(solution)/shard_map/ppermute | solution.py:33
  128.5 3.7 %collective-permute-done.19.g3 = f32[8,320]{1,0:T(8,128)S(1)} collective-permute-done((f32[8,320]{1,0:T(8,128)S(1)}, f32[8,320]{1,0:T(8,128)S(1)}, u32[]{:S(2)}, u32[]{:S(2)}) %collective-permute-start.19) | collective-permute-done | bytes 10272 | tf_op jit(solution)/shard_map/ppermute | solution.py:33
  132.2 1.1 shard_map.143
  133.3 1.5 collective-permute-start.20
  134.9 1.8 %collective-permute-start.21 = (bf16[2,16,8,320]{3,2,1,0:T(8,128)(2,1)S(1)}, bf16[2,16,8,320]{3,2,1,0:T(8,128)(2,1)S(1)}, u32[]{:S(2)}, u32[]{:S(2)}) collective-permute-start(bf16[2,16,8,320]{3,2,1,0:T(8,128)(2,1)S(1)} %get-tuple-element.111), channel_id=1, source_target_pairs={{0,48},{16,0},{32,16},{48,32},{1,49},{17,1},{33,17},{49,33},{2,50}... | collective-permute-start | bytes 491528 | tf_op jit(solution)/shard_map/ppermute | solution.py:33
  136.6 1.8 %collective-permute-start.22 = (bf16[2,16,8,320]{3,2,1,0:T(8,128)(2,1)S(1)}, bf16[2,16,8,320]{3,2,1,0:T(8,128)(2,1)S(1)}, u32[]{:S(2)}, u32[]{:S(2)}) collective-permute-start(bf16[2,16,8,320]{3,2,1,0:T(8,128)(2,1)S(1)} %get-tuple-element.112), channel_id=1, source_target_pairs={{0,32},{16,48},{32,0},{48,16},{1,33},{17,49},{33,1},{49,17},{2,34}... | collective-permute-start | bytes 491528 | tf_op jit(solution)/shard_map/ppermute | solution.py:33
  138.4 2.7 %collective-permute-done.20.down = bf16[2,16,8,320]{3,2,1,0:T(8,128)(2,1)S(1)} collective-permute-done((bf16[2,16,8,320]{3,2,1,0:T(8,128)(2,1)S(1)}, bf16[2,16,8,320]{3,2,1,0:T(8,128)(2,1)S(1)}, u32[]{:S(2)}, u32[]{:S(2)}) %collective-permute-start.20) | collective-permute-done | bytes 163872 | tf_op jit(solution)/shard_map/ppermute | solution.py:33
  141.1 0.9 collective-permute-done.21.up
  142.0 1.8 %collective-permute-done.22.far = bf16[2,16,8,320]{3,2,1,0:T(8,128)(2,1)S(1)} collective-permute-done((bf16[2,16,8,320]{3,2,1,0:T(8,128)(2,1)S(1)}, bf16[2,16,8,320]{3,2,1,0:T(8,128)(2,1)S(1)}, u32[]{:S(2)}, u32[]{:S(2)}) %collective-permute-start.22) | collective-permute-done | bytes 163872 | tf_op jit(solution)/shard_map/ppermute | solution.py:33
  143.8 0.7 shard_map.144
  145.0 5.8 %collective-permute-done.23.got = bf16[16,8,320]{2,1,0:T(8,128)(2,1)S(1)} collective-permute-done((bf16[16,8,320]{2,1,0:T(8,128)(2,1)S(1)}, bf16[16,8,320]{2,1,0:T(8,128)(2,1)S(1)}, u32[]{:S(2)}, u32[]{:S(2)}) %collective-permute-start.23) | collective-permute-done | bytes 81952 | tf_op jit(solution)/shard_map/ppermute | solution.py:29
  152.1 1.4 unpack.1
  153.5 0.7 while.10
  154.2 0.8 copy-done.20
  (64 shorter events, 6.3 us)
Async XLA Ops:
  0.6 7.5 %copy-start.5 = (bf16[11,32,640]{2,1,0:T(8,128)(2,1)S(1)}, bf16[11,32,640]{2,1,0:T(8,128)(2,1)}, u32[]{:S(2)}) copy-start(bf16[11,32,640]{2,1,0:T(8,128)(2,1)} %lat.3) | copy-start | bytes 1351684
  0.7 1.0 copy-start.6
  1.8 1.0 copy-start.8
  2.8 1.0 copy-start.10
  3.8 30.0 %copy-start.7 = (bf16[640,320]{0,1:T(8,128)(2,1)S(1)}, bf16[640,320]{0,1:T(8,128)(2,1)}, u32[]{:S(2)}) copy-start(bf16[640,320]{0,1:T(8,128)(2,1)} %param.18) | copy-start | bytes 1228804
  3.8 30.0 %copy-start.9 = (bf16[640,320]{0,1:T(8,128)(2,1)S(1)}, bf16[640,320]{0,1:T(8,128)(2,1)}, u32[]{:S(2)}) copy-start(bf16[640,320]{0,1:T(8,128)(2,1)} %param.19) | copy-start | bytes 1228804
  3.8 30.0 %copy-start.11 = (bf16[640,320]{0,1:T(8,128)(2,1)S(1)}, bf16[640,320]{0,1:T(8,128)(2,1)}, u32[]{:S(2)}) copy-start(bf16[640,320]{0,1:T(8,128)(2,1)} %param.20) | copy-start | bytes 1228804
  4.4 16.2 %collective-permute-start.3 = (bf16[3,160,640]{2,1,0:T(8,128)(2,1)S(1)}, bf16[3,160,640]{2,1,0:T(8,128)(2,1)S(1)}, u32[]{:S(2)}, u32[]{:S(2)}) collective-permute-start(bf16[3,160,640]{2,1,0:T(8,128)(2,1)S(1)} %halves.1), channel_id=1, source_target_pairs={{0,6},{2,0},{4,2},{6,4},{1,7},{3,1},{5,3},{7,5},{8,14},{10,8},{12,... | collective-permute-start | bytes 1843208 | tf_op jit(solution)/shard_map/ppermute | solution.py:33
  7.5 16.5 %collective-permute-start.1 = (bf16[3,160,640]{2,1,0:T(8,128)(2,1)S(1)}, bf16[3,160,640]{2,1,0:T(8,128)(2,1)S(1)}, u32[]{:S(2)}, u32[]{:S(2)}) collective-permute-start(bf16[3,160,640]{2,1,0:T(8,128)(2,1)S(1)} %halves.1), channel_id=1, source_target_pairs={{0,2},{2,4},{4,6},{6,0},{1,3},{3,5},{5,7},{7,1},{8,10},{10,12},{12... | collective-permute-start | bytes 1843208 | tf_op jit(solution)/shard_map/ppermute | solution.py:33
  8.2 1.0 copy-start.14
  9.2 0.7 copy-start.15
  9.9 0.7 copy-start.16
  10.5 0.7 copy-start.18
  12.2 21.5 %collective-permute-start = (bf16[2,11,32,640]{3,2,1,0:T(8,128)(2,1)S(1)}, bf16[2,11,32,640]{3,2,1,0:T(8,128)(2,1)S(1)}, u32[]{:S(2)}, u32[]{:S(2)}) collective-permute-start(bf16[2,11,32,640]{3,2,1,0:T(8,128)(2,1)S(1)} %prologue.1.grad), channel_id=1, source_target_pairs={{0,1},{1,0},{2,3},{3,2},{4,5},{5,4},{6,7},{7,6},{8,9},{9,8},{10,11... | collective-permute-start | bytes 2703368 | tf_op jit(solution)/shard_map/ppermute | solution.py:29
  20.6 3.4 %collective-permute-start.4 = (bf16[3,160,640]{2,1,0:T(8,128)(2,1)S(1)}, bf16[3,160,640]{2,1,0:T(8,128)(2,1)S(1)}, u32[]{:S(2)}, u32[]{:S(2)}) collective-permute-start(bf16[3,160,640]{2,1,0:T(8,128)(2,1)S(1)} %collective-permute-done.3.above), channel_id=1, source_target_pairs={{0,8},{8,0},{1,9},{9,1},{2,10},{10,2},{3,11},{11,3},{4,12},{12,4},... | collective-permute-start | bytes 1843208 | tf_op jit(solution)/shard_map/ppermute | solution.py:29
  24.0 9.8 %collective-permute-start.2 = (bf16[3,160,640]{2,1,0:T(8,128)(2,1)S(1)}, bf16[3,160,640]{2,1,0:T(8,128)(2,1)S(1)}, u32[]{:S(2)}, u32[]{:S(2)}) collective-permute-start(bf16[3,160,640]{2,1,0:T(8,128)(2,1)S(1)} %collective-permute-done.1.below), channel_id=1, source_target_pairs={{0,8},{8,0},{1,9},{9,1},{2,10},{10,2},{3,11},{11,3},{4,12},{12,4},... | collective-permute-start | bytes 1843208 | tf_op jit(solution)/shard_map/ppermute | solution.py:29
  24.0 24.5 %collective-permute-start.5 = (bf16[3,160,640]{2,1,0:T(8,128)(2,1)S(1)}, bf16[3,160,640]{2,1,0:T(8,128)(2,1)S(1)}, u32[]{:S(2)}, u32[]{:S(2)}) collective-permute-start(bf16[3,160,640]{2,1,0:T(8,128)(2,1)S(1)} %collective-permute-done.1.below), channel_id=1, source_target_pairs={{0,2},{2,4},{4,6},{6,0},{1,3},{3,5},{5,7},{7,1},{8,10},{10,12},{12... | collective-permute-start | bytes 1843208 | tf_op jit(solution)/shard_map/ppermute | solution.py:33
  24.0 24.5 %collective-permute-start.6 = (bf16[3,160,640]{2,1,0:T(8,128)(2,1)S(1)}, bf16[3,160,640]{2,1,0:T(8,128)(2,1)S(1)}, u32[]{:S(2)}, u32[]{:S(2)}) collective-permute-start(bf16[3,160,640]{2,1,0:T(8,128)(2,1)S(1)} %collective-permute-done.4.above2), channel_id=1, source_target_pairs={{0,6},{2,0},{4,2},{6,4},{1,7},{3,1},{5,3},{7,5},{8,14},{10,8},{12,... | collective-permute-start | bytes 1843208 | tf_op jit(solution)/shard_map/ppermute | solution.py:33
  41.5 5.7 %copy-start = (bf16[2,640,704]{2,1,0:T(8,128)(2,1)}, bf16[2,640,704]{2,1,0:T(8,128)(2,1)S(1)}, u32[]{:S(2)}) copy-start(bf16[2,640,704]{2,1,0:T(8,128)(2,1)S(1)} %get-tuple-element.95.turned) | copy-start | bytes 5406724
  47.1 1.4 copy-start.2
  48.5 41.3 %collective-permute-start.8 = (bf16[3,3,8,40,320]{4,3,2,1,0:T(8,128)(2,1)}, bf16[3,3,8,40,320]{4,3,2,1,0:T(8,128)(2,1)}, u32[]{:S(2)}, u32[]{:S(2)}) collective-permute-start(bf16[3,3,8,40,320]{4,3,2,1,0:T(8,128)(2,1)} %get-tuple-element.98), channel_id=1, source_target_pairs={{0,8},{8,0},{1,9},{9,1},{2,10},{10,2},{3,11},{11,3},{4,12},{12,4},... | collective-permute-start | bytes 5529608 | tf_op jit(solution)/shard_map/ppermute | solution.py:29
  48.5 4.6 %copy-start.17 = (s32[16]{0:T(128)S(1)}, s32[16]{0:T(128)}, u32[]{:S(2)}) copy-start(s32[16]{0:T(128)} %trunc.3) | copy-start | bytes 196
  48.5 4.5 %copy-start.19 = (s32[176]{0:T(256)S(1)}, s32[176]{0:T(256)}, u32[]{:S(2)}) copy-start(s32[176]{0:T(256)} %tmap.1) | copy-start | bytes 2116
  52.2 16.6 %copy-start.12 = (bf16[3,704,320]{2,1,0:T(8,128)(2,1)}, bf16[3,704,320]{2,1,0:T(8,128)(2,1)S(1)}, u32[]{:S(2)}) copy-start(bf16[3,704,320]{2,1,0:T(8,128)(2,1)S(1)} %get-tuple-element.102.acts) | copy-start | bytes 4055044
  52.2 12.8 %collective-permute-start.7 = (bf16[352,640]{1,0:T(8,128)(2,1)S(1)}, bf16[352,640]{1,0:T(8,128)(2,1)S(1)}, u32[]{:S(2)}, u32[]{:S(2)}) collective-permute-start(bf16[352,640]{1,0:T(8,128)(2,1)S(1)} %get-tuple-element.90), channel_id=1, source_target_pairs={{0,1},{1,0},{2,3},{3,2},{4,5},{5,4},{6,7},{7,6},{8,9},{9,8},{10,11... | collective-permute-start | bytes 1351688 | tf_op jit(solution)/shard_map/ppermute | solution.py:29
  68.8 1.3 copy-start.4
  70.1 82.0 %all-to-all-start.1 = ((bf16[48,32,640]{2,1,0:T(8,128)(2,1)}), bf16[48,32,640]{2,1,0:T(8,128)(2,1)S(1)}, u32[]{:S(2)}, u32[]{:S(2)}) async-start(bf16[48,32,640]{2,1,0:T(8,128)(2,1)} %copy-done.4), calls=%async_computation.1 | async-start | bytes 3932160 | tf_op jit(solution)/shard_map/all_to_all | solution.py:454
  78.7 1.5 copy-start.1
  80.3 1.4 copy-start.13
  81.7 8.2 %copy-start.3 = (bf16[3,3,8,40,320]{4,3,2,1,0:T(8,128)(2,1)S(1)}, bf16[3,3,8,40,320]{4,3,2,1,0:T(8,128)(2,1)}, u32[]{:S(2)}) copy-start(bf16[3,3,8,40,320]{4,3,2,1,0:T(8,128)(2,1)} %copy-done.2) | copy-start | bytes 5529604
  84.0 2.3 %collective-permute-start.11 = (bf16[25,40,320]{2,1,0:T(8,128)(2,1)S(1)}, bf16[25,40,320]{2,1,0:T(8,128)(2,1)S(1)}, u32[]{:S(2)}, u32[]{:S(2)}) collective-permute-start(bf16[25,40,320]{2,1,0:T(8,128)(2,1)S(1)} %get-tuple-element.105), channel_id=1, source_target_pairs={{0,8},{8,0},{1,9},{9,1},{2,10},{10,2},{3,11},{11,3},{4,12},{12,4},... | collective-permute-start | bytes 1920008 | tf_op jit(solution)/shard_map/ppermute | solution.py:29
  86.5 12.7 %collective-permute-start.12 = (bf16[3,4,40,320]{3,2,1,0:T(8,128)(2,1)S(1)}, bf16[3,4,40,320]{3,2,1,0:T(8,128)(2,1)S(1)}, u32[]{:S(2)}, u32[]{:S(2)}) collective-permute-start(bf16[3,4,40,320]{3,2,1,0:T(8,128)(2,1)S(1)} %get-tuple-element.106), channel_id=1, source_target_pairs={{0,2},{2,4},{4,6},{6,0},{1,3},{3,5},{5,7},{7,1},{8,10},{10,12},{12... | collective-permute-start | bytes 921608 | tf_op jit(solution)/shard_map/ppermute | solution.py:33
  86.9 12.4 %collective-permute-start.14 = (bf16[3,4,40,320]{3,2,1,0:T(8,128)(2,1)S(1)}, bf16[3,4,40,320]{3,2,1,0:T(8,128)(2,1)S(1)}, u32[]{:S(2)}, u32[]{:S(2)}) collective-permute-start(bf16[3,4,40,320]{3,2,1,0:T(8,128)(2,1)S(1)} %get-tuple-element.107), channel_id=1, source_target_pairs={{0,6},{2,0},{4,2},{6,4},{1,7},{3,1},{5,3},{7,5},{8,14},{10,8},{12,... | collective-permute-start | bytes 921608 | tf_op jit(solution)/shard_map/ppermute | solution.py:33
  92.0 40.2 %collective-permute-start.10 = (bf16[3,8,40,320]{3,2,1,0:T(8,128)(2,1)S(1)}, bf16[3,8,40,320]{3,2,1,0:T(8,128)(2,1)S(1)}, u32[]{:S(2)}, u32[]{:S(2)}) collective-permute-start(bf16[3,8,40,320]{3,2,1,0:T(8,128)(2,1)S(1)} %get-tuple-element.101), channel_id=1, source_target_pairs={{0,6},{2,0},{4,2},{6,4},{1,7},{3,1},{5,3},{7,5},{8,14},{10,8},{12,... | collective-permute-start | bytes 1843208 | tf_op jit(solution)/shard_map/ppermute | solution.py:33
  93.8 38.4 %collective-permute-start.9 = (bf16[3,8,40,320]{3,2,1,0:T(8,128)(2,1)S(1)}, bf16[3,8,40,320]{3,2,1,0:T(8,128)(2,1)S(1)}, u32[]{:S(2)}, u32[]{:S(2)}) collective-permute-start(bf16[3,8,40,320]{3,2,1,0:T(8,128)(2,1)S(1)} %get-tuple-element.100), channel_id=1, source_target_pairs={{0,2},{2,4},{4,6},{6,0},{1,3},{3,5},{5,7},{7,1},{8,10},{10,12},{12... | collective-permute-start | bytes 1843208 | tf_op jit(solution)/shard_map/ppermute | solution.py:33
  99.3 32.9 %collective-permute-start.13 = (bf16[3,4,40,320]{3,2,1,0:T(8,128)(2,1)S(1)}, bf16[3,4,40,320]{3,2,1,0:T(8,128)(2,1)S(1)}, u32[]{:S(2)}, u32[]{:S(2)}) collective-permute-start(bf16[3,4,40,320]{3,2,1,0:T(8,128)(2,1)S(1)} %collective-permute-done.12), channel_id=1, source_target_pairs={{0,2},{2,4},{4,6},{6,0},{1,3},{3,5},{5,7},{7,1},{8,10},{10,12},{12... | collective-permute-start | bytes 921608 | tf_op jit(solution)/shard_map/ppermute | solution.py:33
  99.3 32.9 %collective-permute-start.15 = (bf16[3,4,40,320]{3,2,1,0:T(8,128)(2,1)S(1)}, bf16[3,4,40,320]{3,2,1,0:T(8,128)(2,1)S(1)}, u32[]{:S(2)}, u32[]{:S(2)}) collective-permute-start(bf16[3,4,40,320]{3,2,1,0:T(8,128)(2,1)S(1)} %collective-permute-done.14), channel_id=1, source_target_pairs={{0,6},{2,0},{4,2},{6,4},{1,7},{3,1},{5,3},{7,5},{8,14},{10,8},{12,... | collective-permute-start | bytes 921608 | tf_op jit(solution)/shard_map/ppermute | solution.py:33
  102.5 3.7 %collective-permute-start.16 = (f32[8,320]{1,0:T(8,128)S(1)}, f32[8,320]{1,0:T(8,128)S(1)}, u32[]{:S(2)}, u32[]{:S(2)}) collective-permute-start(f32[8,320]{1,0:T(8,128)S(1)} %get-tuple-element.108), channel_id=1, source_target_pairs={{0,1},{1,0},{2,3},{3,2},{4,5},{5,4},{6,7},{7,6},{8,9},{9,8},{10,11... | collective-permute-start | bytes 30728 | tf_op jit(solution)/shard_map/ppermute | solution.py:29
  106.2 17.4 %collective-permute-start.17 = (f32[8,320]{1,0:T(8,128)S(1)}, f32[8,320]{1,0:T(8,128)S(1)}, u32[]{:S(2)}, u32[]{:S(2)}) collective-permute-start(f32[8,320]{1,0:T(8,128)S(1)} %add.44.g0), channel_id=1, source_target_pairs={{0,4},{2,6},{4,0},{6,2},{1,5},{3,7},{5,1},{7,3},{8,12},{10,14},{12... | collective-permute-start | bytes 30728 | tf_op jit(solution)/shard_map/ppermute | solution.py:33
  123.6 4.9 %collective-permute-start.18 = (f32[8,320]{1,0:T(8,128)S(1)}, f32[8,320]{1,0:T(8,128)S(1)}, u32[]{:S(2)}, u32[]{:S(2)}) collective-permute-start(f32[8,320]{1,0:T(8,128)S(1)} %add.44.g0), channel_id=1, source_target_pairs={{0,2},{2,4},{4,6},{6,0},{1,3},{3,5},{5,7},{7,1},{8,10},{10,12},{12... | collective-permute-start | bytes 30728 | tf_op jit(solution)/shard_map/ppermute | solution.py:33
  128.5 3.7 %collective-permute-start.19 = (f32[8,320]{1,0:T(8,128)S(1)}, f32[8,320]{1,0:T(8,128)S(1)}, u32[]{:S(2)}, u32[]{:S(2)}) collective-permute-start(f32[8,320]{1,0:T(8,128)S(1)} %add.44.g0), channel_id=1, source_target_pairs={{0,6},{2,0},{4,2},{6,4},{1,7},{3,1},{5,3},{7,5},{8,14},{10,8},{12,... | collective-permute-start | bytes 30728 | tf_op jit(solution)/shard_map/ppermute | solution.py:33
  133.3 7.8 %collective-permute-start.20 = (bf16[2,16,8,320]{3,2,1,0:T(8,128)(2,1)S(1)}, bf16[2,16,8,320]{3,2,1,0:T(8,128)(2,1)S(1)}, u32[]{:S(2)}, u32[]{:S(2)}) collective-permute-start(bf16[2,16,8,320]{3,2,1,0:T(8,128)(2,1)S(1)} %get-tuple-element.110), channel_id=1, source_target_pairs={{0,16},{16,32},{32,48},{48,0},{1,17},{17,33},{33,49},{49,1},{2,18}... | collective-permute-start | bytes 491528 | tf_op jit(solution)/shard_map/ppermute | solution.py:33
  134.9 7.1 %collective-permute-start.21 = (bf16[2,16,8,320]{3,2,1,0:T(8,128)(2,1)S(1)}, bf16[2,16,8,320]{3,2,1,0:T(8,128)(2,1)S(1)}, u32[]{:S(2)}, u32[]{:S(2)}) collective-permute-start(bf16[2,16,8,320]{3,2,1,0:T(8,128)(2,1)S(1)} %get-tuple-element.111), channel_id=1, source_target_pairs={{0,48},{16,0},{32,16},{48,32},{1,49},{17,1},{33,17},{49,33},{2,50}... | collective-permute-start | bytes 491528 | tf_op jit(solution)/shard_map/ppermute | solution.py:33
  136.6 7.2 %collective-permute-start.22 = (bf16[2,16,8,320]{3,2,1,0:T(8,128)(2,1)S(1)}, bf16[2,16,8,320]{3,2,1,0:T(8,128)(2,1)S(1)}, u32[]{:S(2)}, u32[]{:S(2)}) collective-permute-start(bf16[2,16,8,320]{3,2,1,0:T(8,128)(2,1)S(1)} %get-tuple-element.112), channel_id=1, source_target_pairs={{0,32},{16,48},{32,0},{48,16},{1,33},{17,49},{33,1},{49,17},{2,34}... | collective-permute-start | bytes 491528 | tf_op jit(solution)/shard_map/ppermute | solution.py:33
  144.5 6.2 %collective-permute-start.23 = (bf16[16,8,320]{2,1,0:T(8,128)(2,1)S(1)}, bf16[16,8,320]{2,1,0:T(8,128)(2,1)S(1)}, u32[]{:S(2)}, u32[]{:S(2)}) collective-permute-start(bf16[16,8,320]{2,1,0:T(8,128)(2,1)S(1)} %get-tuple-element.114), channel_id=1, source_target_pairs={{0,64},{64,0},{1,65},{65,1},{2,66},{66,2},{3,67},{67,3},{4,68},{68... | collective-permute-start | bytes 245768 | tf_op jit(solution)/shard_map/ppermute | solution.py:29
  154.2 0.8 copy-start.20

commit v3 on v2

--- a/solution.py
+++ b/solution.py
@@ -17,6 +17,7 @@
 
 VMEM = pltpu.MemorySpace.VMEM
 SMEM = pltpu.MemorySpace.SMEM
+HBM = pltpu.MemorySpace.HBM
 
 
 def noise_table():
@@ -101,23 +102,26 @@
     )(meta, trunc, tmap)
 
 
-def halves_kernel(meta, wv, wg, wo, half):
-    for j, w in enumerate((wv, wg, wo)):
-        half[j] = w[...]
+def halves_kernel(meta, wv, wg, wo, half, sems):
+    start = pl.multiple_of(meta[1] * 160, 16)
+    copies = [
+        pltpu.make_async_copy(w.at[pl.ds(start, 160), :], half.at[j], sems.at[j])
+        for j, w in enumerate((wv, wg, wo))
+    ]
+    for copy in copies:
+        copy.start()
+    for copy in copies:
+        copy.wait()
 
 
 def halves(meta, wv, wg, wo):
-    mine = pl.BlockSpec((160, 640), lambda i, meta: (meta[1], 0))
     return pl.pallas_call(
         halves_kernel,
-        grid_spec=pltpu.PrefetchScalarGridSpec(
-            num_scalar_prefetch=1,
-            grid=(1,),
-            in_specs=[mine] * 3,
-            out_specs=pl.BlockSpec((3, 160, 640), lambda i, meta: (0, 0, 0)),
-        ),
         out_shape=jax.ShapeDtypeStruct((3, 160, 640), BF),
-        compiler_params=grant(6),
+        in_specs=smem(1) + [pl.BlockSpec(memory_space=HBM)] * 3,
+        out_specs=vmem(1)[0],
+        scratch_shapes=[pltpu.SemaphoreType.DMA((3,))],
+        compiler_params=grant(4),
         name="halves",
     )(meta, wv, wg, wo)
 
@@ -183,33 +187,51 @@
     return out
 
 
-def near_kernel(meta, own, other, wv, wg, wo, below, below2, above, above2,
-                dn, acts, rows, turned, w):
+CHUNKS = ((0, 256), (256, 256), (512, 256), (768, 192))
+
+
+def near_own_kernel(meta, rows, wv, wg, wo, below, below2, above, above2, dn, acts, w):
     c = meta[1]
     here = pl.multiple_of(c * 160, 16)
     there = pl.multiple_of((1 - c) * 160, 16)
-    for j in range(2):
-        rows[j, :352] = own[j]
-        rows[j, 352:] = other[j]
-        turned[j] = rows[j].T
     for j, ref in enumerate((wv, wg, wo)):
         w[j, :320] = ref[...]
         w[j, pl.ds(320 + here, 160)] = above[j]
         w[j, pl.ds(320 + there, 160)] = above2[j]
         w[j, pl.ds(640 + here, 160)] = below[j]
         w[j, pl.ds(640 + there, 160)] = below2[j]
-    for start, width in ((0, 256), (256, 256), (512, 256), (768, 192)):
+    for start, width in CHUNKS:
         hidden_part(rows, w, acts, start, width)
     dn[...] = dot(acts[0], w[0]) + dot(acts[1], w[1])
 
 
-def near_forward(meta, *arrays):
+def near_own(meta, *arrays):
     return local(
-        near_kernel, 18,
+        near_own_kernel, 12,
+        (((352, 640), F32), ((3, 352, 960), BF), ((3, 960, 640), BF)), arrays, (), (meta,),
+    )
+
+
+def near_other_kernel(own, other, own_dn, own_acts, w, dn, acts, rows, turned, half):
+    for j in range(2):
+        rows[j, :352] = own[j]
+        rows[j, 352:] = other[j]
+        turned[j] = rows[j].T
+    for start, width in CHUNKS:
+        hidden_part(other, w, half, start, width)
+    dn[:352] = own_dn[...]
+    dn[352:] = dot(half[0], w[0]) + dot(half[1], w[1])
+    acts[:, :352] = own_acts[...]
+    acts[:, 352:] = half[...]
+
+
+def near_other(*arrays):
+    return local(
+        near_other_kernel, 14,
         (
             ((704, 640), F32), ((3, 704, 960), BF), ((2, 704, 640), BF), ((2, 640, 704), BF),
         ),
-        arrays, [((3, 960, 640), BF)], (meta,),
+        arrays, [((3, 352, 960), BF)],
     )
 
 
@@ -332,7 +354,7 @@
             jax.ShapeDtypeStruct((16 * PLACES, 32, 640), BF),
         ),
         in_specs=smem(2) + vmem(5),
-        out_specs=(vmem(1)[0], pl.BlockSpec(memory_space=pltpu.MemorySpace.HBM)),
+        out_specs=(vmem(1)[0], pl.BlockSpec(memory_space=HBM)),
         scratch_shapes=[pltpu.SemaphoreType.DMA((11,))],
         compiler_params=grant(10),
         name="finish",
@@ -487,9 +509,8 @@
     second = ring(above2, "y", -1)
     rows2 = rows.reshape(2, 352, 640)
     other = other.reshape(2, 352, 640)
-    near_dn, near_acts, both, turned = near_forward(
-        meta, rows2, other, wv, wg, wo, below, below2, above, above2
-    )
+    own_dn, own_acts, near_w = near_own(meta, rows2, wv, wg, wo, below, below2, above, above2)
+    near_dn, near_acts, both, turned = near_other(rows2, other, own_dn, own_acts, near_w)
     near_mine, near_send = near_grads(meta, turned, near_acts)
     near_got = swap(near_send, "c")
     dn, dn_send, far_acts, tail = far_forward(meta, both, gain, near_dn, first, second)

time: 155 us -> 151 us (0.974)
  the two profiles are of different devices: /device:TPU:6 before, /device:TPU:4 now
where the time goes in v3:
time: 151 us
  waiting for transfers between devices  64.2 us (43%)
  Pallas kernels  38 us (25%)
  starting transfers between devices  34.4 us (23%)
  local copies, waits for them, and re-layouts  12.5 us (8%)
    ppermute x16, waiting for transfers between devices, ring(): return lax.ppermute(x, axis, [(i, (i + step) % 4) for i in range(4)])  46 us
    pallas_call x10, Pallas kernels, local(): pl.pallas_call(kernel, out_shape=tuple((jax.ShapeDtypeStruct(s, d) for s,...  24.4 us
    ppermute x16, starting transfers between devices, ring(): return lax.ppermute(x, axis, [(i, (i + step) % 4) for i in range(4)])  21.2 us
    ppermute x8, waiting for transfers between devices, swap(): return lax.ppermute(x, axis, [(0, 1), (1, 0)])  18.2 us
    unnamed x42, local copies, waits for them, and re-layouts  11.1 us
    all_to_all x1, starting transfers between devices, route(): return lax.all_to_all(packed, DP, 0, 0, tiled=True)  8.63 us
    pallas_call x1, Pallas kernels, index_work(): pl.pallas_call(index_kernel, out_shape=(i11, i11, i11, i11, jax.ShapeDtyp...  5.96 us
    ppermute x8, starting transfers between devices, swap(): return lax.ppermute(x, axis, [(0, 1), (1, 0)])  4.61 us
  transfers between devices with their start and end apart: 25, of which 14 were waited for; matrix products, arithmetic and copies ran while one was open for 1% of the time, Pallas kernels for 23%

profile of v3, /device:TPU:4, one launch (start us, length us, event | category | flops | bytes accessed | tf_op | source)
XLA Modules:
  0.0 150.6 jit_solution(1564458293016590811)
XLA Ops:
  0.7 1.0 copy-done.6
  1.8 1.0 copy-done.8
  2.8 1.0 copy-done.10
  3.8 1.4 halves.1
  5.2 3.1 %collective-permute-start.3 = (bf16[3,160,640]{2,1,0:T(8,128)(2,1)S(1)}, bf16[3,160,640]{2,1,0:T(8,128)(2,1)S(1)}, u32[]{:S(2)}, u32[]{:S(2)}) collective-permute-start(bf16[3,160,640]{2,1,0:T(8,128)(2,1)S(1)} %halves.1), channel_id=1, source_target_pairs={{0,6},{2,0},{4,2},{6,4},{1,7},{3,1},{5,3},{7,5},{8,14},{10,8},{12,... | collective-permute-start | bytes 1843208 | tf_op jit(solution)/shard_map/ppermute | solution.py:34
  8.9 1.0 copy-done.14
  12.0 1.0 prologue.1.grad
  13.0 1.3 collective-permute-start
  14.3 7.1 %collective-permute-done.3.above = bf16[3,160,640]{2,1,0:T(8,128)(2,1)S(1)} collective-permute-done((bf16[3,160,640]{2,1,0:T(8,128)(2,1)S(1)}, bf16[3,160,640]{2,1,0:T(8,128)(2,1)S(1)}, u32[]{:S(2)}, u32[]{:S(2)}) %collective-permute-start.3) | collective-permute-done | bytes 614432 | tf_op jit(solution)/shard_map/ppermute | solution.py:34
  21.4 3.4 %collective-permute-done.1.below = bf16[3,160,640]{2,1,0:T(8,128)(2,1)S(1)} collective-permute-done((bf16[3,160,640]{2,1,0:T(8,128)(2,1)S(1)}, bf16[3,160,640]{2,1,0:T(8,128)(2,1)S(1)}, u32[]{:S(2)}, u32[]{:S(2)}) %collective-permute-start.1) | collective-permute-done | bytes 614432 | tf_op jit(solution)/shard_map/ppermute | solution.py:34
  24.8 3.2 %collective-permute-start.6 = (bf16[3,160,640]{2,1,0:T(8,128)(2,1)S(1)}, bf16[3,160,640]{2,1,0:T(8,128)(2,1)S(1)}, u32[]{:S(2)}, u32[]{:S(2)}) collective-permute-start(bf16[3,160,640]{2,1,0:T(8,128)(2,1)S(1)} %collective-permute-done.4.above2), channel_id=1, source_target_pairs={{0,6},{2,0},{4,2},{6,4},{1,7},{3,1},{5,3},{7,5},{8,14},{10,8},{12,... | collective-permute-start | bytes 1843208 | tf_op jit(solution)/shard_map/ppermute | solution.py:34
  28.0 4.3 %shard_map.137 = (f32[352,640]{1,0:T(8,128)S(1)}, bf16[3,352,960]{2,1,0:T(8,128)(2,1)S(1)}, bf16[3,960,640]{2,1,0:T(8,128)(2,1)S(1)}) custom-call(s32[4]{0:T(128)S(1)} %pad_add_fusion.meta, bf16[2,352,640]{2,1,0:T(8,128)(2,1)S(1)} %bitcast.29, bf16[320,640]{1,0:T(8,128)(2,1)S(1)} %bitcast.32, bf16[320,640]{1,0:T(8,128)(2,1)S(1)} %bitcast.34, ...), custom_call_target="tpu_custom_call" | custom-call | tf_op jit(solution)/shard_map/pallas_call | solution.py:179
  32.3 2.2 %collective-permute-done = bf16[2,11,32,640]{3,2,1,0:T(8,128)(2,1)S(1)} collective-permute-done((bf16[2,11,32,640]{3,2,1,0:T(8,128)(2,1)S(1)}, bf16[2,11,32,640]{3,2,1,0:T(8,128)(2,1)S(1)}, u32[]{:S(2)}, u32[]{:S(2)}) %collective-permute-start) | collective-permute-done | bytes 901152 | tf_op jit(solution)/shard_map/ppermute | solution.py:30
  34.5 3.8 %shard_map.138 = (f32[704,640]{1,0:T(8,128)S(1)}, bf16[3,704,960]{2,1,0:T(8,128)(2,1)S(1)}, bf16[2,704,640]{2,1,0:T(8,128)(2,1)S(1)}, bf16[2,640,704]{2,1,0:T(8,128)(2,1)S(1)}) custom-call(bf16[2,352,640]{2,1,0:T(8,128)(2,1)S(1)} %bitcast.30, bf16[2,352,640]{2,1,0:T(8,128)(2,1)S(1)} %bitcast.37, f32[352,640]{1,0:T(8,128)S(1)} %get-tuple-element.90.own_dn, ...), custom_call_target="tpu_custom_call" | custom-call | tf_op jit(solution)/shard_map/pallas_call | solution.py:179
  38.4 5.6 %shard_map.140 = (bf16[3,3,8,40,320]{4,3,2,1,0:T(8,128)(2,1)S(1)}, bf16[3,3,8,40,320]{4,3,2,1,0:T(8,128)(2,1)}) custom-call(s32[4]{0:T(128)S(1)} %pad_add_fusion.meta, bf16[2,640,704]{2,1,0:T(8,128)(2,1)S(1)} %get-tuple-element.101.turned, bf16[3,704,960]{2,1,0:T(8,128)(2,1)S(1)} %get-tuple-element.102.acts), custom_call_target="tpu_custom_call" | custom-call | tf_op jit(solution)/shard_map/pallas_call | solution.py:179
  44.1 3.6 %shard_map.139 = (f32[352,640]{1,0:T(8,128)S(1)}, bf16[352,640]{1,0:T(8,128)(2,1)S(1)}, bf16[3,704,320]{2,1,0:T(8,128)(2,1)S(1)}, f32[8,320]{1,0:T(8,128)S(1)}) custom-call(s32[4]{0:T(128)S(1)} %pad_add_fusion.meta, bf16[2,704,640]{2,1,0:T(8,128)(2,1)S(1)} %get-tuple-element.93.rows, f32[1,640]{1,0:T(1,128)S(1)} %broadcast_in_dim.54.gain, ...), custom_call_target="tpu_custom_call" | custom-call | tf_op jit(solution)/shard_map/pallas_call | solution.py:179
  47.7 1.5 collective-permute-start.7
  49.2 6.0 %routes.1 = (s32[11]{0:T(128)S(1)}, s32[11]{0:T(128)S(1)}, s32[11]{0:T(128)S(1)}, s32[11]{0:T(128)S(1)}, s32[1]{0:T(128)}) custom-call(s32[4]{0:T(128)S(1)} %pad_add_fusion.meta, s32[16]{0:T(128)S(1)} %copy-done.17, s32[176]{0:T(256)S(1)} %copy-done.19), custom_call_target="tpu_custom_call" | custom-call | tf_op jit(solution)/shard_map/routes/pallas_call | solution.py:94
  55.2 5.6 %collective-permute-done.7 = bf16[352,640]{1,0:T(8,128)(2,1)S(1)} collective-permute-done((bf16[352,640]{1,0:T(8,128)(2,1)S(1)}, bf16[352,640]{1,0:T(8,128)(2,1)S(1)}, u32[]{:S(2)}, u32[]{:S(2)}) %collective-permute-start.7) | collective-permute-done | bytes 450592 | tf_op jit(solution)/shard_map/ppermute | solution.py:30
  60.7 3.8 %finish.1 = (bf16[11,32,640]{2,1,0:T(8,128)(2,1)S(1)}, bf16[48,32,640]{2,1,0:T(8,128)(2,1)S(1)}) custom-call(s32[11]{0:T(128)S(1)} %get-tuple-element.202.dest_g, s32[11]{0:T(128)S(1)} %get-tuple-element.203.dest_r, f32[11,32,640]{2,1,0:T(8,128)S(1)} %bitcast.38, bf16[11,32,640]{2,1,0:T(8,128)(2,1)S(1)} %bitcast.39, bf16[11,32,640]{2,1,0:T(8,128)(2,1)S(1)} %copy-done.5, ...), custom_call_target="tpu_custom_call" | custom-call | tf_op jit(solution)/shard_map/finish/pallas_call | solution.py:350
  64.5 1.3 copy-done.4
  65.8 8.6 %all-to-all-start.1 = ((bf16[48,32,640]{2,1,0:T(8,128)(2,1)}), bf16[48,32,640]{2,1,0:T(8,128)(2,1)S(1)}, u32[]{:S(2)}, u32[]{:S(2)}) async-start(bf16[48,32,640]{2,1,0:T(8,128)(2,1)} %copy-done.4), calls=%async_computation.1 | async-start | bytes 3932160 | tf_op jit(solution)/shard_map/all_to_all | solution.py:476
  74.5 1.5 %copy-done.1 = bf16[2,640,704]{2,1,0:T(8,128)(2,1)S(1)} copy-done((bf16[2,640,704]{2,1,0:T(8,128)(2,1)S(1)}, bf16[2,640,704]{2,1,0:T(8,128)(2,1)}, u32[]{:S(2)}) %copy-start.1) | copy-done | bytes 1802264
  76.0 1.4 copy-done.13
  77.4 2.3 %shard_map.142 = (bf16[25,40,320]{2,1,0:T(8,128)(2,1)S(1)}, bf16[25,40,320]{2,1,0:T(8,128)(2,1)S(1)}) custom-call(s32[4]{0:T(128)S(1)} %pad_add_fusion.meta, bf16[2,640,704]{2,1,0:T(8,128)(2,1)S(1)} %copy-done.1, bf16[3,704,320]{2,1,0:T(8,128)(2,1)S(1)} %copy-done.13, f32[8,320]{1,0:T(8,128)S(1)} %get-tuple-element.109.tail), custom_call_target="tpu_custom_call" | custom-call | tf_op jit(solution)/shard_map/pallas_call | solution.py:179
  79.9 2.1 %collective-permute-done.11.got = bf16[25,40,320]{2,1,0:T(8,128)(2,1)S(1)} collective-permute-done((bf16[25,40,320]{2,1,0:T(8,128)(2,1)S(1)}, bf16[25,40,320]{2,1,0:T(8,128)(2,1)S(1)}, u32[]{:S(2)}, u32[]{:S(2)}) %collective-permute-start.11) | collective-permute-done | bytes 640032 | tf_op jit(solution)/shard_map/ppermute | solution.py:30
  82.6 2.9 %collective-permute-start.14 = (bf16[3,4,40,320]{3,2,1,0:T(8,128)(2,1)S(1)}, bf16[3,4,40,320]{3,2,1,0:T(8,128)(2,1)S(1)}, u32[]{:S(2)}, u32[]{:S(2)}) collective-permute-start(bf16[3,4,40,320]{3,2,1,0:T(8,128)(2,1)S(1)} %get-tuple-element.113), channel_id=1, source_target_pairs={{0,6},{2,0},{4,2},{6,4},{1,7},{3,1},{5,3},{7,5},{8,14},{10,8},{12,... | collective-permute-start | bytes 921608 | tf_op jit(solution)/shard_map/ppermute | solution.py:34
  85.6 2.1 %shard_map.141 = (f32[3,8,40,320]{3,2,1,0:T(8,128)S(1)}, bf16[3,8,40,320]{3,2,1,0:T(8,128)(2,1)S(1)}, bf16[3,8,40,320]{3,2,1,0:T(8,128)(2,1)S(1)}) custom-call(bf16[3,3,8,40,320]{4,3,2,1,0:T(8,128)(2,1)S(1)} %copy-done.3, bf16[3,3,8,40,320]{4,3,2,1,0:T(8,128)(2,1)} %collective-permute-done.8.got), custom_call_target="tpu_custom_call" | custom-call | tf_op jit(solution)/shard_map/pallas_call | solution.py:179
  87.7 1.8 %collective-permute-start.10 = (bf16[3,8,40,320]{3,2,1,0:T(8,128)(2,1)S(1)}, bf16[3,8,40,320]{3,2,1,0:T(8,128)(2,1)S(1)}, u32[]{:S(2)}, u32[]{:S(2)}) collective-permute-start(bf16[3,8,40,320]{3,2,1,0:T(8,128)(2,1)S(1)} %get-tuple-element.107), channel_id=1, source_target_pairs={{0,6},{2,0},{4,2},{6,4},{1,7},{3,1},{5,3},{7,5},{8,14},{10,8},{12,... | collective-permute-start | bytes 1843208 | tf_op jit(solution)/shard_map/ppermute | solution.py:34
  89.8 5.2 %collective-permute-done.12 = bf16[3,4,40,320]{3,2,1,0:T(8,128)(2,1)S(1)} collective-permute-done((bf16[3,4,40,320]{3,2,1,0:T(8,128)(2,1)S(1)}, bf16[3,4,40,320]{3,2,1,0:T(8,128)(2,1)S(1)}, u32[]{:S(2)}, u32[]{:S(2)}) %collective-permute-start.12) | collective-permute-done | bytes 307232 | tf_op jit(solution)/shard_map/ppermute | solution.py:34
  95.0 3.2 %collective-permute-start.15 = (bf16[3,4,40,320]{3,2,1,0:T(8,128)(2,1)S(1)}, bf16[3,4,40,320]{3,2,1,0:T(8,128)(2,1)S(1)}, u32[]{:S(2)}, u32[]{:S(2)}) collective-permute-start(bf16[3,4,40,320]{3,2,1,0:T(8,128)(2,1)S(1)} %collective-permute-done.14), channel_id=1, source_target_pairs={{0,6},{2,0},{4,2},{6,4},{1,7},{3,1},{5,3},{7,5},{8,14},{10,8},{12,... | collective-permute-start | bytes 921608 | tf_op jit(solution)/shard_map/ppermute | solution.py:34
  98.2 1.2 collective-permute-start.16
  99.4 2.5 %collective-permute-done.16 = f32[8,320]{1,0:T(8,128)S(1)} collective-permute-done((f32[8,320]{1,0:T(8,128)S(1)}, f32[8,320]{1,0:T(8,128)S(1)}, u32[]{:S(2)}, u32[]{:S(2)}) %collective-permute-start.16) | collective-permute-done | bytes 10272 | tf_op jit(solution)/shard_map/ppermute | solution.py:30
  101.9 17.4 %collective-permute-done.17.g1 = f32[8,320]{1,0:T(8,128)S(1)} collective-permute-done((f32[8,320]{1,0:T(8,128)S(1)}, f32[8,320]{1,0:T(8,128)S(1)}, u32[]{:S(2)}, u32[]{:S(2)}) %collective-permute-start.17) | collective-permute-done | bytes 10272 | tf_op jit(solution)/shard_map/ppermute | solution.py:34
  119.3 1.1 collective-permute-start.18
  120.5 3.8 %collective-permute-done.18.g2 = f32[8,320]{1,0:T(8,128)S(1)} collective-permute-done((f32[8,320]{1,0:T(8,128)S(1)}, f32[8,320]{1,0:T(8,128)S(1)}, u32[]{:S(2)}, u32[]{:S(2)}) %collective-permute-start.18) | collective-permute-done | bytes 10272 | tf_op jit(solution)/shard_map/ppermute | solution.py:34
  124.2 3.7 %collective-permute-done.19.g3 = f32[8,320]{1,0:T(8,128)S(1)} collective-permute-done((f32[8,320]{1,0:T(8,128)S(1)}, f32[8,320]{1,0:T(8,128)S(1)}, u32[]{:S(2)}, u32[]{:S(2)}) %collective-permute-start.19) | collective-permute-done | bytes 10272 | tf_op jit(solution)/shard_map/ppermute | solution.py:34
  127.9 1.1 shard_map.144
  129.1 1.5 %collective-permute-start.20 = (bf16[2,16,8,320]{3,2,1,0:T(8,128)(2,1)S(1)}, bf16[2,16,8,320]{3,2,1,0:T(8,128)(2,1)S(1)}, u32[]{:S(2)}, u32[]{:S(2)}) collective-permute-start(bf16[2,16,8,320]{3,2,1,0:T(8,128)(2,1)S(1)} %get-tuple-element.116), channel_id=1, source_target_pairs={{0,16},{16,32},{32,48},{48,0},{1,17},{17,33},{33,49},{49,1},{2,18}... | collective-permute-start | bytes 491528 | tf_op jit(solution)/shard_map/ppermute | solution.py:34
  130.6 1.8 %collective-permute-start.21 = (bf16[2,16,8,320]{3,2,1,0:T(8,128)(2,1)S(1)}, bf16[2,16,8,320]{3,2,1,0:T(8,128)(2,1)S(1)}, u32[]{:S(2)}, u32[]{:S(2)}) collective-permute-start(bf16[2,16,8,320]{3,2,1,0:T(8,128)(2,1)S(1)} %get-tuple-element.117), channel_id=1, source_target_pairs={{0,48},{16,0},{32,16},{48,32},{1,49},{17,1},{33,17},{49,33},{2,50}... | collective-permute-start | bytes 491528 | tf_op jit(solution)/shard_map/ppermute | solution.py:34
  132.4 1.8 %collective-permute-start.22 = (bf16[2,16,8,320]{3,2,1,0:T(8,128)(2,1)S(1)}, bf16[2,16,8,320]{3,2,1,0:T(8,128)(2,1)S(1)}, u32[]{:S(2)}, u32[]{:S(2)}) collective-permute-start(bf16[2,16,8,320]{3,2,1,0:T(8,128)(2,1)S(1)} %get-tuple-element.118), channel_id=1, source_target_pairs={{0,32},{16,48},{32,0},{48,16},{1,33},{17,49},{33,1},{49,17},{2,34}... | collective-permute-start | bytes 491528 | tf_op jit(solution)/shard_map/ppermute | solution.py:34
  134.1 2.7 %collective-permute-done.20.down = bf16[2,16,8,320]{3,2,1,0:T(8,128)(2,1)S(1)} collective-permute-done((bf16[2,16,8,320]{3,2,1,0:T(8,128)(2,1)S(1)}, bf16[2,16,8,320]{3,2,1,0:T(8,128)(2,1)S(1)}, u32[]{:S(2)}, u32[]{:S(2)}) %collective-permute-start.20) | collective-permute-done | bytes 163872 | tf_op jit(solution)/shard_map/ppermute | solution.py:34
  136.8 0.9 collective-permute-done.21.up
  137.7 1.8 %collective-permute-done.22.far = bf16[2,16,8,320]{3,2,1,0:T(8,128)(2,1)S(1)} collective-permute-done((bf16[2,16,8,320]{3,2,1,0:T(8,128)(2,1)S(1)}, bf16[2,16,8,320]{3,2,1,0:T(8,128)(2,1)S(1)}, u32[]{:S(2)}, u32[]{:S(2)}) %collective-permute-start.22) | collective-permute-done | bytes 163872 | tf_op jit(solution)/shard_map/ppermute | solution.py:34
  139.5 0.7 shard_map.145
  140.7 5.8 %collective-permute-done.23.got = bf16[16,8,320]{2,1,0:T(8,128)(2,1)S(1)} collective-permute-done((bf16[16,8,320]{2,1,0:T(8,128)(2,1)S(1)}, bf16[16,8,320]{2,1,0:T(8,128)(2,1)S(1)}, u32[]{:S(2)}, u32[]{:S(2)}) %collective-permute-start.23) | collective-permute-done | bytes 81952 | tf_op jit(solution)/shard_map/ppermute | solution.py:30
  147.8 1.4 unpack.1
  149.9 0.8 copy-done.20
  (65 shorter events, 6.4 us)
Async XLA Ops:
  0.6 8.3 %copy-start.5 = (bf16[11,32,640]{2,1,0:T(8,128)(2,1)S(1)}, bf16[11,32,640]{2,1,0:T(8,128)(2,1)}, u32[]{:S(2)}) copy-start(bf16[11,32,640]{2,1,0:T(8,128)(2,1)} %lat.3) | copy-start | bytes 1351684
  0.7 1.0 copy-start.6
  1.8 1.0 copy-start.8
  2.8 1.0 copy-start.10
  3.8 24.2 %copy-start.7 = (bf16[640,320]{0,1:T(8,128)(2,1)S(1)}, bf16[640,320]{0,1:T(8,128)(2,1)}, u32[]{:S(2)}) copy-start(bf16[640,320]{0,1:T(8,128)(2,1)} %param.18) | copy-start | bytes 1228804
  3.8 24.2 %copy-start.9 = (bf16[640,320]{0,1:T(8,128)(2,1)S(1)}, bf16[640,320]{0,1:T(8,128)(2,1)}, u32[]{:S(2)}) copy-start(bf16[640,320]{0,1:T(8,128)(2,1)} %param.19) | copy-start | bytes 1228804
  3.8 24.2 %copy-start.11 = (bf16[640,320]{0,1:T(8,128)(2,1)S(1)}, bf16[640,320]{0,1:T(8,128)(2,1)}, u32[]{:S(2)}) copy-start(bf16[640,320]{0,1:T(8,128)(2,1)} %param.20) | copy-start | bytes 1228804
  5.2 16.2 %collective-permute-start.3 = (bf16[3,160,640]{2,1,0:T(8,128)(2,1)S(1)}, bf16[3,160,640]{2,1,0:T(8,128)(2,1)S(1)}, u32[]{:S(2)}, u32[]{:S(2)}) collective-permute-start(bf16[3,160,640]{2,1,0:T(8,128)(2,1)S(1)} %halves.1), channel_id=1, source_target_pairs={{0,6},{2,0},{4,2},{6,4},{1,7},{3,1},{5,3},{7,5},{8,14},{10,8},{12,... | collective-permute-start | bytes 1843208 | tf_op jit(solution)/shard_map/ppermute | solution.py:34
  8.2 16.5 %collective-permute-start.1 = (bf16[3,160,640]{2,1,0:T(8,128)(2,1)S(1)}, bf16[3,160,640]{2,1,0:T(8,128)(2,1)S(1)}, u32[]{:S(2)}, u32[]{:S(2)}) collective-permute-start(bf16[3,160,640]{2,1,0:T(8,128)(2,1)S(1)} %halves.1), channel_id=1, source_target_pairs={{0,2},{2,4},{4,6},{6,0},{1,3},{3,5},{5,7},{7,1},{8,10},{10,12},{12... | collective-permute-start | bytes 1843208 | tf_op jit(solution)/shard_map/ppermute | solution.py:34
  8.9 1.0 copy-start.14
  9.9 0.7 copy-start.15
  10.6 0.7 copy-start.16
  11.3 0.7 copy-start.18
  13.0 21.5 %collective-permute-start = (bf16[2,11,32,640]{3,2,1,0:T(8,128)(2,1)S(1)}, bf16[2,11,32,640]{3,2,1,0:T(8,128)(2,1)S(1)}, u32[]{:S(2)}, u32[]{:S(2)}) collective-permute-start(bf16[2,11,32,640]{3,2,1,0:T(8,128)(2,1)S(1)} %prologue.1.grad), channel_id=1, source_target_pairs={{0,1},{1,0},{2,3},{3,2},{4,5},{5,4},{6,7},{7,6},{8,9},{9,8},{10,11... | collective-permute-start | bytes 2703368 | tf_op jit(solution)/shard_map/ppermute | solution.py:30
  21.4 3.4 %collective-permute-start.4 = (bf16[3,160,640]{2,1,0:T(8,128)(2,1)S(1)}, bf16[3,160,640]{2,1,0:T(8,128)(2,1)S(1)}, u32[]{:S(2)}, u32[]{:S(2)}) collective-permute-start(bf16[3,160,640]{2,1,0:T(8,128)(2,1)S(1)} %collective-permute-done.3.above), channel_id=1, source_target_pairs={{0,8},{8,0},{1,9},{9,1},{2,10},{10,2},{3,11},{11,3},{4,12},{12,4},... | collective-permute-start | bytes 1843208 | tf_op jit(solution)/shard_map/ppermute | solution.py:30
  24.8 3.2 %collective-permute-start.2 = (bf16[3,160,640]{2,1,0:T(8,128)(2,1)S(1)}, bf16[3,160,640]{2,1,0:T(8,128)(2,1)S(1)}, u32[]{:S(2)}, u32[]{:S(2)}) collective-permute-start(bf16[3,160,640]{2,1,0:T(8,128)(2,1)S(1)} %collective-permute-done.1.below), channel_id=1, source_target_pairs={{0,8},{8,0},{1,9},{9,1},{2,10},{10,2},{3,11},{11,3},{4,12},{12,4},... | collective-permute-start | bytes 1843208 | tf_op jit(solution)/shard_map/ppermute | solution.py:30
  24.8 19.3 %collective-permute-start.5 = (bf16[3,160,640]{2,1,0:T(8,128)(2,1)S(1)}, bf16[3,160,640]{2,1,0:T(8,128)(2,1)S(1)}, u32[]{:S(2)}, u32[]{:S(2)}) collective-permute-start(bf16[3,160,640]{2,1,0:T(8,128)(2,1)S(1)} %collective-permute-done.1.below), channel_id=1, source_target_pairs={{0,2},{2,4},{4,6},{6,0},{1,3},{3,5},{5,7},{7,1},{8,10},{10,12},{12... | collective-permute-start | bytes 1843208 | tf_op jit(solution)/shard_map/ppermute | solution.py:34
  24.8 19.3 %collective-permute-start.6 = (bf16[3,160,640]{2,1,0:T(8,128)(2,1)S(1)}, bf16[3,160,640]{2,1,0:T(8,128)(2,1)S(1)}, u32[]{:S(2)}, u32[]{:S(2)}) collective-permute-start(bf16[3,160,640]{2,1,0:T(8,128)(2,1)S(1)} %collective-permute-done.4.above2), channel_id=1, source_target_pairs={{0,6},{2,0},{4,2},{6,4},{1,7},{3,1},{5,3},{7,5},{8,14},{10,8},{12,... | collective-permute-start | bytes 1843208 | tf_op jit(solution)/shard_map/ppermute | solution.py:34
  38.4 5.7 %copy-start = (bf16[2,640,704]{2,1,0:T(8,128)(2,1)}, bf16[2,640,704]{2,1,0:T(8,128)(2,1)S(1)}, u32[]{:S(2)}) copy-start(bf16[2,640,704]{2,1,0:T(8,128)(2,1)S(1)} %get-tuple-element.101.turned) | copy-start | bytes 5406724
  44.0 3.7 %copy-start.2 = (bf16[3,3,8,40,320]{4,3,2,1,0:T(8,128)(2,1)}, bf16[3,3,8,40,320]{4,3,2,1,0:T(8,128)(2,1)S(1)}, u32[]{:S(2)}) copy-start(bf16[3,3,8,40,320]{4,3,2,1,0:T(8,128)(2,1)S(1)} %get-tuple-element.103.mine) | copy-start | bytes 5529604
  44.0 41.5 %collective-permute-start.8 = (bf16[3,3,8,40,320]{4,3,2,1,0:T(8,128)(2,1)}, bf16[3,3,8,40,320]{4,3,2,1,0:T(8,128)(2,1)}, u32[]{:S(2)}, u32[]{:S(2)}) collective-permute-start(bf16[3,3,8,40,320]{4,3,2,1,0:T(8,128)(2,1)} %get-tuple-element.104), channel_id=1, source_target_pairs={{0,8},{8,0},{1,9},{9,1},{2,10},{10,2},{3,11},{11,3},{4,12},{12,4},... | collective-permute-start | bytes 5529608 | tf_op jit(solution)/shard_map/ppermute | solution.py:30
  44.1 5.1 %copy-start.17 = (s32[16]{0:T(128)S(1)}, s32[16]{0:T(128)}, u32[]{:S(2)}) copy-start(s32[16]{0:T(128)} %trunc.3) | copy-start | bytes 196
  44.1 5.1 %copy-start.19 = (s32[176]{0:T(256)S(1)}, s32[176]{0:T(256)}, u32[]{:S(2)}) copy-start(s32[176]{0:T(256)} %tmap.1) | copy-start | bytes 2116
  47.7 16.9 %copy-start.12 = (bf16[3,704,320]{2,1,0:T(8,128)(2,1)}, bf16[3,704,320]{2,1,0:T(8,128)(2,1)S(1)}, u32[]{:S(2)}) copy-start(bf16[3,704,320]{2,1,0:T(8,128)(2,1)S(1)} %get-tuple-element.108.acts) | copy-start | bytes 4055044
  47.7 13.0 %collective-permute-start.7 = (bf16[352,640]{1,0:T(8,128)(2,1)S(1)}, bf16[352,640]{1,0:T(8,128)(2,1)S(1)}, u32[]{:S(2)}, u32[]{:S(2)}) collective-permute-start(bf16[352,640]{1,0:T(8,128)(2,1)S(1)} %get-tuple-element.96), channel_id=1, source_target_pairs={{0,1},{1,0},{2,3},{3,2},{4,5},{5,4},{6,7},{7,6},{8,9},{9,8},{10,11... | collective-permute-start | bytes 1351688 | tf_op jit(solution)/shard_map/ppermute | solution.py:30
  64.5 1.3 copy-start.4
  65.8 82.0 %all-to-all-start.1 = ((bf16[48,32,640]{2,1,0:T(8,128)(2,1)}), bf16[48,32,640]{2,1,0:T(8,128)(2,1)S(1)}, u32[]{:S(2)}, u32[]{:S(2)}) async-start(bf16[48,32,640]{2,1,0:T(8,128)(2,1)} %copy-done.4), calls=%async_computation.1 | async-start | bytes 3932160 | tf_op jit(solution)/shard_map/all_to_all | solution.py:476
  74.4 1.5 %copy-start.1 = (bf16[2,640,704]{2,1,0:T(8,128)(2,1)S(1)}, bf16[2,640,704]{2,1,0:T(8,128)(2,1)}, u32[]{:S(2)}) copy-start(bf16[2,640,704]{2,1,0:T(8,128)(2,1)} %copy-done) | copy-start | bytes 5406724
  76.0 1.4 copy-start.13
  77.4 8.2 %copy-start.3 = (bf16[3,3,8,40,320]{4,3,2,1,0:T(8,128)(2,1)S(1)}, bf16[3,3,8,40,320]{4,3,2,1,0:T(8,128)(2,1)}, u32[]{:S(2)}) copy-start(bf16[3,3,8,40,320]{4,3,2,1,0:T(8,128)(2,1)} %copy-done.2) | copy-start | bytes 5529604
  79.7 2.3 %collective-permute-start.11 = (bf16[25,40,320]{2,1,0:T(8,128)(2,1)S(1)}, bf16[25,40,320]{2,1,0:T(8,128)(2,1)S(1)}, u32[]{:S(2)}, u32[]{:S(2)}) collective-permute-start(bf16[25,40,320]{2,1,0:T(8,128)(2,1)S(1)} %get-tuple-element.111), channel_id=1, source_target_pairs={{0,8},{8,0},{1,9},{9,1},{2,10},{10,2},{3,11},{11,3},{4,12},{12,4},... | collective-permute-start | bytes 1920008 | tf_op jit(solution)/shard_map/ppermute | solution.py:30
  82.3 12.7 %collective-permute-start.12 = (bf16[3,4,40,320]{3,2,1,0:T(8,128)(2,1)S(1)}, bf16[3,4,40,320]{3,2,1,0:T(8,128)(2,1)S(1)}, u32[]{:S(2)}, u32[]{:S(2)}) collective-permute-start(bf16[3,4,40,320]{3,2,1,0:T(8,128)(2,1)S(1)} %get-tuple-element.112), channel_id=1, source_target_pairs={{0,2},{2,4},{4,6},{6,0},{1,3},{3,5},{5,7},{7,1},{8,10},{10,12},{12... | collective-permute-start | bytes 921608 | tf_op jit(solution)/shard_map/ppermute | solution.py:34
  82.6 12.4 %collective-permute-start.14 = (bf16[3,4,40,320]{3,2,1,0:T(8,128)(2,1)S(1)}, bf16[3,4,40,320]{3,2,1,0:T(8,128)(2,1)S(1)}, u32[]{:S(2)}, u32[]{:S(2)}) collective-permute-start(bf16[3,4,40,320]{3,2,1,0:T(8,128)(2,1)S(1)} %get-tuple-element.113), channel_id=1, source_target_pairs={{0,6},{2,0},{4,2},{6,4},{1,7},{3,1},{5,3},{7,5},{8,14},{10,8},{12,... | collective-permute-start | bytes 921608 | tf_op jit(solution)/shard_map/ppermute | solution.py:34
  87.7 40.2 %collective-permute-start.10 = (bf16[3,8,40,320]{3,2,1,0:T(8,128)(2,1)S(1)}, bf16[3,8,40,320]{3,2,1,0:T(8,128)(2,1)S(1)}, u32[]{:S(2)}, u32[]{:S(2)}) collective-permute-start(bf16[3,8,40,320]{3,2,1,0:T(8,128)(2,1)S(1)} %get-tuple-element.107), channel_id=1, source_target_pairs={{0,6},{2,0},{4,2},{6,4},{1,7},{3,1},{5,3},{7,5},{8,14},{10,8},{12,... | collective-permute-start | bytes 1843208 | tf_op jit(solution)/shard_map/ppermute | solution.py:34
  89.5 38.4 %collective-permute-start.9 = (bf16[3,8,40,320]{3,2,1,0:T(8,128)(2,1)S(1)}, bf16[3,8,40,320]{3,2,1,0:T(8,128)(2,1)S(1)}, u32[]{:S(2)}, u32[]{:S(2)}) collective-permute-start(bf16[3,8,40,320]{3,2,1,0:T(8,128)(2,1)S(1)} %get-tuple-element.106), channel_id=1, source_target_pairs={{0,2},{2,4},{4,6},{6,0},{1,3},{3,5},{5,7},{7,1},{8,10},{10,12},{12... | collective-permute-start | bytes 1843208 | tf_op jit(solution)/shard_map/ppermute | solution.py:34
  95.0 32.9 %collective-permute-start.13 = (bf16[3,4,40,320]{3,2,1,0:T(8,128)(2,1)S(1)}, bf16[3,4,40,320]{3,2,1,0:T(8,128)(2,1)S(1)}, u32[]{:S(2)}, u32[]{:S(2)}) collective-permute-start(bf16[3,4,40,320]{3,2,1,0:T(8,128)(2,1)S(1)} %collective-permute-done.12), channel_id=1, source_target_pairs={{0,2},{2,4},{4,6},{6,0},{1,3},{3,5},{5,7},{7,1},{8,10},{10,12},{12... | collective-permute-start | bytes 921608 | tf_op jit(solution)/shard_map/ppermute | solution.py:34
  95.0 32.9 %collective-permute-start.15 = (bf16[3,4,40,320]{3,2,1,0:T(8,128)(2,1)S(1)}, bf16[3,4,40,320]{3,2,1,0:T(8,128)(2,1)S(1)}, u32[]{:S(2)}, u32[]{:S(2)}) collective-permute-start(bf16[3,4,40,320]{3,2,1,0:T(8,128)(2,1)S(1)} %collective-permute-done.14), channel_id=1, source_target_pairs={{0,6},{2,0},{4,2},{6,4},{1,7},{3,1},{5,3},{7,5},{8,14},{10,8},{12,... | collective-permute-start | bytes 921608 | tf_op jit(solution)/shard_map/ppermute | solution.py:34
  98.2 3.7 %collective-permute-start.16 = (f32[8,320]{1,0:T(8,128)S(1)}, f32[8,320]{1,0:T(8,128)S(1)}, u32[]{:S(2)}, u32[]{:S(2)}) collective-permute-start(f32[8,320]{1,0:T(8,128)S(1)} %get-tuple-element.114), channel_id=1, source_target_pairs={{0,1},{1,0},{2,3},{3,2},{4,5},{5,4},{6,7},{7,6},{8,9},{9,8},{10,11... | collective-permute-start | bytes 30728 | tf_op jit(solution)/shard_map/ppermute | solution.py:30
  101.9 17.4 %collective-permute-start.17 = (f32[8,320]{1,0:T(8,128)S(1)}, f32[8,320]{1,0:T(8,128)S(1)}, u32[]{:S(2)}, u32[]{:S(2)}) collective-permute-start(f32[8,320]{1,0:T(8,128)S(1)} %add.44.g0), channel_id=1, source_target_pairs={{0,4},{2,6},{4,0},{6,2},{1,5},{3,7},{5,1},{7,3},{8,12},{10,14},{12... | collective-permute-start | bytes 30728 | tf_op jit(solution)/shard_map/ppermute | solution.py:34
  119.3 4.9 %collective-permute-start.18 = (f32[8,320]{1,0:T(8,128)S(1)}, f32[8,320]{1,0:T(8,128)S(1)}, u32[]{:S(2)}, u32[]{:S(2)}) collective-permute-start(f32[8,320]{1,0:T(8,128)S(1)} %add.44.g0), channel_id=1, source_target_pairs={{0,2},{2,4},{4,6},{6,0},{1,3},{3,5},{5,7},{7,1},{8,10},{10,12},{12... | collective-permute-start | bytes 30728 | tf_op jit(solution)/shard_map/ppermute | solution.py:34
  124.2 3.7 %collective-permute-start.19 = (f32[8,320]{1,0:T(8,128)S(1)}, f32[8,320]{1,0:T(8,128)S(1)}, u32[]{:S(2)}, u32[]{:S(2)}) collective-permute-start(f32[8,320]{1,0:T(8,128)S(1)} %add.44.g0), channel_id=1, source_target_pairs={{0,6},{2,0},{4,2},{6,4},{1,7},{3,1},{5,3},{7,5},{8,14},{10,8},{12,... | collective-permute-start | bytes 30728 | tf_op jit(solution)/shard_map/ppermute | solution.py:34
  129.1 7.8 %collective-permute-start.20 = (bf16[2,16,8,320]{3,2,1,0:T(8,128)(2,1)S(1)}, bf16[2,16,8,320]{3,2,1,0:T(8,128)(2,1)S(1)}, u32[]{:S(2)}, u32[]{:S(2)}) collective-permute-start(bf16[2,16,8,320]{3,2,1,0:T(8,128)(2,1)S(1)} %get-tuple-element.116), channel_id=1, source_target_pairs={{0,16},{16,32},{32,48},{48,0},{1,17},{17,33},{33,49},{49,1},{2,18}... | collective-permute-start | bytes 491528 | tf_op jit(solution)/shard_map/ppermute | solution.py:34
  130.6 7.1 %collective-permute-start.21 = (bf16[2,16,8,320]{3,2,1,0:T(8,128)(2,1)S(1)}, bf16[2,16,8,320]{3,2,1,0:T(8,128)(2,1)S(1)}, u32[]{:S(2)}, u32[]{:S(2)}) collective-permute-start(bf16[2,16,8,320]{3,2,1,0:T(8,128)(2,1)S(1)} %get-tuple-element.117), channel_id=1, source_target_pairs={{0,48},{16,0},{32,16},{48,32},{1,49},{17,1},{33,17},{49,33},{2,50}... | collective-permute-start | bytes 491528 | tf_op jit(solution)/shard_map/ppermute | solution.py:34
  132.4 7.2 %collective-permute-start.22 = (bf16[2,16,8,320]{3,2,1,0:T(8,128)(2,1)S(1)}, bf16[2,16,8,320]{3,2,1,0:T(8,128)(2,1)S(1)}, u32[]{:S(2)}, u32[]{:S(2)}) collective-permute-start(bf16[2,16,8,320]{3,2,1,0:T(8,128)(2,1)S(1)} %get-tuple-element.118), channel_id=1, source_target_pairs={{0,32},{16,48},{32,0},{48,16},{1,33},{17,49},{33,1},{49,17},{2,34}... | collective-permute-start | bytes 491528 | tf_op jit(solution)/shard_map/ppermute | solution.py:34
  140.2 6.2 %collective-permute-start.23 = (bf16[16,8,320]{2,1,0:T(8,128)(2,1)S(1)}, bf16[16,8,320]{2,1,0:T(8,128)(2,1)S(1)}, u32[]{:S(2)}, u32[]{:S(2)}) collective-permute-start(bf16[16,8,320]{2,1,0:T(8,128)(2,1)S(1)} %get-tuple-element.120), channel_id=1, source_target_pairs={{0,64},{64,0},{1,65},{65,1},{2,66},{66,2},{3,67},{67,3},{4,68},{68... | collective-permute-start | bytes 245768 | tf_op jit(solution)/shard_map/ppermute | solution.py:30
  149.9 0.8 copy-start.20

commit v4 on v3

--- a/solution.py
+++ b/solution.py
@@ -102,28 +102,8 @@
     )(meta, trunc, tmap)
 
 
-def halves_kernel(meta, wv, wg, wo, half, sems):
-    start = pl.multiple_of(meta[1] * 160, 16)
-    copies = [
-        pltpu.make_async_copy(w.at[pl.ds(start, 160), :], half.at[j], sems.at[j])
-        for j, w in enumerate((wv, wg, wo))
-    ]
-    for copy in copies:
-        copy.start()
-    for copy in copies:
-        copy.wait()
-
-
-def halves(meta, wv, wg, wo):
-    return pl.pallas_call(
-        halves_kernel,
-        out_shape=jax.ShapeDtypeStruct((3, 160, 640), BF),
-        in_specs=smem(1) + [pl.BlockSpec(memory_space=HBM)] * 3,
-        out_specs=vmem(1)[0],
-        scratch_shapes=[pltpu.SemaphoreType.DMA((3,))],
-        compiler_params=grant(4),
-        name="halves",
-    )(meta, wv, wg, wo)
+def halves(c, *weights):
+    return jnp.stack([lax.dynamic_slice_in_dim(w, c * 160, 160, 0) for w in weights])
 
 
 def normalise(tile):
@@ -398,33 +378,40 @@
     down[...] = (mine[2].astype(F32) + got[2].astype(F32)).astype(BF)
 
 
-def far_sums_kernel(mine, got, lower, upper, tail):
+def spread(parts, z, outs):
+    for out, step in zip(outs, (0, 1, 3, 2)):
+        out[...] = parts[:, lax.rem(z + step, 4)].astype(out.dtype)
+
+
+def far_sums_kernel(meta, mine, got, keep, up, down, far, tail, parts):
     for j in range(3):
-        for out, at in ((lower, 8 * j), (upper, 8 * j + 4)):
-            out[j] = (mine[at : at + 4].astype(F32) + got[at : at + 4].astype(F32)).astype(BF)
+        x = mine[8 * j : 8 * j + 8].astype(F32) + got[8 * j : 8 * j + 8].astype(F32)
+        parts[:, :, 5 * j : 5 * j + 5] = x.reshape(2, 4, 5, 8, 320)
+    parts[:, :, 15] = jnp.zeros((2, 4, 8, 320), F32)
+    spread(parts, meta[2], (keep, up, down, far))
     tail[...] = joined(mine[24, :8]) + joined(got[24, :8])
 
 
-def over_y_kernel(meta, own, from_down, from_up, far_lower, far_upper, g0, g1, g2, g3,
-                  keep, up, down, far, parts):
+def far_z_kernel(own, down, up, far, out):
+    x = (own[...] + far[...].astype(F32)) + (down[...].astype(F32) + up[...].astype(F32))
+    out[...] = x.astype(BF)
+
+
+def over_y_kernel(meta, own, from_down, from_up, g0, g1, g2, g3, keep, up, down, far, parts):
     for j in range(3):
-        for half, came in ((0, far_lower), (4, far_upper)):
-            at = slice(half, half + 4)
-            x = own[j, at] + from_down[j, at].astype(F32)
-            x = x + (from_up[j, at].astype(F32) + came[j].astype(F32))
-            parts[half // 4, :, 5 * j : 5 * j + 5] = x.reshape(4, 5, 8, 320)
+        x = own[j] + from_down[j].astype(F32) + from_up[j].astype(F32)
+        parts[:, :, 5 * j : 5 * j + 5] = x.reshape(2, 4, 5, 8, 320)
     tail = resplit((g0[...] + g1[...]) + (g2[...] + g3[...]))
     for k in range(2):
         for z in range(4):
             parts[k, z, 15] = tail
-    z = meta[2]
-    for out, step in ((keep, 0), (up, 1), (down, 3), (far, 2)):
-        out[...] = parts[:, lax.rem(z + step, 4)].astype(out.dtype)
-
-
-def over_z_kernel(meta, own, down, up, far, keep, give, sums):
+    spread(parts, meta[2], (keep, up, down, far))
+
+
+def over_z_kernel(meta, own, down, up, far, across, keep, give, sums):
     sums[...] = (own[...] + far[...].astype(F32)) + (down[...].astype(F32) + up[...].astype(F32))
     for k in range(2):
+        sums[k, :15] += across[k, :15].astype(F32)
         sums[k, 15] = resplit(joined(sums[k, 15]))
     keep[...] = sums[meta[3]]
     give[...] = sums[1 - meta[3]].astype(BF)
@@ -437,33 +424,34 @@
     tail[...] = joined(total[15])
 
 
+def over_ring(up, down, far):
+    return ring(up, "z", 1), ring(down, "z", -1), ring(far, "z", 2)
+
+
 def reduce_weights(meta, near_mine, near_got, far_mine, far_got):
     grads = (3, 8, 40, 320)
-    half = (3, 4, 40, 320)
     row = ((8, 320), F32)
+    part = (2, 16, 8, 320)
+    parts = ((part, F32), (part, BF), (part, BF), (part, BF))
+    whole = [((2, 4, 16, 8, 320), F32)]
     own, up, down = local(
         near_sums_kernel, 4, ((grads, F32), (grads, BF), (grads, BF)),
         (near_mine, near_got),
     )
     from_down = ring(up, "y", 1)
     from_up = ring(down, "y", -1)
-    lower, upper, tail = local(
-        far_sums_kernel, 4, ((half, BF), (half, BF), row), (far_mine, far_got)
-    )
-    lower = ring(lower, "y", 1)
-    upper = ring(upper, "y", -1)
-    lower = ring(lower, "y", 1)
-    upper = ring(upper, "y", -1)
+    far_own, *far_sent, tail = local(
+        far_sums_kernel, 6, (*parts, row), (far_mine, far_got), whole, (meta,)
+    )
     tail = tail + swap(tail, "xl")
+    came = over_ring(*far_sent)
+    (across,) = local(far_z_kernel, 3, ((part, BF),), (far_own, *came))
+    across = ring(across, "y", 2)
     tails = [tail] + [ring(tail, "y", d) for d in (2, 1, -1)]
-    part = (2, 16, 8, 320)
-    own, up, down, far = local(
-        over_y_kernel, 6, ((part, F32), (part, BF), (part, BF), (part, BF)),
-        (own, from_down, from_up, lower, upper, *tails), [((2, 4, 16, 8, 320), F32)], (meta,),
-    )
-    came = ring(up, "z", 1), ring(down, "z", -1), ring(far, "z", 2)
+    own, *sent = local(over_y_kernel, 6, parts, (own, from_down, from_up, *tails), whole, (meta,))
+    came = over_ring(*sent)
     keep, give = local(
-        over_z_kernel, 4, ((part[1:], F32), (part[1:], BF)), (own, *came),
+        over_z_kernel, 4, ((part[1:], F32), (part[1:], BF)), (own, *came, across),
         [(part, F32)], (meta,),
     )
     got = swap(give, "xh")
@@ -497,7 +485,7 @@
     meta = jnp.stack([lax.axis_index(a) for a in (DP, "c", "z", "xh")]).astype(jnp.int32)
     gain = gain[None, :]
     wv, wg, wo = w_value.T, w_gate.T, w_out.T
-    half = halves(meta, wv, wg, wo)
+    half = halves(lax.axis_index("c"), wv, wg, wo)
     below = ring(half, "y", 1)
     above = ring(half, "y", -1)
     rows = prologue(meta, trunc, times, noise_table(), latents, cotangent, gain)

time: 151 us -> 135 us (0.89)
  the two profiles are of different devices: /device:TPU:4 before, /device:TPU:28 now
where the time goes in v4:
time: 135 us
  waiting for transfers between devices  50.1 us (37%)
  Pallas kernels  37.3 us (28%)
  starting transfers between devices  37.1 us (27%)
  local copies, waits for them, and re-layouts  7.92 us (6%)
    ppermute x16, waiting for transfers between devices, ring(): return lax.ppermute(x, axis, [(i, (i + step) % 4) for i in range(4)])  30.4 us
    pallas_call x11, Pallas kernels, local(): pl.pallas_call(kernel, out_shape=tuple((jax.ShapeDtypeStruct(s, d) for s,...  25.1 us
    ppermute x16, starting transfers between devices, ring(): return lax.ppermute(x, axis, [(i, (i + step) % 4) for i in range(4)])  23.2 us
    ppermute x8, waiting for transfers between devices, swap(): return lax.ppermute(x, axis, [(0, 1), (1, 0)])  19.8 us
    all_to_all x1, starting transfers between devices, route(): return lax.all_to_all(packed, DP, 0, 0, tiled=True)  8.64 us
    pallas_call x1, Pallas kernels, index_work(): pl.pallas_call(index_kernel, out_shape=(i11, i11, i11, i11, jax.ShapeDtyp...  5.96 us
    ppermute x8, starting transfers between devices, swap(): return lax.ppermute(x, axis, [(0, 1), (1, 0)])  5.32 us
    unnamed x36, local copies, waits for them, and re-layouts  5.05 us
  transfers between devices with their start and end apart: 25, of which 14 were waited for; matrix products, arithmetic and copies ran while one was open for 1% of the time, Pallas kernels for 27%

profile of v4, /device:TPU:28, one launch (start us, length us, event | category | flops | bytes accessed | tf_op | source)
XLA Modules:
  0.0 135.0 jit_solution(12475767480630513881)
XLA Ops:
  0.7 1.0 dynamic-slice_bitcast_fusion.2
  1.8 1.2 dynamic-slice_bitcast_fusion
  2.9 0.9 pad_maximum_fusion
  3.9 0.7 collective-permute-start.3
  4.6 2.5 %collective-permute-start.1 = (bf16[3,160,640]{2,1,0:T(8,128)(2,1)}, bf16[3,160,640]{2,1,0:T(8,128)(2,1)S(1)}, u32[]{:S(2)}, u32[]{:S(2)}) collective-permute-start(bf16[3,160,640]{2,1,0:T(8,128)(2,1)} %pad_maximum_fusion), channel_id=1, source_target_pairs={{0,2},{2,4},{4,6},{6,0},{1,3},{3,5},{5,7},{7,1},{8,10},{10,12},{12... | collective-permute-start | bytes 1843208 | tf_op jit(solution)/shard_map/ppermute | solution.py:34
  7.2 1.0 prologue.1.grad
  8.3 1.3 collective-permute-start
  9.5 11.4 %collective-permute-done.3.above = bf16[3,160,640]{2,1,0:T(8,128)(2,1)S(1)} collective-permute-done((bf16[3,160,640]{2,1,0:T(8,128)(2,1)}, bf16[3,160,640]{2,1,0:T(8,128)(2,1)S(1)}, u32[]{:S(2)}, u32[]{:S(2)}) %collective-permute-start.3) | collective-permute-done | bytes 614432 | tf_op jit(solution)/shard_map/ppermute | solution.py:34
  21.4 2.4 %collective-permute-start.5 = (bf16[3,160,640]{2,1,0:T(8,128)(2,1)S(1)}, bf16[3,160,640]{2,1,0:T(8,128)(2,1)S(1)}, u32[]{:S(2)}, u32[]{:S(2)}) collective-permute-start(bf16[3,160,640]{2,1,0:T(8,128)(2,1)S(1)} %collective-permute-done.1.below), channel_id=1, source_target_pairs={{0,2},{2,4},{4,6},{6,0},{1,3},{3,5},{5,7},{7,1},{8,10},{10,12},{12... | collective-permute-start | bytes 1843208 | tf_op jit(solution)/shard_map/ppermute | solution.py:34
  23.9 4.3 %shard_map.137 = (f32[352,640]{1,0:T(8,128)S(1)}, bf16[3,352,960]{2,1,0:T(8,128)(2,1)S(1)}, bf16[3,960,640]{2,1,0:T(8,128)(2,1)S(1)}) custom-call(s32[4]{0:T(128)S(1)} %pad_add_fusion.meta, bf16[2,352,640]{2,1,0:T(8,128)(2,1)S(1)} %bitcast.41, bf16[320,640]{1,0:T(8,128)(2,1)S(1)} %bitcast.43, bf16[320,640]{1,0:T(8,128)(2,1)S(1)} %bitcast.44, ...), custom_call_target="tpu_custom_call" | custom-call | tf_op jit(solution)/shard_map/pallas_call | solution.py:159
  28.2 1.4 %collective-permute-done = bf16[2,11,32,640]{3,2,1,0:T(8,128)(2,1)S(1)} collective-permute-done((bf16[2,11,32,640]{3,2,1,0:T(8,128)(2,1)S(1)}, bf16[2,11,32,640]{3,2,1,0:T(8,128)(2,1)S(1)}, u32[]{:S(2)}, u32[]{:S(2)}) %collective-permute-start) | collective-permute-done | bytes 901152 | tf_op jit(solution)/shard_map/ppermute | solution.py:30
  29.5 3.8 %shard_map.138 = (f32[704,640]{1,0:T(8,128)S(1)}, bf16[3,704,960]{2,1,0:T(8,128)(2,1)S(1)}, bf16[2,704,640]{2,1,0:T(8,128)(2,1)S(1)}, bf16[2,640,704]{2,1,0:T(8,128)(2,1)S(1)}) custom-call(bf16[2,352,640]{2,1,0:T(8,128)(2,1)S(1)} %bitcast.42, bf16[2,352,640]{2,1,0:T(8,128)(2,1)S(1)} %bitcast.46, f32[352,640]{1,0:T(8,128)S(1)} %get-tuple-element.92.own_dn, ...), custom_call_target="tpu_custom_call" | custom-call | tf_op jit(solution)/shard_map/pallas_call | solution.py:159
  33.4 5.7 %shard_map.140 = (bf16[3,3,8,40,320]{4,3,2,1,0:T(8,128)(2,1)S(1)}, bf16[3,3,8,40,320]{4,3,2,1,0:T(8,128)(2,1)}) custom-call(s32[4]{0:T(128)S(1)} %pad_add_fusion.meta, bf16[2,640,704]{2,1,0:T(8,128)(2,1)S(1)} %get-tuple-element.103.turned, bf16[3,704,960]{2,1,0:T(8,128)(2,1)S(1)} %get-tuple-element.104.acts), custom_call_target="tpu_custom_call" | custom-call | tf_op jit(solution)/shard_map/pallas_call | solution.py:159
  39.0 2.0 %collective-permute-done.6.second = bf16[3,160,640]{2,1,0:T(8,128)(2,1)S(1)} collective-permute-done((bf16[3,160,640]{2,1,0:T(8,128)(2,1)S(1)}, bf16[3,160,640]{2,1,0:T(8,128)(2,1)S(1)}, u32[]{:S(2)}, u32[]{:S(2)}) %collective-permute-start.6) | collective-permute-done | bytes 614432 | tf_op jit(solution)/shard_map/ppermute | solution.py:34
  41.1 3.6 %shard_map.139 = (f32[352,640]{1,0:T(8,128)S(1)}, bf16[352,640]{1,0:T(8,128)(2,1)S(1)}, bf16[3,704,320]{2,1,0:T(8,128)(2,1)S(1)}, f32[8,320]{1,0:T(8,128)S(1)}) custom-call(s32[4]{0:T(128)S(1)} %pad_add_fusion.meta, bf16[2,704,640]{2,1,0:T(8,128)(2,1)S(1)} %get-tuple-element.95.rows, f32[1,640]{1,0:T(1,128)S(1)} %broadcast_in_dim.54.gain, ...), custom_call_target="tpu_custom_call" | custom-call | tf_op jit(solution)/shard_map/pallas_call | solution.py:159
  44.7 1.5 %collective-permute-start.7 = (bf16[352,640]{1,0:T(8,128)(2,1)S(1)}, bf16[352,640]{1,0:T(8,128)(2,1)S(1)}, u32[]{:S(2)}, u32[]{:S(2)}) collective-permute-start(bf16[352,640]{1,0:T(8,128)(2,1)S(1)} %get-tuple-element.98), channel_id=1, source_target_pairs={{0,1},{1,0},{2,3},{3,2},{4,5},{5,4},{6,7},{7,6},{8,9},{9,8},{10,11... | collective-permute-start | bytes 1351688 | tf_op jit(solution)/shard_map/ppermute | solution.py:30
  46.2 6.0 %routes.1 = (s32[11]{0:T(128)S(1)}, s32[11]{0:T(128)S(1)}, s32[11]{0:T(128)S(1)}, s32[11]{0:T(128)S(1)}, s32[1]{0:T(128)}) custom-call(s32[4]{0:T(128)S(1)} %pad_add_fusion.meta, s32[16]{0:T(128)S(1)} %copy-done.13, s32[176]{0:T(256)S(1)} %copy-done.15), custom_call_target="tpu_custom_call" | custom-call | tf_op jit(solution)/shard_map/routes/pallas_call | solution.py:94
  52.1 4.4 %collective-permute-done.7 = bf16[352,640]{1,0:T(8,128)(2,1)S(1)} collective-permute-done((bf16[352,640]{1,0:T(8,128)(2,1)S(1)}, bf16[352,640]{1,0:T(8,128)(2,1)S(1)}, u32[]{:S(2)}, u32[]{:S(2)}) %collective-permute-start.7) | collective-permute-done | bytes 450592 | tf_op jit(solution)/shard_map/ppermute | solution.py:30
  56.6 3.8 %finish.1 = (bf16[11,32,640]{2,1,0:T(8,128)(2,1)S(1)}, bf16[48,32,640]{2,1,0:T(8,128)(2,1)S(1)}) custom-call(s32[11]{0:T(128)S(1)} %get-tuple-element.208.dest_g, s32[11]{0:T(128)S(1)} %get-tuple-element.209.dest_r, f32[11,32,640]{2,1,0:T(8,128)S(1)} %bitcast.47, bf16[11,32,640]{2,1,0:T(8,128)(2,1)S(1)} %bitcast.48, bf16[11,32,640]{2,1,0:T(8,128)(2,1)S(1)} %copy-done.5, ...), custom_call_target="tpu_custom_call" | custom-call | tf_op jit(solution)/shard_map/finish/pallas_call | solution.py:330
  60.4 1.3 copy-done.4
  61.7 8.6 %all-to-all-start.1 = ((bf16[48,32,640]{2,1,0:T(8,128)(2,1)}), bf16[48,32,640]{2,1,0:T(8,128)(2,1)S(1)}, u32[]{:S(2)}, u32[]{:S(2)}) async-start(bf16[48,32,640]{2,1,0:T(8,128)(2,1)} %copy-done.4), calls=%async_computation.1 | async-start | bytes 3932160 | tf_op jit(solution)/shard_map/all_to_all | solution.py:464
  70.3 1.5 %copy-done.1 = bf16[2,640,704]{2,1,0:T(8,128)(2,1)S(1)} copy-done((bf16[2,640,704]{2,1,0:T(8,128)(2,1)S(1)}, bf16[2,640,704]{2,1,0:T(8,128)(2,1)}, u32[]{:S(2)}) %copy-start.1) | copy-done | bytes 1802264
  71.8 1.4 %copy-done.7 = bf16[3,704,320]{2,1,0:T(8,128)(2,1)S(1)} copy-done((bf16[3,704,320]{2,1,0:T(8,128)(2,1)S(1)}, bf16[3,704,320]{2,1,0:T(8,128)(2,1)}, u32[]{:S(2)}) %copy-start.7) | copy-done | bytes 1351704
  73.3 2.3 %shard_map.142 = (bf16[25,40,320]{2,1,0:T(8,128)(2,1)S(1)}, bf16[25,40,320]{2,1,0:T(8,128)(2,1)S(1)}) custom-call(s32[4]{0:T(128)S(1)} %pad_add_fusion.meta, bf16[2,640,704]{2,1,0:T(8,128)(2,1)S(1)} %copy-done.1, bf16[3,704,320]{2,1,0:T(8,128)(2,1)S(1)} %copy-done.7, f32[8,320]{1,0:T(8,128)S(1)} %get-tuple-element.111.tail), custom_call_target="tpu_custom_call" | custom-call | tf_op jit(solution)/shard_map/pallas_call | solution.py:159
  75.8 2.1 %shard_map.141 = (f32[3,8,40,320]{3,2,1,0:T(8,128)S(1)}, bf16[3,8,40,320]{3,2,1,0:T(8,128)(2,1)S(1)}, bf16[3,8,40,320]{3,2,1,0:T(8,128)(2,1)S(1)}) custom-call(bf16[3,3,8,40,320]{4,3,2,1,0:T(8,128)(2,1)S(1)} %copy-done.3, bf16[3,3,8,40,320]{4,3,2,1,0:T(8,128)(2,1)} %collective-permute-done.8.got), custom_call_target="tpu_custom_call" | custom-call | tf_op jit(solution)/shard_map/pallas_call | solution.py:159
  78.0 3.2 %collective-permute-start.9 = (bf16[3,8,40,320]{3,2,1,0:T(8,128)(2,1)S(1)}, bf16[3,8,40,320]{3,2,1,0:T(8,128)(2,1)S(1)}, u32[]{:S(2)}, u32[]{:S(2)}) collective-permute-start(bf16[3,8,40,320]{3,2,1,0:T(8,128)(2,1)S(1)} %get-tuple-element.108), channel_id=1, source_target_pairs={{0,2},{2,4},{4,6},{6,0},{1,3},{3,5},{5,7},{7,1},{8,10},{10,12},{12... | collective-permute-start | bytes 1843208 | tf_op jit(solution)/shard_map/ppermute | solution.py:34
  81.2 0.9 shard_map.143
  82.1 1.3 collective-permute-start.12
  83.4 1.5 %collective-permute-start.19 = (bf16[2,16,8,320]{3,2,1,0:T(8,128)(2,1)S(1)}, bf16[2,16,8,320]{3,2,1,0:T(8,128)(2,1)S(1)}, u32[]{:S(2)}, u32[]{:S(2)}) collective-permute-start(bf16[2,16,8,320]{3,2,1,0:T(8,128)(2,1)S(1)} %get-tuple-element.120), channel_id=1, source_target_pairs={{0,16},{16,32},{32,48},{48,0},{1,17},{17,33},{33,49},{49,1},{2,18}... | collective-permute-start | bytes 491528 | tf_op jit(solution)/shard_map/ppermute | solution.py:34
  84.8 1.8 %collective-permute-start.20 = (bf16[2,16,8,320]{3,2,1,0:T(8,128)(2,1)S(1)}, bf16[2,16,8,320]{3,2,1,0:T(8,128)(2,1)S(1)}, u32[]{:S(2)}, u32[]{:S(2)}) collective-permute-start(bf16[2,16,8,320]{3,2,1,0:T(8,128)(2,1)S(1)} %get-tuple-element.121), channel_id=1, source_target_pairs={{0,48},{16,0},{32,16},{48,32},{1,49},{17,1},{33,17},{49,33},{2,50}... | collective-permute-start | bytes 491528 | tf_op jit(solution)/shard_map/ppermute | solution.py:34
  86.6 8.3 %collective-permute-done.12 = f32[8,320]{1,0:T(8,128)S(1)} collective-permute-done((f32[8,320]{1,0:T(8,128)S(1)}, f32[8,320]{1,0:T(8,128)S(1)}, u32[]{:S(2)}, u32[]{:S(2)}) %collective-permute-start.12) | collective-permute-done | bytes 10272 | tf_op jit(solution)/shard_map/ppermute | solution.py:30
  94.9 3.0 %collective-permute-start.21 = (bf16[2,16,8,320]{3,2,1,0:T(8,128)(2,1)S(1)}, bf16[2,16,8,320]{3,2,1,0:T(8,128)(2,1)S(1)}, u32[]{:S(2)}, u32[]{:S(2)}) collective-permute-start(bf16[2,16,8,320]{3,2,1,0:T(8,128)(2,1)S(1)} %get-tuple-element.122), channel_id=1, source_target_pairs={{0,32},{16,48},{32,0},{48,16},{1,33},{17,49},{33,1},{49,17},{2,34}... | collective-permute-start | bytes 491528 | tf_op jit(solution)/shard_map/ppermute | solution.py:34
  97.9 1.5 %collective-permute-done.19.down = bf16[2,16,8,320]{3,2,1,0:T(8,128)(2,1)S(1)} collective-permute-done((bf16[2,16,8,320]{3,2,1,0:T(8,128)(2,1)S(1)}, bf16[2,16,8,320]{3,2,1,0:T(8,128)(2,1)S(1)}, u32[]{:S(2)}, u32[]{:S(2)}) %collective-permute-start.19) | collective-permute-done | bytes 163872 | tf_op jit(solution)/shard_map/ppermute | solution.py:34
  100.0 1.4 %collective-permute-start.14 = (f32[8,320]{1,0:T(8,128)S(1)}, f32[8,320]{1,0:T(8,128)S(1)}, u32[]{:S(2)}, u32[]{:S(2)}) collective-permute-start(f32[8,320]{1,0:T(8,128)S(1)} %add.50.g0), channel_id=1, source_target_pairs={{0,2},{2,4},{4,6},{6,0},{1,3},{3,5},{5,7},{7,1},{8,10},{10,12},{12... | collective-permute-start | bytes 30728 | tf_op jit(solution)/shard_map/ppermute | solution.py:34
  101.4 2.5 %collective-permute-done.21.far = bf16[2,16,8,320]{3,2,1,0:T(8,128)(2,1)S(1)} collective-permute-done((bf16[2,16,8,320]{3,2,1,0:T(8,128)(2,1)S(1)}, bf16[2,16,8,320]{3,2,1,0:T(8,128)(2,1)S(1)}, u32[]{:S(2)}, u32[]{:S(2)}) %collective-permute-start.21) | collective-permute-done | bytes 163872 | tf_op jit(solution)/shard_map/ppermute | solution.py:34
  104.6 2.0 %collective-permute-start.22 = (bf16[2,16,8,320]{3,2,1,0:T(8,128)(2,1)S(1)}, bf16[2,16,8,320]{3,2,1,0:T(8,128)(2,1)S(1)}, u32[]{:S(2)}, u32[]{:S(2)}) collective-permute-start(bf16[2,16,8,320]{3,2,1,0:T(8,128)(2,1)S(1)} %shard_map.145), channel_id=1, source_target_pairs={{0,4},{2,6},{4,0},{6,2},{1,5},{3,7},{5,1},{7,3},{8,12},{10,14},{12... | collective-permute-start | bytes 491528 | tf_op jit(solution)/shard_map/ppermute | solution.py:34
  106.6 5.9 %collective-permute-done.15.g3 = f32[8,320]{1,0:T(8,128)S(1)} collective-permute-done((f32[8,320]{1,0:T(8,128)S(1)}, f32[8,320]{1,0:T(8,128)S(1)}, u32[]{:S(2)}, u32[]{:S(2)}) %collective-permute-start.15) | collective-permute-done | bytes 10272 | tf_op jit(solution)/shard_map/ppermute | solution.py:34
  112.5 1.0 shard_map.144
  113.5 1.5 %collective-permute-start.16 = (bf16[2,16,8,320]{3,2,1,0:T(8,128)(2,1)S(1)}, bf16[2,16,8,320]{3,2,1,0:T(8,128)(2,1)S(1)}, u32[]{:S(2)}, u32[]{:S(2)}) collective-permute-start(bf16[2,16,8,320]{3,2,1,0:T(8,128)(2,1)S(1)} %get-tuple-element.116), channel_id=1, source_target_pairs={{0,16},{16,32},{32,48},{48,0},{1,17},{17,33},{33,49},{49,1},{2,18}... | collective-permute-start | bytes 491528 | tf_op jit(solution)/shard_map/ppermute | solution.py:34
  114.9 1.8 %collective-permute-start.17 = (bf16[2,16,8,320]{3,2,1,0:T(8,128)(2,1)S(1)}, bf16[2,16,8,320]{3,2,1,0:T(8,128)(2,1)S(1)}, u32[]{:S(2)}, u32[]{:S(2)}) collective-permute-start(bf16[2,16,8,320]{3,2,1,0:T(8,128)(2,1)S(1)} %get-tuple-element.117), channel_id=1, source_target_pairs={{0,48},{16,0},{32,16},{48,32},{1,49},{17,1},{33,17},{49,33},{2,50}... | collective-permute-start | bytes 491528 | tf_op jit(solution)/shard_map/ppermute | solution.py:34
  116.8 1.2 collective-permute-start.18
  118.0 2.4 %collective-permute-done.16.down = bf16[2,16,8,320]{3,2,1,0:T(8,128)(2,1)S(1)} collective-permute-done((bf16[2,16,8,320]{3,2,1,0:T(8,128)(2,1)S(1)}, bf16[2,16,8,320]{3,2,1,0:T(8,128)(2,1)S(1)}, u32[]{:S(2)}, u32[]{:S(2)}) %collective-permute-start.16) | collective-permute-done | bytes 163872 | tf_op jit(solution)/shard_map/ppermute | solution.py:34
  120.6 3.3 %collective-permute-done.18.far = bf16[2,16,8,320]{3,2,1,0:T(8,128)(2,1)S(1)} collective-permute-done((bf16[2,16,8,320]{3,2,1,0:T(8,128)(2,1)S(1)}, bf16[2,16,8,320]{3,2,1,0:T(8,128)(2,1)S(1)}, u32[]{:S(2)}, u32[]{:S(2)}) %collective-permute-start.18) | collective-permute-done | bytes 163872 | tf_op jit(solution)/shard_map/ppermute | solution.py:34
  123.9 0.7 shard_map.146
  125.2 5.6 %collective-permute-done.23.got = bf16[16,8,320]{2,1,0:T(8,128)(2,1)S(1)} collective-permute-done((bf16[16,8,320]{2,1,0:T(8,128)(2,1)S(1)}, bf16[16,8,320]{2,1,0:T(8,128)(2,1)S(1)}, u32[]{:S(2)}, u32[]{:S(2)}) %collective-permute-start.23) | collective-permute-done | bytes 81952 | tf_op jit(solution)/shard_map/ppermute | solution.py:30
  130.9 0.7 shard_map.147
  132.2 1.4 %unpack.1 = bf16[11,32,640]{2,1,0:T(8,128)(2,1)S(1)} custom-call(s32[11]{0:T(128)S(1)} %get-tuple-element.207.src_p, s32[11]{0:T(128)S(1)} %get-tuple-element.206.src_r, bf16[48,32,640]{2,1,0:T(8,128)(2,1)S(1)} %all-to-all-done.1.came), custom_call_target="tpu_custom_call" | custom-call | tf_op jit(solution)/shard_map/unpack/pallas_call | solution.py:364
  134.3 0.8 copy-done.16
  (62 shorter events, 4.3 us)
Async XLA Ops:
  0.6 6.6 %copy-start.12 = (f32[1000]{0:T(1024)S(1)}, f32[1000]{0:T(1024)}, u32[]{:S(2)}) copy-start(f32[1000]{0:T(1024)} %constant.62.clone.table) | copy-start | bytes 12004
  0.6 6.5 %copy-start.17 = (f32[640]{0:T(1024)S(1)}, f32[640]{0:T(1024)}, u32[]{:S(2)}) copy-start(f32[640]{0:T(1024)} %param.17) | copy-start | bytes 7684
  0.7 6.5 %copy-start.5 = (bf16[11,32,640]{2,1,0:T(8,128)(2,1)S(1)}, bf16[11,32,640]{2,1,0:T(8,128)(2,1)}, u32[]{:S(2)}) copy-start(bf16[11,32,640]{2,1,0:T(8,128)(2,1)} %lat.3) | copy-start | bytes 1351684
  0.7 6.5 %copy-start.11 = (bf16[11,32,640]{2,1,0:T(8,128)(2,1)S(1)}, bf16[11,32,640]{2,1,0:T(8,128)(2,1)}, u32[]{:S(2)}) copy-start(bf16[11,32,640]{2,1,0:T(8,128)(2,1)} %cot.1) | copy-start | bytes 1351684
  0.7 6.5 %copy-start.13 = (s32[16]{0:T(128)S(1)}, s32[16]{0:T(128)}, u32[]{:S(2)}) copy-start(s32[16]{0:T(128)} %trunc.3) | copy-start | bytes 196
  0.7 6.5 %copy-start.14 = (s32[176]{0:T(256)S(1)}, s32[176]{0:T(256)}, u32[]{:S(2)}) copy-start(s32[176]{0:T(256)} %times.1) | copy-start | bytes 2116
  1.7 22.1 %copy-start.8 = (bf16[640,320]{0,1:T(8,128)(2,1)S(1)}, bf16[640,320]{0,1:T(8,128)(2,1)}, u32[]{:S(2)}) copy-start(bf16[640,320]{0,1:T(8,128)(2,1)} %param.18) | copy-start | bytes 1228804
  1.7 22.1 %copy-start.9 = (bf16[640,320]{0,1:T(8,128)(2,1)S(1)}, bf16[640,320]{0,1:T(8,128)(2,1)}, u32[]{:S(2)}) copy-start(bf16[640,320]{0,1:T(8,128)(2,1)} %param.19) | copy-start | bytes 1228804
  1.8 22.1 %copy-start.10 = (bf16[640,320]{0,1:T(8,128)(2,1)S(1)}, bf16[640,320]{0,1:T(8,128)(2,1)}, u32[]{:S(2)}) copy-start(bf16[640,320]{0,1:T(8,128)(2,1)} %param.20) | copy-start | bytes 1228804
  3.9 17.0 %collective-permute-start.3 = (bf16[3,160,640]{2,1,0:T(8,128)(2,1)}, bf16[3,160,640]{2,1,0:T(8,128)(2,1)S(1)}, u32[]{:S(2)}, u32[]{:S(2)}) collective-permute-start(bf16[3,160,640]{2,1,0:T(8,128)(2,1)} %pad_maximum_fusion), channel_id=1, source_target_pairs={{0,6},{2,0},{4,2},{6,4},{1,7},{3,1},{5,3},{7,5},{8,14},{10,8},{12,... | collective-permute-start | bytes 1843208 | tf_op jit(solution)/shard_map/ppermute | solution.py:34
  4.6 16.3 %collective-permute-start.1 = (bf16[3,160,640]{2,1,0:T(8,128)(2,1)}, bf16[3,160,640]{2,1,0:T(8,128)(2,1)S(1)}, u32[]{:S(2)}, u32[]{:S(2)}) collective-permute-start(bf16[3,160,640]{2,1,0:T(8,128)(2,1)} %pad_maximum_fusion), channel_id=1, source_target_pairs={{0,2},{2,4},{4,6},{6,0},{1,3},{3,5},{5,7},{7,1},{8,10},{10,12},{12... | collective-permute-start | bytes 1843208 | tf_op jit(solution)/shard_map/ppermute | solution.py:34
  8.3 21.3 %collective-permute-start = (bf16[2,11,32,640]{3,2,1,0:T(8,128)(2,1)S(1)}, bf16[2,11,32,640]{3,2,1,0:T(8,128)(2,1)S(1)}, u32[]{:S(2)}, u32[]{:S(2)}) collective-permute-start(bf16[2,11,32,640]{3,2,1,0:T(8,128)(2,1)S(1)} %prologue.1.grad), channel_id=1, source_target_pairs={{0,1},{1,0},{2,3},{3,2},{4,5},{5,4},{6,7},{7,6},{8,9},{9,8},{10,11... | collective-permute-start | bytes 2703368 | tf_op jit(solution)/shard_map/ppermute | solution.py:30
  20.9 3.0 %collective-permute-start.4 = (bf16[3,160,640]{2,1,0:T(8,128)(2,1)S(1)}, bf16[3,160,640]{2,1,0:T(8,128)(2,1)S(1)}, u32[]{:S(2)}, u32[]{:S(2)}) collective-permute-start(bf16[3,160,640]{2,1,0:T(8,128)(2,1)S(1)} %collective-permute-done.3.above), channel_id=1, source_target_pairs={{0,8},{8,0},{1,9},{9,1},{2,10},{10,2},{3,11},{11,3},{4,12},{12,4},... | collective-permute-start | bytes 1843208 | tf_op jit(solution)/shard_map/ppermute | solution.py:30
  20.9 3.0 %collective-permute-start.2 = (bf16[3,160,640]{2,1,0:T(8,128)(2,1)S(1)}, bf16[3,160,640]{2,1,0:T(8,128)(2,1)S(1)}, u32[]{:S(2)}, u32[]{:S(2)}) collective-permute-start(bf16[3,160,640]{2,1,0:T(8,128)(2,1)S(1)} %collective-permute-done.1.below), channel_id=1, source_target_pairs={{0,8},{8,0},{1,9},{9,1},{2,10},{10,2},{3,11},{11,3},{4,12},{12,4},... | collective-permute-start | bytes 1843208 | tf_op jit(solution)/shard_map/ppermute | solution.py:30
  21.4 17.6 %collective-permute-start.5 = (bf16[3,160,640]{2,1,0:T(8,128)(2,1)S(1)}, bf16[3,160,640]{2,1,0:T(8,128)(2,1)S(1)}, u32[]{:S(2)}, u32[]{:S(2)}) collective-permute-start(bf16[3,160,640]{2,1,0:T(8,128)(2,1)S(1)} %collective-permute-done.1.below), channel_id=1, source_target_pairs={{0,2},{2,4},{4,6},{6,0},{1,3},{3,5},{5,7},{7,1},{8,10},{10,12},{12... | collective-permute-start | bytes 1843208 | tf_op jit(solution)/shard_map/ppermute | solution.py:34
  23.9 17.2 %collective-permute-start.6 = (bf16[3,160,640]{2,1,0:T(8,128)(2,1)S(1)}, bf16[3,160,640]{2,1,0:T(8,128)(2,1)S(1)}, u32[]{:S(2)}, u32[]{:S(2)}) collective-permute-start(bf16[3,160,640]{2,1,0:T(8,128)(2,1)S(1)} %collective-permute-done.4.above2), channel_id=1, source_target_pairs={{0,6},{2,0},{4,2},{6,4},{1,7},{3,1},{5,3},{7,5},{8,14},{10,8},{12,... | collective-permute-start | bytes 1843208 | tf_op jit(solution)/shard_map/ppermute | solution.py:34
  33.3 5.7 %copy-start = (bf16[2,640,704]{2,1,0:T(8,128)(2,1)}, bf16[2,640,704]{2,1,0:T(8,128)(2,1)S(1)}, u32[]{:S(2)}) copy-start(bf16[2,640,704]{2,1,0:T(8,128)(2,1)S(1)} %get-tuple-element.103.turned) | copy-start | bytes 5406724
  39.0 5.6 %copy-start.2 = (bf16[3,3,8,40,320]{4,3,2,1,0:T(8,128)(2,1)}, bf16[3,3,8,40,320]{4,3,2,1,0:T(8,128)(2,1)S(1)}, u32[]{:S(2)}) copy-start(bf16[3,3,8,40,320]{4,3,2,1,0:T(8,128)(2,1)S(1)} %get-tuple-element.105.mine) | copy-start | bytes 5529604
  39.0 36.8 %collective-permute-start.8 = (bf16[3,3,8,40,320]{4,3,2,1,0:T(8,128)(2,1)}, bf16[3,3,8,40,320]{4,3,2,1,0:T(8,128)(2,1)}, u32[]{:S(2)}, u32[]{:S(2)}) collective-permute-start(bf16[3,3,8,40,320]{4,3,2,1,0:T(8,128)(2,1)} %get-tuple-element.106), channel_id=1, source_target_pairs={{0,8},{8,0},{1,9},{9,1},{2,10},{10,2},{3,11},{11,3},{4,12},{12,4},... | collective-permute-start | bytes 5529608 | tf_op jit(solution)/shard_map/ppermute | solution.py:30
  41.1 5.1 %copy-start.15 = (s32[176]{0:T(256)S(1)}, s32[176]{0:T(256)}, u32[]{:S(2)}) copy-start(s32[176]{0:T(256)} %tmap.1) | copy-start | bytes 2116
  44.6 15.7 %copy-start.6 = (bf16[3,704,320]{2,1,0:T(8,128)(2,1)}, bf16[3,704,320]{2,1,0:T(8,128)(2,1)S(1)}, u32[]{:S(2)}) copy-start(bf16[3,704,320]{2,1,0:T(8,128)(2,1)S(1)} %get-tuple-element.110.acts) | copy-start | bytes 4055044
  44.7 11.9 %collective-permute-start.7 = (bf16[352,640]{1,0:T(8,128)(2,1)S(1)}, bf16[352,640]{1,0:T(8,128)(2,1)S(1)}, u32[]{:S(2)}, u32[]{:S(2)}) collective-permute-start(bf16[352,640]{1,0:T(8,128)(2,1)S(1)} %get-tuple-element.98), channel_id=1, source_target_pairs={{0,1},{1,0},{2,3},{3,2},{4,5},{5,4},{6,7},{7,6},{8,9},{9,8},{10,11... | collective-permute-start | bytes 1351688 | tf_op jit(solution)/shard_map/ppermute | solution.py:30
  60.4 1.3 copy-start.4
  61.7 70.6 %all-to-all-start.1 = ((bf16[48,32,640]{2,1,0:T(8,128)(2,1)}), bf16[48,32,640]{2,1,0:T(8,128)(2,1)S(1)}, u32[]{:S(2)}, u32[]{:S(2)}) async-start(bf16[48,32,640]{2,1,0:T(8,128)(2,1)} %copy-done.4), calls=%async_computation.1 | async-start | bytes 3932160 | tf_op jit(solution)/shard_map/all_to_all | solution.py:464
  70.3 1.5 %copy-start.1 = (bf16[2,640,704]{2,1,0:T(8,128)(2,1)S(1)}, bf16[2,640,704]{2,1,0:T(8,128)(2,1)}, u32[]{:S(2)}) copy-start(bf16[2,640,704]{2,1,0:T(8,128)(2,1)} %copy-done) | copy-start | bytes 5406724
  71.8 1.4 %copy-start.7 = (bf16[3,704,320]{2,1,0:T(8,128)(2,1)S(1)}, bf16[3,704,320]{2,1,0:T(8,128)(2,1)}, u32[]{:S(2)}) copy-start(bf16[3,704,320]{2,1,0:T(8,128)(2,1)} %copy-done.6) | copy-start | bytes 4055044
  73.3 2.5 %copy-start.3 = (bf16[3,3,8,40,320]{4,3,2,1,0:T(8,128)(2,1)S(1)}, bf16[3,3,8,40,320]{4,3,2,1,0:T(8,128)(2,1)}, u32[]{:S(2)}) copy-start(bf16[3,3,8,40,320]{4,3,2,1,0:T(8,128)(2,1)} %copy-done.2) | copy-start | bytes 5529604
  75.6 5.6 %collective-permute-start.11 = (bf16[25,40,320]{2,1,0:T(8,128)(2,1)S(1)}, bf16[25,40,320]{2,1,0:T(8,128)(2,1)S(1)}, u32[]{:S(2)}, u32[]{:S(2)}) collective-permute-start(bf16[25,40,320]{2,1,0:T(8,128)(2,1)S(1)} %get-tuple-element.113), channel_id=1, source_target_pairs={{0,8},{8,0},{1,9},{9,1},{2,10},{10,2},{3,11},{11,3},{4,12},{12,4},... | collective-permute-start | bytes 1920008 | tf_op jit(solution)/shard_map/ppermute | solution.py:30
  77.9 34.6 %collective-permute-start.10 = (bf16[3,8,40,320]{3,2,1,0:T(8,128)(2,1)S(1)}, bf16[3,8,40,320]{3,2,1,0:T(8,128)(2,1)S(1)}, u32[]{:S(2)}, u32[]{:S(2)}) collective-permute-start(bf16[3,8,40,320]{3,2,1,0:T(8,128)(2,1)S(1)} %get-tuple-element.109), channel_id=1, source_target_pairs={{0,6},{2,0},{4,2},{6,4},{1,7},{3,1},{5,3},{7,5},{8,14},{10,8},{12,... | collective-permute-start | bytes 1843208 | tf_op jit(solution)/shard_map/ppermute | solution.py:34
  78.0 34.5 %collective-permute-start.9 = (bf16[3,8,40,320]{3,2,1,0:T(8,128)(2,1)S(1)}, bf16[3,8,40,320]{3,2,1,0:T(8,128)(2,1)S(1)}, u32[]{:S(2)}, u32[]{:S(2)}) collective-permute-start(bf16[3,8,40,320]{3,2,1,0:T(8,128)(2,1)S(1)} %get-tuple-element.108), channel_id=1, source_target_pairs={{0,2},{2,4},{4,6},{6,0},{1,3},{3,5},{5,7},{7,1},{8,10},{10,12},{12... | collective-permute-start | bytes 1843208 | tf_op jit(solution)/shard_map/ppermute | solution.py:34
  82.1 12.8 %collective-permute-start.12 = (f32[8,320]{1,0:T(8,128)S(1)}, f32[8,320]{1,0:T(8,128)S(1)}, u32[]{:S(2)}, u32[]{:S(2)}) collective-permute-start(f32[8,320]{1,0:T(8,128)S(1)} %get-tuple-element.114), channel_id=1, source_target_pairs={{0,1},{1,0},{2,3},{3,2},{4,5},{5,4},{6,7},{7,6},{8,9},{9,8},{10,11... | collective-permute-start | bytes 30728 | tf_op jit(solution)/shard_map/ppermute | solution.py:30
  83.4 16.0 %collective-permute-start.19 = (bf16[2,16,8,320]{3,2,1,0:T(8,128)(2,1)S(1)}, bf16[2,16,8,320]{3,2,1,0:T(8,128)(2,1)S(1)}, u32[]{:S(2)}, u32[]{:S(2)}) collective-permute-start(bf16[2,16,8,320]{3,2,1,0:T(8,128)(2,1)S(1)} %get-tuple-element.120), channel_id=1, source_target_pairs={{0,16},{16,32},{32,48},{48,0},{1,17},{17,33},{33,49},{49,1},{2,18}... | collective-permute-start | bytes 491528 | tf_op jit(solution)/shard_map/ppermute | solution.py:34
  84.8 15.2 %collective-permute-start.20 = (bf16[2,16,8,320]{3,2,1,0:T(8,128)(2,1)S(1)}, bf16[2,16,8,320]{3,2,1,0:T(8,128)(2,1)S(1)}, u32[]{:S(2)}, u32[]{:S(2)}) collective-permute-start(bf16[2,16,8,320]{3,2,1,0:T(8,128)(2,1)S(1)} %get-tuple-element.121), channel_id=1, source_target_pairs={{0,48},{16,0},{32,16},{48,32},{1,49},{17,1},{33,17},{49,33},{2,50}... | collective-permute-start | bytes 491528 | tf_op jit(solution)/shard_map/ppermute | solution.py:34
  94.9 9.0 %collective-permute-start.21 = (bf16[2,16,8,320]{3,2,1,0:T(8,128)(2,1)S(1)}, bf16[2,16,8,320]{3,2,1,0:T(8,128)(2,1)S(1)}, u32[]{:S(2)}, u32[]{:S(2)}) collective-permute-start(bf16[2,16,8,320]{3,2,1,0:T(8,128)(2,1)S(1)} %get-tuple-element.122), channel_id=1, source_target_pairs={{0,32},{16,48},{32,0},{48,16},{1,33},{17,49},{33,1},{49,17},{2,34}... | collective-permute-start | bytes 491528 | tf_op jit(solution)/shard_map/ppermute | solution.py:34
  99.4 5.2 %collective-permute-start.13 = (f32[8,320]{1,0:T(8,128)S(1)}, f32[8,320]{1,0:T(8,128)S(1)}, u32[]{:S(2)}, u32[]{:S(2)}) collective-permute-start(f32[8,320]{1,0:T(8,128)S(1)} %add.50.g0), channel_id=1, source_target_pairs={{0,4},{2,6},{4,0},{6,2},{1,5},{3,7},{5,1},{7,3},{8,12},{10,14},{12... | collective-permute-start | bytes 30728 | tf_op jit(solution)/shard_map/ppermute | solution.py:34
  100.0 6.6 %collective-permute-start.14 = (f32[8,320]{1,0:T(8,128)S(1)}, f32[8,320]{1,0:T(8,128)S(1)}, u32[]{:S(2)}, u32[]{:S(2)}) collective-permute-start(f32[8,320]{1,0:T(8,128)S(1)} %add.50.g0), channel_id=1, source_target_pairs={{0,2},{2,4},{4,6},{6,0},{1,3},{3,5},{5,7},{7,1},{8,10},{10,12},{12... | collective-permute-start | bytes 30728 | tf_op jit(solution)/shard_map/ppermute | solution.py:34
  104.0 8.5 %collective-permute-start.15 = (f32[8,320]{1,0:T(8,128)S(1)}, f32[8,320]{1,0:T(8,128)S(1)}, u32[]{:S(2)}, u32[]{:S(2)}) collective-permute-start(f32[8,320]{1,0:T(8,128)S(1)} %add.50.g0), channel_id=1, source_target_pairs={{0,6},{2,0},{4,2},{6,4},{1,7},{3,1},{5,3},{7,5},{8,14},{10,8},{12,... | collective-permute-start | bytes 30728 | tf_op jit(solution)/shard_map/ppermute | solution.py:34
  104.6 13.4 %collective-permute-start.22 = (bf16[2,16,8,320]{3,2,1,0:T(8,128)(2,1)S(1)}, bf16[2,16,8,320]{3,2,1,0:T(8,128)(2,1)S(1)}, u32[]{:S(2)}, u32[]{:S(2)}) collective-permute-start(bf16[2,16,8,320]{3,2,1,0:T(8,128)(2,1)S(1)} %shard_map.145), channel_id=1, source_target_pairs={{0,4},{2,6},{4,0},{6,2},{1,5},{3,7},{5,1},{7,3},{8,12},{10,14},{12... | collective-permute-start | bytes 491528 | tf_op jit(solution)/shard_map/ppermute | solution.py:34
  113.5 6.9 %collective-permute-start.16 = (bf16[2,16,8,320]{3,2,1,0:T(8,128)(2,1)S(1)}, bf16[2,16,8,320]{3,2,1,0:T(8,128)(2,1)S(1)}, u32[]{:S(2)}, u32[]{:S(2)}) collective-permute-start(bf16[2,16,8,320]{3,2,1,0:T(8,128)(2,1)S(1)} %get-tuple-element.116), channel_id=1, source_target_pairs={{0,16},{16,32},{32,48},{48,0},{1,17},{17,33},{33,49},{49,1},{2,18}... | collective-permute-start | bytes 491528 | tf_op jit(solution)/shard_map/ppermute | solution.py:34
  114.9 5.7 %collective-permute-start.17 = (bf16[2,16,8,320]{3,2,1,0:T(8,128)(2,1)S(1)}, bf16[2,16,8,320]{3,2,1,0:T(8,128)(2,1)S(1)}, u32[]{:S(2)}, u32[]{:S(2)}) collective-permute-start(bf16[2,16,8,320]{3,2,1,0:T(8,128)(2,1)S(1)} %get-tuple-element.117), channel_id=1, source_target_pairs={{0,48},{16,0},{32,16},{48,32},{1,49},{17,1},{33,17},{49,33},{2,50}... | collective-permute-start | bytes 491528 | tf_op jit(solution)/shard_map/ppermute | solution.py:34
  116.8 7.2 %collective-permute-start.18 = (bf16[2,16,8,320]{3,2,1,0:T(8,128)(2,1)S(1)}, bf16[2,16,8,320]{3,2,1,0:T(8,128)(2,1)S(1)}, u32[]{:S(2)}, u32[]{:S(2)}) collective-permute-start(bf16[2,16,8,320]{3,2,1,0:T(8,128)(2,1)S(1)} %get-tuple-element.118), channel_id=1, source_target_pairs={{0,32},{16,48},{32,0},{48,16},{1,33},{17,49},{33,1},{49,17},{2,34}... | collective-permute-start | bytes 491528 | tf_op jit(solution)/shard_map/ppermute | solution.py:34
  124.7 6.2 %collective-permute-start.23 = (bf16[16,8,320]{2,1,0:T(8,128)(2,1)S(1)}, bf16[16,8,320]{2,1,0:T(8,128)(2,1)S(1)}, u32[]{:S(2)}, u32[]{:S(2)}) collective-permute-start(bf16[16,8,320]{2,1,0:T(8,128)(2,1)S(1)} %get-tuple-element.124), channel_id=1, source_target_pairs={{0,64},{64,0},{1,65},{65,1},{2,66},{66,2},{3,67},{67,3},{4,68},{68... | collective-permute-start | bytes 245768 | tf_op jit(solution)/shard_map/ppermute | solution.py:30
  134.3 0.8 copy-start.16

commit v5 on v4

--- a/solution.py
+++ b/solution.py
@@ -10,8 +10,9 @@
 
 TENSOR = ("y", "xl")
 DP = ("xh", "z", "c")
+CHIP = ("xh", "z")
 EPS = 1e-05
-PLACES = 3
+PLACES = 4
 BF = jnp.bfloat16
 F32 = jnp.float32
 
@@ -63,7 +64,7 @@
             g = lax.div(m, 11)
             s = m - g * 11
             live = k < alive
-            at = p * 16 + g
+            at = lax.shift_right_logical(p, 1) * 16 + g
             r = cnt[at]
 
             @pl.when(live)
@@ -72,14 +73,15 @@
 
             rank = jnp.where(live, r, -1)
 
-            @pl.when(p == me)
+            @pl.when(lax.shift_right_logical(p, 1) == lax.shift_right_logical(me, 1))
             def _():
-                dest_g[k] = g
-                dest_r[k] = rank
+                q = jnp.where(p == me, k, k + 11)
+                dest_g[q] = lax.shift_right_logical(g, 1)
+                dest_r[q] = jnp.where((g & 1) == (me & 1), rank, -1)
 
             @pl.when(g == me)
             def _():
-                src_p[s] = p
+                src_p[s] = lax.shift_right_logical(p, 1)
                 src_r[s] = rank
 
             return jnp.maximum(top, rank + 1)
@@ -91,9 +93,10 @@
 
 def index_work(meta, trunc, tmap):
     i11 = jax.ShapeDtypeStruct((11,), jnp.int32)
+    i22 = jax.ShapeDtypeStruct((22,), jnp.int32)
     return pl.pallas_call(
         index_kernel,
-        out_shape=(i11, i11, i11, i11, jax.ShapeDtypeStruct((1,), jnp.int32)),
+        out_shape=(i22, i22, i11, i11, jax.ShapeDtypeStruct((1,), jnp.int32)),
         in_specs=smem(3),
         out_specs=tuple(smem(5)),
         scratch_shapes=[pltpu.SMEM((256,), jnp.int32)],
@@ -299,11 +302,7 @@
     )
 
 
-def finish_kernel(dest_g, dest_r, dn, got, lat, grad, gain, own, packed, sems):
-    def sent(k):
-        rank = dest_r[k]
-        return (rank >= 0) & (rank < PLACES)
-
+def finish_kernel(alive, dn, got, lat, grad, gain, own):
     for k in range(11):
         x_hat, inv_std = normalise(lat[k])
         d_hat = (dn[k] + got[k].astype(F32)) * gain[...]
@@ -312,33 +311,37 @@
             - jnp.mean(d_hat, axis=-1, keepdims=True)
             - x_hat * jnp.mean(d_hat * x_hat, axis=-1, keepdims=True)
         )
-        own[k] = jnp.where(dest_r[k] >= 0, out, 0.0).astype(BF)
-
-        @pl.when(sent(k))
-        def _():
-            place = dest_g[k] * PLACES + dest_r[k]
-            pltpu.make_async_copy(own.at[k], packed.at[place], sems.at[k]).start()
-
-    for k in range(11):
-
-        @pl.when(sent(k))
-        def _():
-            pltpu.make_async_copy(own.at[k], packed.at[0], sems.at[k]).wait()
-
-
-def finish(dest_g, dest_r, dn, got, lat, grad, gain):
+        own[k] = jnp.where(k < alive[0], out, 0.0).astype(BF)
+
+
+def finish(alive, *arrays):
+    return local(finish_kernel, 10, (((11, 32, 640), BF),), arrays, (), (alive,))[0]
+
+
+def pack_kernel(dest_g, dest_r, own, peer, packed, sems):
+    def each(act):
+        for q in range(22):
+            rank = dest_r[q]
+
+            @pl.when((rank >= 0) & (rank < PLACES))
+            def _():
+                tile = own.at[q] if q < 11 else peer.at[q - 11]
+                act(pltpu.make_async_copy(tile, packed.at[dest_g[q] * PLACES + rank], sems.at[q]))
+
+    each(lambda copy: copy.start())
+    each(lambda copy: copy.wait())
+
+
+def pack(dest_g, dest_r, own, peer):
     return pl.pallas_call(
-        finish_kernel,
-        out_shape=(
-            jax.ShapeDtypeStruct((11, 32, 640), BF),
-            jax.ShapeDtypeStruct((16 * PLACES, 32, 640), BF),
-        ),
-        in_specs=smem(2) + vmem(5),
-        out_specs=(vmem(1)[0], pl.BlockSpec(memory_space=HBM)),
-        scratch_shapes=[pltpu.SemaphoreType.DMA((11,))],
-        compiler_params=grant(10),
-        name="finish",
-    )(dest_g, dest_r, dn, got, lat, grad, gain)
+        pack_kernel,
+        out_shape=HBM((8 * PLACES, 32, 640), BF),
+        in_specs=smem(2) + vmem(2),
+        out_specs=pl.BlockSpec(memory_space=HBM),
+        scratch_shapes=[pltpu.SemaphoreType.DMA((22,))],
+        compiler_params=grant(3),
+        name="pack",
+    )(dest_g, dest_r, own, peer)
 
 
 def unpack_kernel(src_p, src_r, came, placed, blank, sems):
@@ -397,11 +400,11 @@
     out[...] = x.astype(BF)
 
 
-def over_y_kernel(meta, own, from_down, from_up, g0, g1, g2, g3, keep, up, down, far, parts):
+def over_y_kernel(meta, own, from_down, from_up, near, across, keep, up, down, far, parts):
     for j in range(3):
         x = own[j] + from_down[j].astype(F32) + from_up[j].astype(F32)
         parts[:, :, 5 * j : 5 * j + 5] = x.reshape(2, 4, 5, 8, 320)
-    tail = resplit((g0[...] + g1[...]) + (g2[...] + g3[...]))
+    tail = resplit(near[...] + across[...])
     for k in range(2):
         for z in range(4):
             parts[k, z, 15] = tail
@@ -447,8 +450,11 @@
     came = over_ring(*far_sent)
     (across,) = local(far_z_kernel, 3, ((part, BF),), (far_own, *came))
     across = ring(across, "y", 2)
-    tails = [tail] + [ring(tail, "y", d) for d in (2, 1, -1)]
-    own, *sent = local(over_y_kernel, 6, parts, (own, from_down, from_up, *tails), whole, (meta,))
+    tail = tail + lax.ppermute(tail, "y", [(0, 1), (1, 0), (2, 3), (3, 2)])
+    across_y = lax.ppermute(tail, "y", [(0, 3), (3, 0), (1, 2), (2, 1)])
+    own, *sent = local(
+        over_y_kernel, 6, parts, (own, from_down, from_up, tail, across_y), whole, (meta,)
+    )
     came = over_ring(*sent)
     keep, give = local(
         over_z_kernel, 4, ((part[1:], F32), (part[1:], BF)), (own, *came, across),
@@ -461,19 +467,19 @@
 
 
 def route(packed):
-    return lax.all_to_all(packed, DP, 0, 0, tiled=True)
-
-
-def more_rounds(placed, own, most, dest_g, dest_r, src_p, src_r):
+    return lax.all_to_all(packed, CHIP, 0, 0, tiled=True)
+
+
+def more_rounds(placed, own, peer, most, dest_g, dest_r, src_p, src_r):
     def more(state):
         return state[0] < most[0]
 
     def one(state):
         t, placed = state
-        groups = jnp.arange(16, dtype=jnp.int32)
+        groups = jnp.arange(8, dtype=jnp.int32)
         hit = (dest_g[None, :] == groups[:, None]) & (dest_r[None, :] == t)
-        pick = jnp.sum(jnp.where(hit, jnp.arange(11, dtype=jnp.int32)[None, :], 0), axis=1)
-        came = route(jnp.take(own, pick, axis=0))
+        pick = jnp.sum(jnp.where(hit, jnp.arange(22, dtype=jnp.int32)[None, :], 0), axis=1)
+        came = route(jnp.take(jnp.concatenate([own, peer]), pick, axis=0))
         here = src_r == t
         new = jnp.take(came, jnp.where(here, src_p, 0), axis=0)
         return t + 1, jnp.where(here[:, None, None], new, placed)
@@ -506,12 +512,13 @@
     far_mine, far_send = far_grads(meta, turned, far_acts, tail)
     far_got = swap(far_send, "c")
     tiles = (11, 32, 640)
-    own, packed = finish(
-        dest_g, dest_r, dn.reshape(tiles), got.reshape(tiles), latents, rows, gain
-    )
+    alive = lax.dynamic_slice_in_dim(trunc, lax.axis_index(DP), 1) - 29
+    own = finish(alive, dn.reshape(tiles), got.reshape(tiles), latents, rows, gain)
+    peer = swap(own, "c")
+    packed = pack(dest_g, dest_r, own, peer)
     came = route(packed)
     placed = unpack(src_p, src_r, came)
-    placed = more_rounds(placed, own, most, dest_g, dest_r, src_p, src_r)
+    placed = more_rounds(placed, own, peer, most, dest_g, dest_r, src_p, src_r)
     grads = reduce_weights(meta, near_mine, near_got, far_mine, far_got)
     return placed, *grads
 

time: 135 us -> 177 us (1.31)
  the two profiles are of different devices: /device:TPU:28 before, /device:TPU:0 now
where the time goes in v5:
time: 177 us
  waiting for transfers between devices  68.1 us (38%)
  starting transfers between devices  49.3 us (28%)
  Pallas kernels  37.9 us (21%)
  local copies, waits for them, and re-layouts  15.9 us (9%)
  other arithmetic  2.49 us (1%)
    ppermute x13, waiting for transfers between devices, ring(): return lax.ppermute(x, axis, [(i, (i + step) % 4) for i in range(4)])  33.1 us
    pallas_call x12, Pallas kernels, local(): pl.pallas_call(kernel, out_shape=tuple((jax.ShapeDtypeStruct(s, d) for s,...  27.8 us
    ppermute x13, starting transfers between devices, ring(): return lax.ppermute(x, axis, [(i, (i + step) % 4) for i in range(4)])  25.4 us
    ppermute x9, waiting for transfers between devices, swap(): return lax.ppermute(x, axis, [(0, 1), (1, 0)])  20.1 us
    all_to_all x2, starting transfers between devices, route(): return lax.all_to_all(packed, CHIP, 0, 0, tiled=True)  13.5 us
    unnamed x44, local copies, waits for them, and re-layouts  11.3 us
    all_to_all x2, waiting for transfers between devices, route(): return lax.all_to_all(packed, CHIP, 0, 0, tiled=True)  8.96 us
    ppermute x9, starting transfers between devices, swap(): return lax.ppermute(x, axis, [(0, 1), (1, 0)])  7.65 us
  transfers between devices with their start and end apart: 26, of which 15 were waited for; matrix products, arithmetic and copies ran while one was open for 0% of the time, Pallas kernels for 16%

profile of v5, /device:TPU:0, one launch (start us, length us, event | category | flops | bytes accessed | tf_op | source)
XLA Modules:
  0.0 176.6 jit_solution(9490443376761983722)
XLA Ops:
  1.7 1.2 dynamic-slice_bitcast_fusion
  3.8 1.7 collective-permute-start.1
  5.5 1.5 collective-permute-start.3
  8.2 1.0 prologue.1.grad
  9.2 1.7 collective-permute-start
  10.9 10.1 %collective-permute-done.1.below = bf16[3,160,640]{2,1,0:T(8,128)(2,1)S(1)} collective-permute-done((bf16[3,160,640]{2,1,0:T(8,128)(2,1)}, bf16[3,160,640]{2,1,0:T(8,128)(2,1)S(1)}, u32[]{:S(2)}, u32[]{:S(2)}) %collective-permute-start.1) | collective-permute-done | bytes 614432 | tf_op jit(solution)/shard_map/ppermute | solution.py:35
  21.5 1.5 collective-permute-done.2.below2
  23.9 4.8 %shard_map.137 = (f32[352,640]{1,0:T(8,128)S(1)}, bf16[3,352,960]{2,1,0:T(8,128)(2,1)S(1)}, bf16[3,960,640]{2,1,0:T(8,128)(2,1)S(1)}) custom-call(s32[4]{0:T(128)S(1)} %pad_add_fusion.meta, bf16[2,352,640]{2,1,0:T(8,128)(2,1)S(1)} %bitcast.41, bf16[320,640]{1,0:T(8,128)(2,1)S(1)} %bitcast.43, bf16[320,640]{1,0:T(8,128)(2,1)S(1)} %bitcast.44, ...), custom_call_target="tpu_custom_call" | custom-call | tf_op jit(solution)/shard_map/pallas_call | solution.py:162
  28.8 1.9 %collective-permute-done = bf16[2,11,32,640]{3,2,1,0:T(8,128)(2,1)S(1)} collective-permute-done((bf16[2,11,32,640]{3,2,1,0:T(8,128)(2,1)S(1)}, bf16[2,11,32,640]{3,2,1,0:T(8,128)(2,1)S(1)}, u32[]{:S(2)}, u32[]{:S(2)}) %collective-permute-start) | collective-permute-done | bytes 901152 | tf_op jit(solution)/shard_map/ppermute | solution.py:31
  30.6 3.8 %shard_map.138 = (f32[704,640]{1,0:T(8,128)S(1)}, bf16[3,704,960]{2,1,0:T(8,128)(2,1)S(1)}, bf16[2,704,640]{2,1,0:T(8,128)(2,1)S(1)}, bf16[2,640,704]{2,1,0:T(8,128)(2,1)S(1)}) custom-call(bf16[2,352,640]{2,1,0:T(8,128)(2,1)S(1)} %bitcast.42, bf16[2,352,640]{2,1,0:T(8,128)(2,1)S(1)} %bitcast.46, f32[352,640]{1,0:T(8,128)S(1)} %get-tuple-element.152.own_dn, ...), custom_call_target="tpu_custom_call" | custom-call | tf_op jit(solution)/shard_map/pallas_call | solution.py:162
  34.5 5.6 %shard_map.141 = (bf16[3,3,8,40,320]{4,3,2,1,0:T(8,128)(2,1)S(1)}, bf16[3,3,8,40,320]{4,3,2,1,0:T(8,128)(2,1)}) custom-call(s32[4]{0:T(128)S(1)} %pad_add_fusion.meta, bf16[2,640,704]{2,1,0:T(8,128)(2,1)S(1)} %get-tuple-element.161.turned, bf16[3,704,960]{2,1,0:T(8,128)(2,1)S(1)} %get-tuple-element.162.acts), custom_call_target="tpu_custom_call" | custom-call | tf_op jit(solution)/shard_map/pallas_call | solution.py:162
  40.4 2.9 %collective-permute-start.6 = (bf16[3,160,640]{2,1,0:T(8,128)(2,1)S(1)}, bf16[3,160,640]{2,1,0:T(8,128)(2,1)S(1)}, u32[]{:S(2)}, u32[]{:S(2)}) collective-permute-start(bf16[3,160,640]{2,1,0:T(8,128)(2,1)S(1)} %collective-permute-done.4.above2), channel_id=1, source_target_pairs={{0,6},{2,0},{4,2},{6,4},{1,7},{3,1},{5,3},{7,5},{8,14},{10,8},{12,... | collective-permute-start | bytes 1843208 | tf_op jit(solution)/shard_map/ppermute | solution.py:35
  43.4 14.2 %collective-permute-done.5.first = bf16[3,160,640]{2,1,0:T(8,128)(2,1)S(1)} collective-permute-done((bf16[3,160,640]{2,1,0:T(8,128)(2,1)S(1)}, bf16[3,160,640]{2,1,0:T(8,128)(2,1)S(1)}, u32[]{:S(2)}, u32[]{:S(2)}) %collective-permute-start.5) | collective-permute-done | bytes 614432 | tf_op jit(solution)/shard_map/ppermute | solution.py:35
  57.6 4.2 %shard_map.139 = (f32[352,640]{1,0:T(8,128)S(1)}, bf16[352,640]{1,0:T(8,128)(2,1)}, bf16[3,704,320]{2,1,0:T(8,128)(2,1)S(1)}, f32[8,320]{1,0:T(8,128)S(1)}) custom-call(s32[4]{0:T(128)S(1)} %pad_add_fusion.meta, bf16[2,704,640]{2,1,0:T(8,128)(2,1)S(1)} %get-tuple-element.155.rows, f32[1,640]{1,0:T(1,128)S(1)} %broadcast_in_dim.67.gain, ...), custom_call_target="tpu_custom_call" | custom-call | tf_op jit(solution)/shard_map/pallas_call | solution.py:162
  61.8 1.2 copy-done.4
  64.0 1.5 collective-permute-start.7
  66.7 9.4 %collective-permute-done.7 = bf16[352,640]{1,0:T(8,128)(2,1)S(1)} collective-permute-done((bf16[352,640]{1,0:T(8,128)(2,1)}, bf16[352,640]{1,0:T(8,128)(2,1)S(1)}, u32[]{:S(2)}, u32[]{:S(2)}) %collective-permute-start.7) | collective-permute-done | bytes 450592 | tf_op jit(solution)/shard_map/ppermute | solution.py:31
  76.9 1.0 copy-done.3
  77.9 1.2 copy-done.10
  79.1 1.0 copy-done.12
  80.9 6.1 %routes.1 = (s32[22]{0:T(128)S(1)}, s32[22]{0:T(128)S(1)}, s32[11]{0:T(128)S(1)}, s32[11]{0:T(128)S(1)}, s32[1]{0:T(128)}) custom-call(s32[4]{0:T(128)S(1)} %pad_add_fusion.meta, s32[16]{0:T(128)S(1)} %copy-done.17, s32[176]{0:T(256)S(1)} %copy-done.19), custom_call_target="tpu_custom_call" | custom-call | tf_op jit(solution)/shard_map/routes/pallas_call | solution.py:97
  86.9 1.5 pack.1
  88.4 7.8 %all-to-all-start.1 = ((bf16[32,32,640]{2,1,0:T(8,128)(2,1)}), bf16[32,32,640]{2,1,0:T(8,128)(2,1)}, u32[]{:S(2)}, u32[]{:S(2)}) async-start(bf16[32,32,640]{2,1,0:T(8,128)(2,1)} %pack.1), calls=%async_computation.1 | async-start | bytes 2621440 | tf_op jit(solution)/shard_map/all_to_all | solution.py:470
  96.2 1.6 copy-done.5
  97.8 2.3 %shard_map.143 = (bf16[25,40,320]{2,1,0:T(8,128)(2,1)S(1)}, bf16[25,40,320]{2,1,0:T(8,128)(2,1)S(1)}) custom-call(s32[4]{0:T(128)S(1)} %pad_add_fusion.meta, bf16[2,640,704]{2,1,0:T(8,128)(2,1)S(1)} %get-tuple-element.161.turned, bf16[3,704,320]{2,1,0:T(8,128)(2,1)S(1)} %copy-done.5, f32[8,320]{1,0:T(8,128)S(1)} %get-tuple-element.169.tail), custom_call_target="tpu_custom_call" | custom-call | tf_op jit(solution)/shard_map/pallas_call | solution.py:162
  100.4 2.1 %shard_map.142 = (f32[3,8,40,320]{3,2,1,0:T(8,128)S(1)}, bf16[3,8,40,320]{3,2,1,0:T(8,128)(2,1)S(1)}, bf16[3,8,40,320]{3,2,1,0:T(8,128)(2,1)S(1)}) custom-call(bf16[3,3,8,40,320]{4,3,2,1,0:T(8,128)(2,1)S(1)} %copy-done.1, bf16[3,3,8,40,320]{4,3,2,1,0:T(8,128)(2,1)} %collective-permute-done.9.got), custom_call_target="tpu_custom_call" | custom-call | tf_op jit(solution)/shard_map/pallas_call | solution.py:162
  102.7 3.1 %collective-permute-start.11 = (bf16[3,8,40,320]{3,2,1,0:T(8,128)(2,1)S(1)}, bf16[3,8,40,320]{3,2,1,0:T(8,128)(2,1)S(1)}, u32[]{:S(2)}, u32[]{:S(2)}) collective-permute-start(bf16[3,8,40,320]{3,2,1,0:T(8,128)(2,1)S(1)} %get-tuple-element.167), channel_id=1, source_target_pairs={{0,6},{2,0},{4,2},{6,4},{1,7},{3,1},{5,3},{7,5},{8,14},{10,8},{12,... | collective-permute-start | bytes 1843208 | tf_op jit(solution)/shard_map/ppermute | solution.py:35
  107.4 5.0 %collective-permute-done.13 = f32[8,320]{1,0:T(8,128)S(1)} collective-permute-done((f32[8,320]{1,0:T(8,128)S(1)}, f32[8,320]{1,0:T(8,128)S(1)}, u32[]{:S(2)}, u32[]{:S(2)}) %collective-permute-start.13) | collective-permute-done | bytes 10272 | tf_op jit(solution)/shard_map/ppermute | solution.py:31
  112.5 1.7 collective-permute-start.19
  114.2 1.5 collective-permute-start.20
  115.7 5.9 %collective-permute-done.14 = f32[8,320]{1,0:T(8,128)S(1)} collective-permute-done((f32[8,320]{1,0:T(8,128)S(1)}, f32[8,320]{1,0:T(8,128)S(1)}, u32[]{:S(2)}, u32[]{:S(2)}) %collective-permute-start.14) | collective-permute-done | bytes 10272 | tf_op jit(solution)/shard_map/ppermute | solution.py:453
  121.7 3.5 %collective-permute-start.21 = (bf16[2,16,8,320]{3,2,1,0:T(8,128)(2,1)S(1)}, bf16[2,16,8,320]{3,2,1,0:T(8,128)(2,1)S(1)}, u32[]{:S(2)}, u32[]{:S(2)}) collective-permute-start(bf16[2,16,8,320]{3,2,1,0:T(8,128)(2,1)S(1)} %get-tuple-element.180), channel_id=1, source_target_pairs={{0,32},{16,48},{32,0},{48,16},{1,33},{17,49},{33,1},{49,17},{2,34}... | collective-permute-start | bytes 491528 | tf_op jit(solution)/shard_map/ppermute | solution.py:35
  125.2 2.6 %collective-permute-start.15 = (f32[8,320]{1,0:T(8,128)S(1)}, f32[8,320]{1,0:T(8,128)S(1)}, u32[]{:S(2)}, u32[]{:S(2)}) collective-permute-start(f32[8,320]{1,0:T(8,128)S(1)} %add.71.near), channel_id=1, source_target_pairs={{0,6},{6,0},{2,4},{4,2},{1,7},{7,1},{3,5},{5,3},{8,14},{14,8},{10,... | collective-permute-start | bytes 30728 | tf_op jit(solution)/shard_map/ppermute | solution.py:454
  127.8 2.1 %collective-permute-done.21.far = bf16[2,16,8,320]{3,2,1,0:T(8,128)(2,1)S(1)} collective-permute-done((bf16[2,16,8,320]{3,2,1,0:T(8,128)(2,1)S(1)}, bf16[2,16,8,320]{3,2,1,0:T(8,128)(2,1)S(1)}, u32[]{:S(2)}, u32[]{:S(2)}) %collective-permute-start.21) | collective-permute-done | bytes 163872 | tf_op jit(solution)/shard_map/ppermute | solution.py:35
  129.9 3.6 %collective-permute-start.22 = (bf16[2,16,8,320]{3,2,1,0:T(8,128)(2,1)S(1)}, bf16[2,16,8,320]{3,2,1,0:T(8,128)(2,1)S(1)}, u32[]{:S(2)}, u32[]{:S(2)}) collective-permute-start(bf16[2,16,8,320]{3,2,1,0:T(8,128)(2,1)S(1)} %shard_map.146), channel_id=1, source_target_pairs={{0,4},{2,6},{4,0},{6,2},{1,5},{3,7},{5,1},{7,3},{8,12},{10,14},{12... | collective-permute-start | bytes 491528 | tf_op jit(solution)/shard_map/ppermute | solution.py:35
  133.5 1.8 %shard_map.145 = (f32[2,16,8,320]{3,2,1,0:T(8,128)S(1)}, bf16[2,16,8,320]{3,2,1,0:T(8,128)(2,1)}, bf16[2,16,8,320]{3,2,1,0:T(8,128)(2,1)}, bf16[2,16,8,320]{3,2,1,0:T(8,128)(2,1)}) custom-call(s32[4]{0:T(128)S(1)} %pad_add_fusion.meta, f32[3,8,40,320]{3,2,1,0:T(8,128)S(1)} %get-tuple-element.165.own, ...), custom_call_target="tpu_custom_call" | custom-call | tf_op jit(solution)/shard_map/pallas_call | solution.py:162
  136.1 1.7 collective-permute-start.16
  137.8 1.5 collective-permute-start.17
  139.3 2.0 %collective-permute-start.18 = (bf16[2,16,8,320]{3,2,1,0:T(8,128)(2,1)}, bf16[2,16,8,320]{3,2,1,0:T(8,128)(2,1)S(1)}, u32[]{:S(2)}, u32[]{:S(2)}) collective-permute-start(bf16[2,16,8,320]{3,2,1,0:T(8,128)(2,1)} %get-tuple-element.176), channel_id=1, source_target_pairs={{0,32},{16,48},{32,0},{48,16},{1,33},{17,49},{33,1},{49,17},{2,34}... | collective-permute-start | bytes 491528 | tf_op jit(solution)/shard_map/ppermute | solution.py:35
  141.3 3.9 %collective-permute-done.16.down = bf16[2,16,8,320]{3,2,1,0:T(8,128)(2,1)S(1)} collective-permute-done((bf16[2,16,8,320]{3,2,1,0:T(8,128)(2,1)}, bf16[2,16,8,320]{3,2,1,0:T(8,128)(2,1)S(1)}, u32[]{:S(2)}, u32[]{:S(2)}) %collective-permute-start.16) | collective-permute-done | bytes 163872 | tf_op jit(solution)/shard_map/ppermute | solution.py:35
  145.3 1.1 collective-permute-done.17.up
  146.4 1.5 collective-permute-done.18.far
  149.6 3.0 %collective-permute-start.23 = (bf16[16,8,320]{2,1,0:T(8,128)(2,1)S(1)}, bf16[16,8,320]{2,1,0:T(8,128)(2,1)S(1)}, u32[]{:S(2)}, u32[]{:S(2)}) collective-permute-start(bf16[16,8,320]{2,1,0:T(8,128)(2,1)S(1)} %get-tuple-element.182), channel_id=1, source_target_pairs={{0,64},{64,0},{1,65},{65,1},{2,66},{66,2},{3,67},{67,3},{4,68},{68... | collective-permute-start | bytes 245768 | tf_op jit(solution)/shard_map/ppermute | solution.py:31
  152.8 1.6 unpack.1
  154.4 1.5 collective-permute-done.23.got
  157.2 18.7 %while.12 = (s32[]{:T(128)}, bf16[11,32,640]{2,1,0:T(8,128)(2,1)S(1)}, s32[1]{0:T(128)}, s32[11]{0:T(128)S(1)}, s32[11]{0:T(128)S(1)}, /*index=5*/s32[22]{0:T(12...) while((s32[]{:T(128)}, bf16[11,32,640]{2,1,0:T(8,128)(2,1)S(1)}, s32[1]{0:T(128)}, ...), condition=%wide.region_2.3_spmd, body=%wide.region_0.2_spmd.sunk | while | flops 617372 | bytes 4555640 | solution.py:487
  159.4 5.7 %all-to-all-start = ((bf16[8,32,640]{2,1,0:T(8,128)(2,1)}), bf16[8,32,640]{2,1,0:T(8,128)(2,1)S(1)}, u32[]{:S(2)}, u32[]{:S(2)}) async-start(bf16[8,32,640]{2,1,0:T(8,128)(2,1)} %broadcast_select_fusion.3), calls=%async_computation | async-start | bytes 655360 | tf_op jit(solution)/shard_map/while/body/all_to_all | solution.py:470
  165.2 9.0 %all-to-all-done = bf16[8,32,640]{2,1,0:T(8,128)(2,1)S(1)} async-done(((bf16[8,32,640]{2,1,0:T(8,128)(2,1)}), bf16[8,32,640]{2,1,0:T(8,128)(2,1)S(1)}, u32[]{:S(2)}, u32[]{:S(2)}) %all-to-all-start) | async-done | bytes 327712 | tf_op jit(solution)/shard_map/while/body/all_to_all | solution.py:470
  (88 shorter events, 17.4 us)
Async XLA Ops:
  0.6 6.5 %copy-start.16 = (f32[1000]{0:T(1024)S(1)}, f32[1000]{0:T(1024)}, u32[]{:S(2)}) copy-start(f32[1000]{0:T(1024)} %constant.82.clone.table) | copy-start | bytes 12004
  0.6 6.4 %copy-start.21 = (f32[640]{0:T(1024)S(1)}, f32[640]{0:T(1024)}, u32[]{:S(2)}) copy-start(f32[640]{0:T(1024)} %param.17) | copy-start | bytes 7684
  0.7 6.5 %copy-start.2 = (bf16[11,32,640]{2,1,0:T(8,128)(2,1)S(1)}, bf16[11,32,640]{2,1,0:T(8,128)(2,1)}, u32[]{:S(2)}) copy-start(bf16[11,32,640]{2,1,0:T(8,128)(2,1)} %lat.3) | copy-start | bytes 1351684
  0.7 6.5 %copy-start.17 = (s32[16]{0:T(128)S(1)}, s32[16]{0:T(128)}, u32[]{:S(2)}) copy-start(s32[16]{0:T(128)} %trunc.3) | copy-start | bytes 196
  0.7 6.5 %copy-start.18 = (s32[176]{0:T(256)S(1)}, s32[176]{0:T(256)}, u32[]{:S(2)}) copy-start(s32[176]{0:T(256)} %times.1) | copy-start | bytes 2116
  1.7 22.2 %copy-start.6 = (bf16[640,320]{0,1:T(8,128)(2,1)S(1)}, bf16[640,320]{0,1:T(8,128)(2,1)}, u32[]{:S(2)}) copy-start(bf16[640,320]{0,1:T(8,128)(2,1)} %param.18) | copy-start | bytes 1228804
  1.7 22.2 %copy-start.7 = (bf16[640,320]{0,1:T(8,128)(2,1)S(1)}, bf16[640,320]{0,1:T(8,128)(2,1)}, u32[]{:S(2)}) copy-start(bf16[640,320]{0,1:T(8,128)(2,1)} %param.19) | copy-start | bytes 1228804
  1.7 22.2 %copy-start.8 = (bf16[640,320]{0,1:T(8,128)(2,1)S(1)}, bf16[640,320]{0,1:T(8,128)(2,1)}, u32[]{:S(2)}) copy-start(bf16[640,320]{0,1:T(8,128)(2,1)} %param.20) | copy-start | bytes 1228804
  3.8 17.2 %collective-permute-start.1 = (bf16[3,160,640]{2,1,0:T(8,128)(2,1)}, bf16[3,160,640]{2,1,0:T(8,128)(2,1)S(1)}, u32[]{:S(2)}, u32[]{:S(2)}) collective-permute-start(bf16[3,160,640]{2,1,0:T(8,128)(2,1)} %pad_maximum_fusion.1), channel_id=1, source_target_pairs={{0,2},{2,4},{4,6},{6,0},{1,3},{3,5},{5,7},{7,1},{8,10},{10,12},{12... | collective-permute-start | bytes 1843208 | tf_op jit(solution)/shard_map/ppermute | solution.py:35
  5.5 15.6 %collective-permute-start.3 = (bf16[3,160,640]{2,1,0:T(8,128)(2,1)}, bf16[3,160,640]{2,1,0:T(8,128)(2,1)}, u32[]{:S(2)}, u32[]{:S(2)}) collective-permute-start(bf16[3,160,640]{2,1,0:T(8,128)(2,1)} %pad_maximum_fusion.1), channel_id=1, source_target_pairs={{0,6},{2,0},{4,2},{6,4},{1,7},{3,1},{5,3},{7,5},{8,14},{10,8},{12,... | collective-permute-start | bytes 1843208 | tf_op jit(solution)/shard_map/ppermute | solution.py:35
  7.2 1.0 copy-start.13
  9.2 21.4 %collective-permute-start = (bf16[2,11,32,640]{3,2,1,0:T(8,128)(2,1)S(1)}, bf16[2,11,32,640]{3,2,1,0:T(8,128)(2,1)S(1)}, u32[]{:S(2)}, u32[]{:S(2)}) collective-permute-start(bf16[2,11,32,640]{3,2,1,0:T(8,128)(2,1)S(1)} %prologue.1.grad), channel_id=1, source_target_pairs={{0,1},{1,0},{2,3},{3,2},{4,5},{5,4},{6,7},{7,6},{8,9},{9,8},{10,11... | collective-permute-start | bytes 2703368 | tf_op jit(solution)/shard_map/ppermute | solution.py:31
  21.0 2.0 %collective-permute-start.2 = (bf16[3,160,640]{2,1,0:T(8,128)(2,1)S(1)}, bf16[3,160,640]{2,1,0:T(8,128)(2,1)S(1)}, u32[]{:S(2)}, u32[]{:S(2)}) collective-permute-start(bf16[3,160,640]{2,1,0:T(8,128)(2,1)S(1)} %collective-permute-done.1.below), channel_id=1, source_target_pairs={{0,8},{8,0},{1,9},{9,1},{2,10},{10,2},{3,11},{11,3},{4,12},{12,4},... | collective-permute-start | bytes 1843208 | tf_op jit(solution)/shard_map/ppermute | solution.py:31
  21.1 2.8 %collective-permute-start.4 = (bf16[3,160,640]{2,1,0:T(8,128)(2,1)}, bf16[3,160,640]{2,1,0:T(8,128)(2,1)S(1)}, u32[]{:S(2)}, u32[]{:S(2)}) collective-permute-start(bf16[3,160,640]{2,1,0:T(8,128)(2,1)} %collective-permute-done.3.above), channel_id=1, source_target_pairs={{0,8},{8,0},{1,9},{9,1},{2,10},{10,2},{3,11},{11,3},{4,12},{12,4},... | collective-permute-start | bytes 1843208 | tf_op jit(solution)/shard_map/ppermute | solution.py:31
  40.1 21.7 %copy-start = (bf16[3,3,8,40,320]{4,3,2,1,0:T(8,128)(2,1)}, bf16[3,3,8,40,320]{4,3,2,1,0:T(8,128)(2,1)S(1)}, u32[]{:S(2)}) copy-start(bf16[3,3,8,40,320]{4,3,2,1,0:T(8,128)(2,1)S(1)} %get-tuple-element.163.mine) | copy-start | bytes 5529604
  40.1 60.3 %collective-permute-start.9 = (bf16[3,3,8,40,320]{4,3,2,1,0:T(8,128)(2,1)}, bf16[3,3,8,40,320]{4,3,2,1,0:T(8,128)(2,1)}, u32[]{:S(2)}, u32[]{:S(2)}) collective-permute-start(bf16[3,3,8,40,320]{4,3,2,1,0:T(8,128)(2,1)} %get-tuple-element.164), channel_id=1, source_target_pairs={{0,8},{8,0},{1,9},{9,1},{2,10},{10,2},{3,11},{11,3},{4,12},{12,4},... | collective-permute-start | bytes 5529608 | tf_op jit(solution)/shard_map/ppermute | solution.py:31
  40.1 17.5 %collective-permute-start.5 = (bf16[3,160,640]{2,1,0:T(8,128)(2,1)S(1)}, bf16[3,160,640]{2,1,0:T(8,128)(2,1)S(1)}, u32[]{:S(2)}, u32[]{:S(2)}) collective-permute-start(bf16[3,160,640]{2,1,0:T(8,128)(2,1)S(1)} %collective-permute-done.1.below), channel_id=1, source_target_pairs={{0,2},{2,4},{4,6},{6,0},{1,3},{3,5},{5,7},{7,1},{8,10},{10,12},{12... | collective-permute-start | bytes 1843208 | tf_op jit(solution)/shard_map/ppermute | solution.py:35
  40.4 17.2 %collective-permute-start.6 = (bf16[3,160,640]{2,1,0:T(8,128)(2,1)S(1)}, bf16[3,160,640]{2,1,0:T(8,128)(2,1)S(1)}, u32[]{:S(2)}, u32[]{:S(2)}) collective-permute-start(bf16[3,160,640]{2,1,0:T(8,128)(2,1)S(1)} %collective-permute-done.4.above2), channel_id=1, source_target_pairs={{0,6},{2,0},{4,2},{6,4},{1,7},{3,1},{5,3},{7,5},{8,14},{10,8},{12,... | collective-permute-start | bytes 1843208 | tf_op jit(solution)/shard_map/ppermute | solution.py:35
  61.8 1.3 copy-start.4
  63.1 0.9 copy-start.9
  64.0 16.8 %copy-start.19 = (s32[176]{0:T(256)S(1)}, s32[176]{0:T(256)}, u32[]{:S(2)}) copy-start(s32[176]{0:T(256)} %tmap.1) | copy-start | bytes 2116
  64.0 12.1 %collective-permute-start.7 = (bf16[352,640]{1,0:T(8,128)(2,1)}, bf16[352,640]{1,0:T(8,128)(2,1)S(1)}, u32[]{:S(2)}, u32[]{:S(2)}) collective-permute-start(bf16[352,640]{1,0:T(8,128)(2,1)} %get-tuple-element.158), channel_id=1, source_target_pairs={{0,1},{1,0},{2,3},{3,2},{4,5},{5,4},{6,7},{7,6},{8,9},{9,8},{10,11... | collective-permute-start | bytes 1351688 | tf_op jit(solution)/shard_map/ppermute | solution.py:31
  76.1 0.8 copy-start.11
  76.9 1.0 copy-start.3
  77.9 1.2 copy-start.10
  79.1 1.0 copy-start.12
  80.8 6.2 %collective-permute-start.8 = (bf16[11,32,640]{2,1,0:T(8,128)(2,1)S(1)}, bf16[11,32,640]{2,1,0:T(8,128)(2,1)S(1)}, u32[]{:S(2)}, u32[]{:S(2)}) collective-permute-start(bf16[11,32,640]{2,1,0:T(8,128)(2,1)S(1)} %shard_map.140.own), channel_id=1, source_target_pairs={{0,8},{8,0},{1,9},{9,1},{2,10},{10,2},{3,11},{11,3},{4,12},{12,4},... | collective-permute-start | bytes 1351688 | tf_op jit(solution)/shard_map/ppermute | solution.py:31
  88.4 64.4 %all-to-all-start.1 = ((bf16[32,32,640]{2,1,0:T(8,128)(2,1)}), bf16[32,32,640]{2,1,0:T(8,128)(2,1)}, u32[]{:S(2)}, u32[]{:S(2)}) async-start(bf16[32,32,640]{2,1,0:T(8,128)(2,1)} %pack.1), calls=%async_computation.1 | async-start | bytes 2621440 | tf_op jit(solution)/shard_map/all_to_all | solution.py:470
  96.2 4.2 %copy-start.1 = (bf16[3,3,8,40,320]{4,3,2,1,0:T(8,128)(2,1)S(1)}, bf16[3,3,8,40,320]{4,3,2,1,0:T(8,128)(2,1)}, u32[]{:S(2)}) copy-start(bf16[3,3,8,40,320]{4,3,2,1,0:T(8,128)(2,1)} %copy-done) | copy-start | bytes 5529604
  96.2 1.6 copy-start.5
  100.1 5.7 %collective-permute-start.12 = (bf16[25,40,320]{2,1,0:T(8,128)(2,1)S(1)}, bf16[25,40,320]{2,1,0:T(8,128)(2,1)S(1)}, u32[]{:S(2)}, u32[]{:S(2)}) collective-permute-start(bf16[25,40,320]{2,1,0:T(8,128)(2,1)S(1)} %get-tuple-element.171), channel_id=1, source_target_pairs={{0,8},{8,0},{1,9},{9,1},{2,10},{10,2},{3,11},{11,3},{4,12},{12,4},... | collective-permute-start | bytes 1920008 | tf_op jit(solution)/shard_map/ppermute | solution.py:31
  102.5 31.0 %collective-permute-start.10 = (bf16[3,8,40,320]{3,2,1,0:T(8,128)(2,1)S(1)}, bf16[3,8,40,320]{3,2,1,0:T(8,128)(2,1)S(1)}, u32[]{:S(2)}, u32[]{:S(2)}) collective-permute-start(bf16[3,8,40,320]{3,2,1,0:T(8,128)(2,1)S(1)} %get-tuple-element.166), channel_id=1, source_target_pairs={{0,2},{2,4},{4,6},{6,0},{1,3},{3,5},{5,7},{7,1},{8,10},{10,12},{12... | collective-permute-start | bytes 1843208 | tf_op jit(solution)/shard_map/ppermute | solution.py:35
  102.7 30.8 %collective-permute-start.11 = (bf16[3,8,40,320]{3,2,1,0:T(8,128)(2,1)S(1)}, bf16[3,8,40,320]{3,2,1,0:T(8,128)(2,1)S(1)}, u32[]{:S(2)}, u32[]{:S(2)}) collective-permute-start(bf16[3,8,40,320]{3,2,1,0:T(8,128)(2,1)S(1)} %get-tuple-element.167), channel_id=1, source_target_pairs={{0,6},{2,0},{4,2},{6,4},{1,7},{3,1},{5,3},{7,5},{8,14},{10,8},{12,... | collective-permute-start | bytes 1843208 | tf_op jit(solution)/shard_map/ppermute | solution.py:35
  106.7 5.6 %collective-permute-start.13 = (f32[8,320]{1,0:T(8,128)S(1)}, f32[8,320]{1,0:T(8,128)S(1)}, u32[]{:S(2)}, u32[]{:S(2)}) collective-permute-start(f32[8,320]{1,0:T(8,128)S(1)} %get-tuple-element.172), channel_id=1, source_target_pairs={{0,1},{1,0},{2,3},{3,2},{4,5},{5,4},{6,7},{7,6},{8,9},{9,8},{10,11... | collective-permute-start | bytes 30728 | tf_op jit(solution)/shard_map/ppermute | solution.py:31
  112.4 9.3 %collective-permute-start.14 = (f32[8,320]{1,0:T(8,128)S(1)}, f32[8,320]{1,0:T(8,128)S(1)}, u32[]{:S(2)}, u32[]{:S(2)}) collective-permute-start(f32[8,320]{1,0:T(8,128)S(1)} %add.70), channel_id=1, source_target_pairs={{0,2},{2,0},{4,6},{6,4},{1,3},{3,1},{5,7},{7,5},{8,10},{10,8},{12,... | collective-permute-start | bytes 30728 | tf_op jit(solution)/shard_map/ppermute | solution.py:453
  112.5 12.7 %collective-permute-start.19 = (bf16[2,16,8,320]{3,2,1,0:T(8,128)(2,1)S(1)}, bf16[2,16,8,320]{3,2,1,0:T(8,128)(2,1)S(1)}, u32[]{:S(2)}, u32[]{:S(2)}) collective-permute-start(bf16[2,16,8,320]{3,2,1,0:T(8,128)(2,1)S(1)} %get-tuple-element.178), channel_id=1, source_target_pairs={{0,16},{16,32},{32,48},{48,0},{1,17},{17,33},{33,49},{49,1},{2,18}... | collective-permute-start | bytes 491528 | tf_op jit(solution)/shard_map/ppermute | solution.py:35
  114.2 13.5 %collective-permute-start.20 = (bf16[2,16,8,320]{3,2,1,0:T(8,128)(2,1)S(1)}, bf16[2,16,8,320]{3,2,1,0:T(8,128)(2,1)S(1)}, u32[]{:S(2)}, u32[]{:S(2)}) collective-permute-start(bf16[2,16,8,320]{3,2,1,0:T(8,128)(2,1)S(1)} %get-tuple-element.179), channel_id=1, source_target_pairs={{0,48},{16,0},{32,16},{48,32},{1,49},{17,1},{33,17},{49,33},{2,50}... | collective-permute-start | bytes 491528 | tf_op jit(solution)/shard_map/ppermute | solution.py:35
  121.7 8.2 %collective-permute-start.21 = (bf16[2,16,8,320]{3,2,1,0:T(8,128)(2,1)S(1)}, bf16[2,16,8,320]{3,2,1,0:T(8,128)(2,1)S(1)}, u32[]{:S(2)}, u32[]{:S(2)}) collective-permute-start(bf16[2,16,8,320]{3,2,1,0:T(8,128)(2,1)S(1)} %get-tuple-element.180), channel_id=1, source_target_pairs={{0,32},{16,48},{32,0},{48,16},{1,33},{17,49},{33,1},{49,17},{2,34}... | collective-permute-start | bytes 491528 | tf_op jit(solution)/shard_map/ppermute | solution.py:35
  125.2 8.3 %collective-permute-start.15 = (f32[8,320]{1,0:T(8,128)S(1)}, f32[8,320]{1,0:T(8,128)S(1)}, u32[]{:S(2)}, u32[]{:S(2)}) collective-permute-start(f32[8,320]{1,0:T(8,128)S(1)} %add.71.near), channel_id=1, source_target_pairs={{0,6},{6,0},{2,4},{4,2},{1,7},{7,1},{3,5},{5,3},{8,14},{14,8},{10,... | collective-permute-start | bytes 30728 | tf_op jit(solution)/shard_map/ppermute | solution.py:454
  129.9 11.4 %collective-permute-start.22 = (bf16[2,16,8,320]{3,2,1,0:T(8,128)(2,1)S(1)}, bf16[2,16,8,320]{3,2,1,0:T(8,128)(2,1)S(1)}, u32[]{:S(2)}, u32[]{:S(2)}) collective-permute-start(bf16[2,16,8,320]{3,2,1,0:T(8,128)(2,1)S(1)} %shard_map.146), channel_id=1, source_target_pairs={{0,4},{2,6},{4,0},{6,2},{1,5},{3,7},{5,1},{7,3},{8,12},{10,14},{12... | collective-permute-start | bytes 491528 | tf_op jit(solution)/shard_map/ppermute | solution.py:35
  135.3 0.7 copy-start.14
  136.1 9.2 %collective-permute-start.16 = (bf16[2,16,8,320]{3,2,1,0:T(8,128)(2,1)}, bf16[2,16,8,320]{3,2,1,0:T(8,128)(2,1)S(1)}, u32[]{:S(2)}, u32[]{:S(2)}) collective-permute-start(bf16[2,16,8,320]{3,2,1,0:T(8,128)(2,1)} %get-tuple-element.174), channel_id=1, source_target_pairs={{0,16},{16,32},{32,48},{48,0},{1,17},{17,33},{33,49},{49,1},{2,18}... | collective-permute-start | bytes 491528 | tf_op jit(solution)/shard_map/ppermute | solution.py:35
  137.8 8.6 %collective-permute-start.17 = (bf16[2,16,8,320]{3,2,1,0:T(8,128)(2,1)}, bf16[2,16,8,320]{3,2,1,0:T(8,128)(2,1)S(1)}, u32[]{:S(2)}, u32[]{:S(2)}) collective-permute-start(bf16[2,16,8,320]{3,2,1,0:T(8,128)(2,1)} %get-tuple-element.175), channel_id=1, source_target_pairs={{0,48},{16,0},{32,16},{48,32},{1,49},{17,1},{33,17},{49,33},{2,50}... | collective-permute-start | bytes 491528 | tf_op jit(solution)/shard_map/ppermute | solution.py:35
  139.3 8.6 %collective-permute-start.18 = (bf16[2,16,8,320]{3,2,1,0:T(8,128)(2,1)}, bf16[2,16,8,320]{3,2,1,0:T(8,128)(2,1)S(1)}, u32[]{:S(2)}, u32[]{:S(2)}) collective-permute-start(bf16[2,16,8,320]{3,2,1,0:T(8,128)(2,1)} %get-tuple-element.176), channel_id=1, source_target_pairs={{0,32},{16,48},{32,0},{48,16},{1,33},{17,49},{33,1},{49,17},{2,34}... | collective-permute-start | bytes 491528 | tf_op jit(solution)/shard_map/ppermute | solution.py:35
  147.9 1.0 copy-start.15
  149.6 6.2 %collective-permute-start.23 = (bf16[16,8,320]{2,1,0:T(8,128)(2,1)S(1)}, bf16[16,8,320]{2,1,0:T(8,128)(2,1)S(1)}, u32[]{:S(2)}, u32[]{:S(2)}) collective-permute-start(bf16[16,8,320]{2,1,0:T(8,128)(2,1)S(1)} %get-tuple-element.182), channel_id=1, source_target_pairs={{0,64},{64,0},{1,65},{65,1},{2,66},{66,2},{3,67},{67,3},{4,68},{68... | collective-permute-start | bytes 245768 | tf_op jit(solution)/shard_map/ppermute | solution.py:31
  159.4 14.7 %all-to-all-start = ((bf16[8,32,640]{2,1,0:T(8,128)(2,1)}), bf16[8,32,640]{2,1,0:T(8,128)(2,1)S(1)}, u32[]{:S(2)}, u32[]{:S(2)}) async-start(bf16[8,32,640]{2,1,0:T(8,128)(2,1)} %broadcast_select_fusion.3), calls=%async_computation | async-start | bytes 655360 | tf_op jit(solution)/shard_map/while/body/all_to_all | solution.py:470
  175.9 0.8 copy-start.20

commit v6 on v5

--- a/solution.py
+++ b/solution.py
@@ -33,6 +33,10 @@
 
 def ring(x, axis, step):
     return lax.ppermute(x, axis, [(i, (i + step) % 4) for i in range(4)])
+
+
+def in_hbm(x):
+    return pltpu.with_memory_space_constraint(x, HBM)
 
 
 def grant(mib):
@@ -105,8 +109,28 @@
     )(meta, trunc, tmap)
 
 
-def halves(c, *weights):
-    return jnp.stack([lax.dynamic_slice_in_dim(w, c * 160, 160, 0) for w in weights])
+def halves_kernel(meta, wv, wg, wo, half, sems):
+    start = pl.multiple_of(meta[1] * 160, 16)
+    copies = [
+        pltpu.make_async_copy(w.at[pl.ds(start, 160), :], half.at[j], sems.at[j])
+        for j, w in enumerate((wv, wg, wo))
+    ]
+    for copy in copies:
+        copy.start()
+    for copy in copies:
+        copy.wait()
+
+
+def halves(meta, *weights):
+    return pl.pallas_call(
+        halves_kernel,
+        out_shape=jax.ShapeDtypeStruct((3, 160, 640), BF),
+        in_specs=smem(1) + [pl.BlockSpec(memory_space=HBM)] * 3,
+        out_specs=vmem(1)[0],
+        scratch_shapes=[pltpu.SemaphoreType.DMA((3,))],
+        compiler_params=grant(4),
+        name="halves",
+    )(meta, *(in_hbm(w) for w in weights))
 
 
 def normalise(tile):
@@ -134,7 +158,7 @@
         out_specs=vmem(1)[0],
         compiler_params=grant(10),
         name="prologue",
-    )(meta, trunc, times, table, lat, cot, gain)
+    )(meta, *(in_hbm(x) for x in (trunc, times, table, lat, cot)), gain)
 
 
 LAST = (((1,), (1,)), ((), ()))
@@ -269,8 +293,8 @@
         w[j, pl.ds(there, 160)] = second[j]
     hidden_part(rows, w, acts, 0, 320)
     total = near_dn[...] + dot(acts[0], w[0]) + dot(acts[1], w[1])
-    dn[...] = total[:352]
-    dn_send[...] = total[352:].astype(BF)
+    dn[...] = total[:352].reshape(11, 32, 640)
+    dn_send[...] = total[352:].reshape(11, 32, 640).astype(BF)
     gsum = jnp.sum(total * rows[0].astype(F32), axis=0, keepdims=True) / gain[...]
     tail[...] = split_gain(gsum)
 
@@ -278,7 +302,7 @@
 def far_forward(meta, *arrays):
     return local(
         far_kernel, 14,
-        (((352, 640), F32), ((352, 640), BF), ((3, 704, 320), BF), ((8, 320), F32)),
+        (((11, 32, 640), F32), ((11, 32, 640), BF), ((3, 704, 320), BF), ((8, 320), F32)),
         arrays, [((3, 320, 640), BF)], (meta,),
     )
 
@@ -302,7 +326,7 @@
     )
 
 
-def finish_kernel(alive, dn, got, lat, grad, gain, own):
+def finish_kernel(meta, trunc, dn, got, lat, grad, gain, own):
     for k in range(11):
         x_hat, inv_std = normalise(lat[k])
         d_hat = (dn[k] + got[k].astype(F32)) * gain[...]
@@ -311,11 +335,11 @@
             - jnp.mean(d_hat, axis=-1, keepdims=True)
             - x_hat * jnp.mean(d_hat * x_hat, axis=-1, keepdims=True)
         )
-        own[k] = jnp.where(k < alive[0], out, 0.0).astype(BF)
-
-
-def finish(alive, *arrays):
-    return local(finish_kernel, 10, (((11, 32, 640), BF),), arrays, (), (alive,))[0]
+        own[k] = jnp.where(k < trunc[meta[0]] - 29, out, 0.0).astype(BF)
+
+
+def finish(meta, trunc, *arrays):
+    return local(finish_kernel, 10, (((11, 32, 640), BF),), arrays, (), (meta, trunc))[0]
 
 
 def pack_kernel(dest_g, dest_r, own, peer, packed, sems):
@@ -428,7 +452,10 @@
 
 
 def over_ring(up, down, far):
-    return ring(up, "z", 1), ring(down, "z", -1), ring(far, "z", 2)
+    up = ring(up, "z", 1)
+    down = ring(down, "z", -1)
+    far = ring(far, "z", 2)
+    return up, down, far
 
 
 def reduce_weights(meta, near_mine, near_got, far_mine, far_got):
@@ -491,7 +518,7 @@
     meta = jnp.stack([lax.axis_index(a) for a in (DP, "c", "z", "xh")]).astype(jnp.int32)
     gain = gain[None, :]
     wv, wg, wo = w_value.T, w_gate.T, w_out.T
-    half = halves(lax.axis_index("c"), wv, wg, wo)
+    half = halves(meta, wv, wg, wo)
     below = ring(half, "y", 1)
     above = ring(half, "y", -1)
     rows = prologue(meta, trunc, times, noise_table(), latents, cotangent, gain)
@@ -511,9 +538,7 @@
     got = swap(dn_send, "xl")
     far_mine, far_send = far_grads(meta, turned, far_acts, tail)
     far_got = swap(far_send, "c")
-    tiles = (11, 32, 640)
-    alive = lax.dynamic_slice_in_dim(trunc, lax.axis_index(DP), 1) - 29
-    own = finish(alive, dn.reshape(tiles), got.reshape(tiles), latents, rows, gain)
+    own = finish(meta, trunc, dn, got, latents, rows, gain)
     peer = swap(own, "c")
     packed = pack(dest_g, dest_r, own, peer)
     came = route(packed)

time: 177 us -> 174 us (0.983)
  local copies, waits for them, and re-layouts: 15.9 us -> 11.1 us
    unnamed x44 -> x38, local copies, waits for them, and re-layouts: 11.3 us -> 7.31 us
    another operation x2 -> x0, local copies, waits for them, and re-layouts: 2.17 us -> none  [halves(): jnp.stack([lax.dynamic_slice_in_dim(w, c * 160, 160, 0) for w in weights])]
  transfers between devices with their start and end apart: 26 -> 26, of which waited for: 15 -> 14; matrix products, arithmetic and copies ran while one was open for 0% -> 1% of each run, Pallas kernels for 16% -> 16%
where the time goes in v6:
time: 174 us
  waiting for transfers between devices  68.9 us (40%)
  starting transfers between devices  49.4 us (28%)
  Pallas kernels  39.5 us (23%)
  local copies, waits for them, and re-layouts  11.1 us (6%)
  other arithmetic  2.53 us (1%)
    ppermute x13, waiting for transfers between devices, ring(): return lax.ppermute(x, axis, [(i, (i + step) % 4) for i in range(4)])  32.7 us
    pallas_call x12, Pallas kernels, local(): pl.pallas_call(kernel, out_shape=tuple((jax.ShapeDtypeStruct(s, d) for s,...  27.4 us
    ppermute x13, starting transfers between devices, ring(): return lax.ppermute(x, axis, [(i, (i + step) % 4) for i in range(4)])  25.5 us
    ppermute x9, waiting for transfers between devices, swap(): return lax.ppermute(x, axis, [(0, 1), (1, 0)])  21.2 us
    all_to_all x2, starting transfers between devices, route(): return lax.all_to_all(packed, CHIP, 0, 0, tiled=True)  13.5 us
    all_to_all x2, waiting for transfers between devices, route(): return lax.all_to_all(packed, CHIP, 0, 0, tiled=True)  8.96 us
    ppermute x9, starting transfers between devices, swap(): return lax.ppermute(x, axis, [(0, 1), (1, 0)])  7.83 us
    unnamed x38, local copies, waits for them, and re-layouts  7.31 us
  transfers between devices with their start and end apart: 26, of which 14 were waited for; matrix products, arithmetic and copies ran while one was open for 1% of the time, Pallas kernels for 16%

profile of v6, /device:TPU:0, one launch (start us, length us, event | category | flops | bytes accessed | tf_op | source)
XLA Modules:
  0.0 173.7 jit_solution(1593345776927653251)
XLA Ops:
  0.8 1.7 halves.1
  2.5 1.8 %collective-permute-start.1 = (bf16[3,160,640]{2,1,0:T(8,128)(2,1)S(1)}, bf16[3,160,640]{2,1,0:T(8,128)(2,1)S(1)}, u32[]{:S(2)}, u32[]{:S(2)}) collective-permute-start(bf16[3,160,640]{2,1,0:T(8,128)(2,1)S(1)} %halves.1), channel_id=1, source_target_pairs={{0,2},{2,4},{4,6},{6,0},{1,3},{3,5},{5,7},{7,1},{8,10},{10,12},{12... | collective-permute-start | bytes 1843208 | tf_op jit(solution)/shard_map/ppermute | solution.py:35
  4.2 1.5 collective-permute-start.3
  6.5 1.6 prologue.1.grad
  8.0 1.7 collective-permute-start
  9.7 9.8 %collective-permute-done.1.below = bf16[3,160,640]{2,1,0:T(8,128)(2,1)S(1)} collective-permute-done((bf16[3,160,640]{2,1,0:T(8,128)(2,1)S(1)}, bf16[3,160,640]{2,1,0:T(8,128)(2,1)S(1)}, u32[]{:S(2)}, u32[]{:S(2)}) %collective-permute-start.1) | collective-permute-done | bytes 614432 | tf_op jit(solution)/shard_map/ppermute | solution.py:35
  20.0 1.5 collective-permute-done.2.below2
  22.4 4.3 %shard_map.137 = (f32[352,640]{1,0:T(8,128)S(1)}, bf16[3,352,960]{2,1,0:T(8,128)(2,1)S(1)}, bf16[3,960,640]{2,1,0:T(8,128)(2,1)S(1)}) custom-call(s32[4]{0:T(128)S(1)} %pad_add_fusion.meta, bf16[2,352,640]{2,1,0:T(8,128)(2,1)S(1)} %bitcast.27, bf16[320,640]{1,0:T(8,128)(2,1)S(1)} %bitcast.30, bf16[320,640]{1,0:T(8,128)(2,1)S(1)} %bitcast.32, ...), custom_call_target="tpu_custom_call" | custom-call | tf_op jit(solution)/shard_map/pallas_call | solution.py:186
  26.8 2.7 %collective-permute-done = bf16[2,11,32,640]{3,2,1,0:T(8,128)(2,1)S(1)} collective-permute-done((bf16[2,11,32,640]{3,2,1,0:T(8,128)(2,1)S(1)}, bf16[2,11,32,640]{3,2,1,0:T(8,128)(2,1)S(1)}, u32[]{:S(2)}, u32[]{:S(2)}) %collective-permute-start) | collective-permute-done | bytes 901152 | tf_op jit(solution)/shard_map/ppermute | solution.py:31
  29.5 3.8 %shard_map.138 = (f32[704,640]{1,0:T(8,128)S(1)}, bf16[3,704,960]{2,1,0:T(8,128)(2,1)S(1)}, bf16[2,704,640]{2,1,0:T(8,128)(2,1)S(1)}, bf16[2,640,704]{2,1,0:T(8,128)(2,1)S(1)}) custom-call(bf16[2,352,640]{2,1,0:T(8,128)(2,1)S(1)} %bitcast.28, bf16[2,352,640]{2,1,0:T(8,128)(2,1)S(1)} %bitcast.35, f32[352,640]{1,0:T(8,128)S(1)} %get-tuple-element.152.own_dn, ...), custom_call_target="tpu_custom_call" | custom-call | tf_op jit(solution)/shard_map/pallas_call | solution.py:186
  33.4 5.7 %shard_map.141 = (bf16[3,3,8,40,320]{4,3,2,1,0:T(8,128)(2,1)S(1)}, bf16[3,3,8,40,320]{4,3,2,1,0:T(8,128)(2,1)}) custom-call(s32[4]{0:T(128)S(1)} %pad_add_fusion.meta, bf16[2,640,704]{2,1,0:T(8,128)(2,1)S(1)} %get-tuple-element.161.turned, bf16[3,704,960]{2,1,0:T(8,128)(2,1)S(1)} %get-tuple-element.162.acts), custom_call_target="tpu_custom_call" | custom-call | tf_op jit(solution)/shard_map/pallas_call | solution.py:186
  39.3 3.0 %collective-permute-start.6 = (bf16[3,160,640]{2,1,0:T(8,128)(2,1)S(1)}, bf16[3,160,640]{2,1,0:T(8,128)(2,1)S(1)}, u32[]{:S(2)}, u32[]{:S(2)}) collective-permute-start(bf16[3,160,640]{2,1,0:T(8,128)(2,1)S(1)} %collective-permute-done.4.above2), channel_id=1, source_target_pairs={{0,6},{2,0},{4,2},{6,4},{1,7},{3,1},{5,3},{7,5},{8,14},{10,8},{12,... | collective-permute-start | bytes 1843208 | tf_op jit(solution)/shard_map/ppermute | solution.py:35
  42.3 14.2 %collective-permute-done.5.first = bf16[3,160,640]{2,1,0:T(8,128)(2,1)S(1)} collective-permute-done((bf16[3,160,640]{2,1,0:T(8,128)(2,1)S(1)}, bf16[3,160,640]{2,1,0:T(8,128)(2,1)S(1)}, u32[]{:S(2)}, u32[]{:S(2)}) %collective-permute-start.5) | collective-permute-done | bytes 614432 | tf_op jit(solution)/shard_map/ppermute | solution.py:35
  56.6 3.6 %shard_map.139 = (f32[11,32,640]{2,1,0:T(8,128)S(1)}, bf16[11,32,640]{2,1,0:T(8,128)(2,1)S(1)}, bf16[3,704,320]{2,1,0:T(8,128)(2,1)S(1)}, f32[8,320]{1,0:T(8,128)S(1)}) custom-call(s32[4]{0:T(128)S(1)} %pad_add_fusion.meta, bf16[2,704,640]{2,1,0:T(8,128)(2,1)S(1)} %get-tuple-element.155.rows, f32[1,640]{1,0:T(1,128)S(1)} %broadcast_in_dim.67.gain, ...), custom_call_target="tpu_custom_call" | custom-call | tf_op jit(solution)/shard_map/pallas_call | solution.py:186
  60.2 1.6 collective-permute-start.7
  61.8 10.4 %collective-permute-done.7.got = bf16[11,32,640]{2,1,0:T(8,128)(2,1)S(1)} collective-permute-done((bf16[11,32,640]{2,1,0:T(8,128)(2,1)S(1)}, bf16[11,32,640]{2,1,0:T(8,128)(2,1)S(1)}, u32[]{:S(2)}, u32[]{:S(2)}) %collective-permute-start.7) | collective-permute-done | bytes 450592 | tf_op jit(solution)/shard_map/ppermute | solution.py:31
  72.2 1.2 shard_map.140.own
  73.5 6.1 %routes.1 = (s32[22]{0:T(128)S(1)}, s32[22]{0:T(128)S(1)}, s32[11]{0:T(128)S(1)}, s32[11]{0:T(128)S(1)}, s32[1]{0:T(128)}) custom-call(s32[4]{0:T(128)S(1)} %pad_add_fusion.meta, s32[16]{0:T(128)S(1)} %copy-done.16, s32[176]{0:T(256)S(1)} %copy-done.17), custom_call_target="tpu_custom_call" | custom-call | tf_op jit(solution)/shard_map/routes/pallas_call | solution.py:101
  79.6 1.5 pack.1
  82.7 7.8 %all-to-all-start.1 = ((bf16[32,32,640]{2,1,0:T(8,128)(2,1)}), bf16[32,32,640]{2,1,0:T(8,128)(2,1)S(1)}, u32[]{:S(2)}, u32[]{:S(2)}) async-start(bf16[32,32,640]{2,1,0:T(8,128)(2,1)} %pack.1), calls=%async_computation.1 | async-start | bytes 2621440 | tf_op jit(solution)/shard_map/all_to_all | solution.py:497
  90.4 1.6 copy-done.11
  92.0 2.3 %shard_map.143 = (bf16[25,40,320]{2,1,0:T(8,128)(2,1)S(1)}, bf16[25,40,320]{2,1,0:T(8,128)(2,1)S(1)}) custom-call(s32[4]{0:T(128)S(1)} %pad_add_fusion.meta, bf16[2,640,704]{2,1,0:T(8,128)(2,1)S(1)} %get-tuple-element.161.turned, bf16[3,704,320]{2,1,0:T(8,128)(2,1)S(1)} %copy-done.11, f32[8,320]{1,0:T(8,128)S(1)} %get-tuple-element.169.tail), custom_call_target="tpu_custom_call" | custom-call | tf_op jit(solution)/shard_map/pallas_call | solution.py:186
  94.6 2.1 %shard_map.142 = (f32[3,8,40,320]{3,2,1,0:T(8,128)S(1)}, bf16[3,8,40,320]{3,2,1,0:T(8,128)(2,1)S(1)}, bf16[3,8,40,320]{3,2,1,0:T(8,128)(2,1)S(1)}) custom-call(bf16[3,3,8,40,320]{4,3,2,1,0:T(8,128)(2,1)S(1)} %copy-done.3, bf16[3,3,8,40,320]{4,3,2,1,0:T(8,128)(2,1)} %collective-permute-done.9.got), custom_call_target="tpu_custom_call" | custom-call | tf_op jit(solution)/shard_map/pallas_call | solution.py:186
  96.8 3.2 %collective-permute-start.11 = (bf16[3,8,40,320]{3,2,1,0:T(8,128)(2,1)S(1)}, bf16[3,8,40,320]{3,2,1,0:T(8,128)(2,1)S(1)}, u32[]{:S(2)}, u32[]{:S(2)}) collective-permute-start(bf16[3,8,40,320]{3,2,1,0:T(8,128)(2,1)S(1)} %get-tuple-element.167), channel_id=1, source_target_pairs={{0,6},{2,0},{4,2},{6,4},{1,7},{3,1},{5,3},{7,5},{8,14},{10,8},{12,... | collective-permute-start | bytes 1843208 | tf_op jit(solution)/shard_map/ppermute | solution.py:35
  101.6 5.0 %collective-permute-done.13 = f32[8,320]{1,0:T(8,128)S(1)} collective-permute-done((f32[8,320]{1,0:T(8,128)S(1)}, f32[8,320]{1,0:T(8,128)S(1)}, u32[]{:S(2)}, u32[]{:S(2)}) %collective-permute-start.13) | collective-permute-done | bytes 10272 | tf_op jit(solution)/shard_map/ppermute | solution.py:31
  106.6 1.7 %collective-permute-start.19 = (bf16[2,16,8,320]{3,2,1,0:T(8,128)(2,1)S(1)}, bf16[2,16,8,320]{3,2,1,0:T(8,128)(2,1)S(1)}, u32[]{:S(2)}, u32[]{:S(2)}) collective-permute-start(bf16[2,16,8,320]{3,2,1,0:T(8,128)(2,1)S(1)} %get-tuple-element.178), channel_id=1, source_target_pairs={{0,16},{16,32},{32,48},{48,0},{1,17},{17,33},{33,49},{49,1},{2,18}... | collective-permute-start | bytes 491528 | tf_op jit(solution)/shard_map/ppermute | solution.py:35
  108.4 1.5 collective-permute-start.20
  109.9 6.0 %collective-permute-done.14 = f32[8,320]{1,0:T(8,128)S(1)} collective-permute-done((f32[8,320]{1,0:T(8,128)S(1)}, f32[8,320]{1,0:T(8,128)S(1)}, u32[]{:S(2)}, u32[]{:S(2)}) %collective-permute-start.14) | collective-permute-done | bytes 10272 | tf_op jit(solution)/shard_map/ppermute | solution.py:480
  115.9 3.5 %collective-permute-start.21 = (bf16[2,16,8,320]{3,2,1,0:T(8,128)(2,1)S(1)}, bf16[2,16,8,320]{3,2,1,0:T(8,128)(2,1)S(1)}, u32[]{:S(2)}, u32[]{:S(2)}) collective-permute-start(bf16[2,16,8,320]{3,2,1,0:T(8,128)(2,1)S(1)} %get-tuple-element.180), channel_id=1, source_target_pairs={{0,32},{16,48},{32,0},{48,16},{1,33},{17,49},{33,1},{49,17},{2,34}... | collective-permute-start | bytes 491528 | tf_op jit(solution)/shard_map/ppermute | solution.py:35
  119.4 2.6 %collective-permute-start.15 = (f32[8,320]{1,0:T(8,128)S(1)}, f32[8,320]{1,0:T(8,128)S(1)}, u32[]{:S(2)}, u32[]{:S(2)}) collective-permute-start(f32[8,320]{1,0:T(8,128)S(1)} %add.58.near), channel_id=1, source_target_pairs={{0,6},{6,0},{2,4},{4,2},{1,7},{7,1},{3,5},{5,3},{8,14},{14,8},{10,... | collective-permute-start | bytes 30728 | tf_op jit(solution)/shard_map/ppermute | solution.py:481
  122.0 2.1 %collective-permute-done.21.far = bf16[2,16,8,320]{3,2,1,0:T(8,128)(2,1)S(1)} collective-permute-done((bf16[2,16,8,320]{3,2,1,0:T(8,128)(2,1)S(1)}, bf16[2,16,8,320]{3,2,1,0:T(8,128)(2,1)S(1)}, u32[]{:S(2)}, u32[]{:S(2)}) %collective-permute-start.21) | collective-permute-done | bytes 163872 | tf_op jit(solution)/shard_map/ppermute | solution.py:35
  124.2 3.6 %collective-permute-start.22 = (bf16[2,16,8,320]{3,2,1,0:T(8,128)(2,1)S(1)}, bf16[2,16,8,320]{3,2,1,0:T(8,128)(2,1)S(1)}, u32[]{:S(2)}, u32[]{:S(2)}) collective-permute-start(bf16[2,16,8,320]{3,2,1,0:T(8,128)(2,1)S(1)} %shard_map.146), channel_id=1, source_target_pairs={{0,4},{2,6},{4,0},{6,2},{1,5},{3,7},{5,1},{7,3},{8,12},{10,14},{12... | collective-permute-start | bytes 491528 | tf_op jit(solution)/shard_map/ppermute | solution.py:35
  127.8 1.8 %shard_map.145 = (f32[2,16,8,320]{3,2,1,0:T(8,128)S(1)}, bf16[2,16,8,320]{3,2,1,0:T(8,128)(2,1)}, bf16[2,16,8,320]{3,2,1,0:T(8,128)(2,1)}, bf16[2,16,8,320]{3,2,1,0:T(8,128)(2,1)}) custom-call(s32[4]{0:T(128)S(1)} %pad_add_fusion.meta, f32[3,8,40,320]{3,2,1,0:T(8,128)S(1)} %get-tuple-element.165.own, ...), custom_call_target="tpu_custom_call" | custom-call | tf_op jit(solution)/shard_map/pallas_call | solution.py:186
  130.3 1.7 %collective-permute-start.16 = (bf16[2,16,8,320]{3,2,1,0:T(8,128)(2,1)}, bf16[2,16,8,320]{3,2,1,0:T(8,128)(2,1)S(1)}, u32[]{:S(2)}, u32[]{:S(2)}) collective-permute-start(bf16[2,16,8,320]{3,2,1,0:T(8,128)(2,1)} %get-tuple-element.174), channel_id=1, source_target_pairs={{0,16},{16,32},{32,48},{48,0},{1,17},{17,33},{33,49},{49,1},{2,18}... | collective-permute-start | bytes 491528 | tf_op jit(solution)/shard_map/ppermute | solution.py:35
  132.1 1.5 collective-permute-start.17
  133.6 2.0 %collective-permute-start.18 = (bf16[2,16,8,320]{3,2,1,0:T(8,128)(2,1)}, bf16[2,16,8,320]{3,2,1,0:T(8,128)(2,1)S(1)}, u32[]{:S(2)}, u32[]{:S(2)}) collective-permute-start(bf16[2,16,8,320]{3,2,1,0:T(8,128)(2,1)} %get-tuple-element.176), channel_id=1, source_target_pairs={{0,32},{16,48},{32,0},{48,16},{1,33},{17,49},{33,1},{49,17},{2,34}... | collective-permute-start | bytes 491528 | tf_op jit(solution)/shard_map/ppermute | solution.py:35
  135.6 3.9 %collective-permute-done.16.down = bf16[2,16,8,320]{3,2,1,0:T(8,128)(2,1)S(1)} collective-permute-done((bf16[2,16,8,320]{3,2,1,0:T(8,128)(2,1)}, bf16[2,16,8,320]{3,2,1,0:T(8,128)(2,1)S(1)}, u32[]{:S(2)}, u32[]{:S(2)}) %collective-permute-start.16) | collective-permute-done | bytes 163872 | tf_op jit(solution)/shard_map/ppermute | solution.py:35
  139.5 1.1 collective-permute-done.17.up
  140.7 1.5 collective-permute-done.18.far
  142.9 1.0 copy-done.13
  143.9 0.9 copy-done.15
  145.5 3.0 %collective-permute-start.23 = (bf16[16,8,320]{2,1,0:T(8,128)(2,1)S(1)}, bf16[16,8,320]{2,1,0:T(8,128)(2,1)S(1)}, u32[]{:S(2)}, u32[]{:S(2)}) collective-permute-start(bf16[16,8,320]{2,1,0:T(8,128)(2,1)S(1)} %get-tuple-element.182), channel_id=1, source_target_pairs={{0,64},{64,0},{1,65},{65,1},{2,66},{66,2},{3,67},{67,3},{4,68},{68... | collective-permute-start | bytes 245768 | tf_op jit(solution)/shard_map/ppermute | solution.py:31
  148.6 1.1 pad_maximum_fusion
  149.6 1.4 unpack.1
  153.1 19.8 %while.12 = (s32[]{:T(128)}, bf16[11,32,640]{2,1,0:T(8,128)(2,1)S(1)}, s32[1]{0:T(128)}, s32[11]{0:T(128)S(1)}, s32[11]{0:T(128)S(1)}, /*index=5*/s32[22]{0:T(12...) while((s32[]{:T(128)}, bf16[11,32,640]{2,1,0:T(8,128)(2,1)S(1)}, s32[1]{0:T(128)}, ...), condition=%wide.region_2.3_spmd, body=%wide.region_0.2_spmd.sunk | while | flops 617372 | bytes 4555640 | solution.py:514
  153.9 1.8 %gather_fusion = bf16[8,32,640]{2,1,0:T(8,128)(2,1)S(1)} fusion(bf16[22,32,640]{2,1,0:T(8,128)(2,1)} %get-tuple-element.284, s32[1024]{0:T(1024)S(1)} %pad_clamp_fusion.4), kind=kCustom, calls=%fused_computation.clone.1 | custom fusion | bytes 655392 | tf_op jit(solution)/shard_map/while/body/jit(_take)/gather | solution.py:509
  156.5 5.7 %all-to-all-start = ((bf16[8,32,640]{2,1,0:T(8,128)(2,1)}), bf16[8,32,640]{2,1,0:T(8,128)(2,1)S(1)}, u32[]{:S(2)}, u32[]{:S(2)}) async-start(bf16[8,32,640]{2,1,0:T(8,128)(2,1)} %broadcast_select_fusion.3), calls=%async_computation | async-start | bytes 655360 | tf_op jit(solution)/shard_map/while/body/all_to_all | solution.py:497
  162.3 9.0 %all-to-all-done = bf16[8,32,640]{2,1,0:T(8,128)(2,1)S(1)} async-done(((bf16[8,32,640]{2,1,0:T(8,128)(2,1)}), bf16[8,32,640]{2,1,0:T(8,128)(2,1)S(1)}, u32[]{:S(2)}, u32[]{:S(2)}) %all-to-all-start) | async-done | bytes 327712 | tf_op jit(solution)/shard_map/while/body/all_to_all | solution.py:497
  (79 shorter events, 13.2 us)
Async XLA Ops:
  0.6 21.8 %copy-start.7 = (bf16[640,320]{0,1:T(8,128)(2,1)S(1)}, bf16[640,320]{0,1:T(8,128)(2,1)}, u32[]{:S(2)}) copy-start(bf16[640,320]{0,1:T(8,128)(2,1)} %param.18) | copy-start | bytes 1228804
  0.6 21.8 %copy-start.8 = (bf16[640,320]{0,1:T(8,128)(2,1)S(1)}, bf16[640,320]{0,1:T(8,128)(2,1)}, u32[]{:S(2)}) copy-start(bf16[640,320]{0,1:T(8,128)(2,1)} %param.19) | copy-start | bytes 1228804
  0.7 21.8 %copy-start.9 = (bf16[640,320]{0,1:T(8,128)(2,1)S(1)}, bf16[640,320]{0,1:T(8,128)(2,1)}, u32[]{:S(2)}) copy-start(bf16[640,320]{0,1:T(8,128)(2,1)} %param.20) | copy-start | bytes 1228804
  2.5 17.0 %collective-permute-start.1 = (bf16[3,160,640]{2,1,0:T(8,128)(2,1)S(1)}, bf16[3,160,640]{2,1,0:T(8,128)(2,1)S(1)}, u32[]{:S(2)}, u32[]{:S(2)}) collective-permute-start(bf16[3,160,640]{2,1,0:T(8,128)(2,1)S(1)} %halves.1), channel_id=1, source_target_pairs={{0,2},{2,4},{4,6},{6,0},{1,3},{3,5},{5,7},{7,1},{8,10},{10,12},{12... | collective-permute-start | bytes 1843208 | tf_op jit(solution)/shard_map/ppermute | solution.py:35
  4.2 15.3 %collective-permute-start.3 = (bf16[3,160,640]{2,1,0:T(8,128)(2,1)S(1)}, bf16[3,160,640]{2,1,0:T(8,128)(2,1)S(1)}, u32[]{:S(2)}, u32[]{:S(2)}) collective-permute-start(bf16[3,160,640]{2,1,0:T(8,128)(2,1)S(1)} %halves.1), channel_id=1, source_target_pairs={{0,6},{2,0},{4,2},{6,4},{1,7},{3,1},{5,3},{7,5},{8,14},{10,8},{12,... | collective-permute-start | bytes 1843208 | tf_op jit(solution)/shard_map/ppermute | solution.py:35
  8.0 21.5 %collective-permute-start = (bf16[2,11,32,640]{3,2,1,0:T(8,128)(2,1)S(1)}, bf16[2,11,32,640]{3,2,1,0:T(8,128)(2,1)S(1)}, u32[]{:S(2)}, u32[]{:S(2)}) collective-permute-start(bf16[2,11,32,640]{3,2,1,0:T(8,128)(2,1)S(1)} %prologue.1.grad), channel_id=1, source_target_pairs={{0,1},{1,0},{2,3},{3,2},{4,5},{5,4},{6,7},{7,6},{8,9},{9,8},{10,11... | collective-permute-start | bytes 2703368 | tf_op jit(solution)/shard_map/ppermute | solution.py:31
  19.5 2.0 %collective-permute-start.2 = (bf16[3,160,640]{2,1,0:T(8,128)(2,1)S(1)}, bf16[3,160,640]{2,1,0:T(8,128)(2,1)S(1)}, u32[]{:S(2)}, u32[]{:S(2)}) collective-permute-start(bf16[3,160,640]{2,1,0:T(8,128)(2,1)S(1)} %collective-permute-done.1.below), channel_id=1, source_target_pairs={{0,8},{8,0},{1,9},{9,1},{2,10},{10,2},{3,11},{11,3},{4,12},{12,4},... | collective-permute-start | bytes 1843208 | tf_op jit(solution)/shard_map/ppermute | solution.py:31
  19.5 2.9 %collective-permute-start.4 = (bf16[3,160,640]{2,1,0:T(8,128)(2,1)S(1)}, bf16[3,160,640]{2,1,0:T(8,128)(2,1)S(1)}, u32[]{:S(2)}, u32[]{:S(2)}) collective-permute-start(bf16[3,160,640]{2,1,0:T(8,128)(2,1)S(1)} %collective-permute-done.3.above), channel_id=1, source_target_pairs={{0,8},{8,0},{1,9},{9,1},{2,10},{10,2},{3,11},{11,3},{4,12},{12,4},... | collective-permute-start | bytes 1843208 | tf_op jit(solution)/shard_map/ppermute | solution.py:31
  39.1 21.1 %copy-start.2 = (bf16[3,3,8,40,320]{4,3,2,1,0:T(8,128)(2,1)}, bf16[3,3,8,40,320]{4,3,2,1,0:T(8,128)(2,1)S(1)}, u32[]{:S(2)}) copy-start(bf16[3,3,8,40,320]{4,3,2,1,0:T(8,128)(2,1)S(1)} %get-tuple-element.163.mine) | copy-start | bytes 5529604
  39.1 55.5 %collective-permute-start.9 = (bf16[3,3,8,40,320]{4,3,2,1,0:T(8,128)(2,1)}, bf16[3,3,8,40,320]{4,3,2,1,0:T(8,128)(2,1)}, u32[]{:S(2)}, u32[]{:S(2)}) collective-permute-start(bf16[3,3,8,40,320]{4,3,2,1,0:T(8,128)(2,1)} %get-tuple-element.164), channel_id=1, source_target_pairs={{0,8},{8,0},{1,9},{9,1},{2,10},{10,2},{3,11},{11,3},{4,12},{12,4},... | collective-permute-start | bytes 5529608 | tf_op jit(solution)/shard_map/ppermute | solution.py:31
  39.1 17.5 %collective-permute-start.5 = (bf16[3,160,640]{2,1,0:T(8,128)(2,1)S(1)}, bf16[3,160,640]{2,1,0:T(8,128)(2,1)S(1)}, u32[]{:S(2)}, u32[]{:S(2)}) collective-permute-start(bf16[3,160,640]{2,1,0:T(8,128)(2,1)S(1)} %collective-permute-done.1.below), channel_id=1, source_target_pairs={{0,2},{2,4},{4,6},{6,0},{1,3},{3,5},{5,7},{7,1},{8,10},{10,12},{12... | collective-permute-start | bytes 1843208 | tf_op jit(solution)/shard_map/ppermute | solution.py:35
  39.3 17.3 %collective-permute-start.6 = (bf16[3,160,640]{2,1,0:T(8,128)(2,1)S(1)}, bf16[3,160,640]{2,1,0:T(8,128)(2,1)S(1)}, u32[]{:S(2)}, u32[]{:S(2)}) collective-permute-start(bf16[3,160,640]{2,1,0:T(8,128)(2,1)S(1)} %collective-permute-done.4.above2), channel_id=1, source_target_pairs={{0,6},{2,0},{4,2},{6,4},{1,7},{3,1},{5,3},{7,5},{8,14},{10,8},{12,... | collective-permute-start | bytes 1843208 | tf_op jit(solution)/shard_map/ppermute | solution.py:35
  56.6 15.6 %copy-start.6 = (bf16[11,32,640]{2,1,0:T(8,128)(2,1)S(1)}, bf16[11,32,640]{2,1,0:T(8,128)(2,1)}, u32[]{:S(2)}) copy-start(bf16[11,32,640]{2,1,0:T(8,128)(2,1)} %lat.3) | copy-start | bytes 1351684
  56.6 15.6 %copy-start.16 = (s32[16]{0:T(128)S(1)}, s32[16]{0:T(128)}, u32[]{:S(2)}) copy-start(s32[16]{0:T(128)} %trunc.5) | copy-start | bytes 196
  60.2 19.4 %copy-start.10 = (bf16[3,704,320]{2,1,0:T(8,128)(2,1)}, bf16[3,704,320]{2,1,0:T(8,128)(2,1)S(1)}, u32[]{:S(2)}) copy-start(bf16[3,704,320]{2,1,0:T(8,128)(2,1)S(1)} %get-tuple-element.168.acts) | copy-start | bytes 4055044
  60.2 13.3 %copy-start.17 = (s32[176]{0:T(256)S(1)}, s32[176]{0:T(256)}, u32[]{:S(2)}) copy-start(s32[176]{0:T(256)} %tmap.1) | copy-start | bytes 2116
  60.2 12.0 %collective-permute-start.7 = (bf16[11,32,640]{2,1,0:T(8,128)(2,1)S(1)}, bf16[11,32,640]{2,1,0:T(8,128)(2,1)S(1)}, u32[]{:S(2)}, u32[]{:S(2)}) collective-permute-start(bf16[11,32,640]{2,1,0:T(8,128)(2,1)S(1)} %get-tuple-element.158), channel_id=1, source_target_pairs={{0,1},{1,0},{2,3},{3,2},{4,5},{5,4},{6,7},{7,6},{8,9},{9,8},{10,11... | collective-permute-start | bytes 1351688 | tf_op jit(solution)/shard_map/ppermute | solution.py:31
  73.4 6.2 %collective-permute-start.8 = (bf16[11,32,640]{2,1,0:T(8,128)(2,1)S(1)}, bf16[11,32,640]{2,1,0:T(8,128)(2,1)S(1)}, u32[]{:S(2)}, u32[]{:S(2)}) collective-permute-start(bf16[11,32,640]{2,1,0:T(8,128)(2,1)S(1)} %shard_map.140.own), channel_id=1, source_target_pairs={{0,8},{8,0},{1,9},{9,1},{2,10},{10,2},{3,11},{11,3},{4,12},{12,4},... | collective-permute-start | bytes 1351688 | tf_op jit(solution)/shard_map/ppermute | solution.py:31
  81.1 0.8 copy-start
  81.9 0.8 copy-start.4
  82.7 67.0 %all-to-all-start.1 = ((bf16[32,32,640]{2,1,0:T(8,128)(2,1)}), bf16[32,32,640]{2,1,0:T(8,128)(2,1)S(1)}, u32[]{:S(2)}, u32[]{:S(2)}) async-start(bf16[32,32,640]{2,1,0:T(8,128)(2,1)} %pack.1), calls=%async_computation.1 | async-start | bytes 2621440 | tf_op jit(solution)/shard_map/all_to_all | solution.py:497
  90.4 4.2 %copy-start.3 = (bf16[3,3,8,40,320]{4,3,2,1,0:T(8,128)(2,1)S(1)}, bf16[3,3,8,40,320]{4,3,2,1,0:T(8,128)(2,1)}, u32[]{:S(2)}) copy-start(bf16[3,3,8,40,320]{4,3,2,1,0:T(8,128)(2,1)} %copy-done.2) | copy-start | bytes 5529604
  90.4 1.6 copy-start.11
  94.3 5.7 %collective-permute-start.12 = (bf16[25,40,320]{2,1,0:T(8,128)(2,1)S(1)}, bf16[25,40,320]{2,1,0:T(8,128)(2,1)S(1)}, u32[]{:S(2)}, u32[]{:S(2)}) collective-permute-start(bf16[25,40,320]{2,1,0:T(8,128)(2,1)S(1)} %get-tuple-element.171), channel_id=1, source_target_pairs={{0,8},{8,0},{1,9},{9,1},{2,10},{10,2},{3,11},{11,3},{4,12},{12,4},... | collective-permute-start | bytes 1920008 | tf_op jit(solution)/shard_map/ppermute | solution.py:31
  96.8 31.0 %collective-permute-start.10 = (bf16[3,8,40,320]{3,2,1,0:T(8,128)(2,1)S(1)}, bf16[3,8,40,320]{3,2,1,0:T(8,128)(2,1)S(1)}, u32[]{:S(2)}, u32[]{:S(2)}) collective-permute-start(bf16[3,8,40,320]{3,2,1,0:T(8,128)(2,1)S(1)} %get-tuple-element.166), channel_id=1, source_target_pairs={{0,2},{2,4},{4,6},{6,0},{1,3},{3,5},{5,7},{7,1},{8,10},{10,12},{12... | collective-permute-start | bytes 1843208 | tf_op jit(solution)/shard_map/ppermute | solution.py:35
  96.8 30.9 %collective-permute-start.11 = (bf16[3,8,40,320]{3,2,1,0:T(8,128)(2,1)S(1)}, bf16[3,8,40,320]{3,2,1,0:T(8,128)(2,1)S(1)}, u32[]{:S(2)}, u32[]{:S(2)}) collective-permute-start(bf16[3,8,40,320]{3,2,1,0:T(8,128)(2,1)S(1)} %get-tuple-element.167), channel_id=1, source_target_pairs={{0,6},{2,0},{4,2},{6,4},{1,7},{3,1},{5,3},{7,5},{8,14},{10,8},{12,... | collective-permute-start | bytes 1843208 | tf_op jit(solution)/shard_map/ppermute | solution.py:35
  100.9 5.6 %collective-permute-start.13 = (f32[8,320]{1,0:T(8,128)S(1)}, f32[8,320]{1,0:T(8,128)S(1)}, u32[]{:S(2)}, u32[]{:S(2)}) collective-permute-start(f32[8,320]{1,0:T(8,128)S(1)} %get-tuple-element.172), channel_id=1, source_target_pairs={{0,1},{1,0},{2,3},{3,2},{4,5},{5,4},{6,7},{7,6},{8,9},{9,8},{10,11... | collective-permute-start | bytes 30728 | tf_op jit(solution)/shard_map/ppermute | solution.py:31
  106.6 9.3 %collective-permute-start.14 = (f32[8,320]{1,0:T(8,128)S(1)}, f32[8,320]{1,0:T(8,128)S(1)}, u32[]{:S(2)}, u32[]{:S(2)}) collective-permute-start(f32[8,320]{1,0:T(8,128)S(1)} %add.57), channel_id=1, source_target_pairs={{0,2},{2,0},{4,6},{6,4},{1,3},{3,1},{5,7},{7,5},{8,10},{10,8},{12,... | collective-permute-start | bytes 30728 | tf_op jit(solution)/shard_map/ppermute | solution.py:480
  106.6 12.8 %collective-permute-start.19 = (bf16[2,16,8,320]{3,2,1,0:T(8,128)(2,1)S(1)}, bf16[2,16,8,320]{3,2,1,0:T(8,128)(2,1)S(1)}, u32[]{:S(2)}, u32[]{:S(2)}) collective-permute-start(bf16[2,16,8,320]{3,2,1,0:T(8,128)(2,1)S(1)} %get-tuple-element.178), channel_id=1, source_target_pairs={{0,16},{16,32},{32,48},{48,0},{1,17},{17,33},{33,49},{49,1},{2,18}... | collective-permute-start | bytes 491528 | tf_op jit(solution)/shard_map/ppermute | solution.py:35
  108.4 13.6 %collective-permute-start.20 = (bf16[2,16,8,320]{3,2,1,0:T(8,128)(2,1)S(1)}, bf16[2,16,8,320]{3,2,1,0:T(8,128)(2,1)S(1)}, u32[]{:S(2)}, u32[]{:S(2)}) collective-permute-start(bf16[2,16,8,320]{3,2,1,0:T(8,128)(2,1)S(1)} %get-tuple-element.179), channel_id=1, source_target_pairs={{0,48},{16,0},{32,16},{48,32},{1,49},{17,1},{33,17},{49,33},{2,50}... | collective-permute-start | bytes 491528 | tf_op jit(solution)/shard_map/ppermute | solution.py:35
  115.9 8.2 %collective-permute-start.21 = (bf16[2,16,8,320]{3,2,1,0:T(8,128)(2,1)S(1)}, bf16[2,16,8,320]{3,2,1,0:T(8,128)(2,1)S(1)}, u32[]{:S(2)}, u32[]{:S(2)}) collective-permute-start(bf16[2,16,8,320]{3,2,1,0:T(8,128)(2,1)S(1)} %get-tuple-element.180), channel_id=1, source_target_pairs={{0,32},{16,48},{32,0},{48,16},{1,33},{17,49},{33,1},{49,17},{2,34}... | collective-permute-start | bytes 491528 | tf_op jit(solution)/shard_map/ppermute | solution.py:35
  119.4 8.4 %collective-permute-start.15 = (f32[8,320]{1,0:T(8,128)S(1)}, f32[8,320]{1,0:T(8,128)S(1)}, u32[]{:S(2)}, u32[]{:S(2)}) collective-permute-start(f32[8,320]{1,0:T(8,128)S(1)} %add.58.near), channel_id=1, source_target_pairs={{0,6},{6,0},{2,4},{4,2},{1,7},{7,1},{3,5},{5,3},{8,14},{14,8},{10,... | collective-permute-start | bytes 30728 | tf_op jit(solution)/shard_map/ppermute | solution.py:481
  124.2 11.4 %collective-permute-start.22 = (bf16[2,16,8,320]{3,2,1,0:T(8,128)(2,1)S(1)}, bf16[2,16,8,320]{3,2,1,0:T(8,128)(2,1)S(1)}, u32[]{:S(2)}, u32[]{:S(2)}) collective-permute-start(bf16[2,16,8,320]{3,2,1,0:T(8,128)(2,1)S(1)} %shard_map.146), channel_id=1, source_target_pairs={{0,4},{2,6},{4,0},{6,2},{1,5},{3,7},{5,1},{7,3},{8,12},{10,14},{12... | collective-permute-start | bytes 491528 | tf_op jit(solution)/shard_map/ppermute | solution.py:35
  127.8 20.8 %copy-start.1 = (bf16[11,32,640]{2,1,0:T(8,128)(2,1)S(1)}, bf16[11,32,640]{2,1,0:T(8,128)(2,1)}, u32[]{:S(2)}) copy-start(bf16[11,32,640]{2,1,0:T(8,128)(2,1)} %copy-done) | copy-start | bytes 1351684
  127.8 20.8 %copy-start.5 = (bf16[11,32,640]{2,1,0:T(8,128)(2,1)S(1)}, bf16[11,32,640]{2,1,0:T(8,128)(2,1)}, u32[]{:S(2)}) copy-start(bf16[11,32,640]{2,1,0:T(8,128)(2,1)} %copy-done.4) | copy-start | bytes 1351684
  129.6 0.8 copy-start.12
  130.3 9.2 %collective-permute-start.16 = (bf16[2,16,8,320]{3,2,1,0:T(8,128)(2,1)}, bf16[2,16,8,320]{3,2,1,0:T(8,128)(2,1)S(1)}, u32[]{:S(2)}, u32[]{:S(2)}) collective-permute-start(bf16[2,16,8,320]{3,2,1,0:T(8,128)(2,1)} %get-tuple-element.174), channel_id=1, source_target_pairs={{0,16},{16,32},{32,48},{48,0},{1,17},{17,33},{33,49},{49,1},{2,18}... | collective-permute-start | bytes 491528 | tf_op jit(solution)/shard_map/ppermute | solution.py:35
  132.1 8.6 %collective-permute-start.17 = (bf16[2,16,8,320]{3,2,1,0:T(8,128)(2,1)}, bf16[2,16,8,320]{3,2,1,0:T(8,128)(2,1)S(1)}, u32[]{:S(2)}, u32[]{:S(2)}) collective-permute-start(bf16[2,16,8,320]{3,2,1,0:T(8,128)(2,1)} %get-tuple-element.175), channel_id=1, source_target_pairs={{0,48},{16,0},{32,16},{48,32},{1,49},{17,1},{33,17},{49,33},{2,50}... | collective-permute-start | bytes 491528 | tf_op jit(solution)/shard_map/ppermute | solution.py:35
  133.6 8.6 %collective-permute-start.18 = (bf16[2,16,8,320]{3,2,1,0:T(8,128)(2,1)}, bf16[2,16,8,320]{3,2,1,0:T(8,128)(2,1)S(1)}, u32[]{:S(2)}, u32[]{:S(2)}) collective-permute-start(bf16[2,16,8,320]{3,2,1,0:T(8,128)(2,1)} %get-tuple-element.176), channel_id=1, source_target_pairs={{0,32},{16,48},{32,0},{48,16},{1,33},{17,49},{33,1},{49,17},{2,34}... | collective-permute-start | bytes 491528 | tf_op jit(solution)/shard_map/ppermute | solution.py:35
  142.2 0.7 copy-start.14
  142.9 1.0 copy-start.13
  143.9 0.9 copy-start.15
  145.5 6.2 %collective-permute-start.23 = (bf16[16,8,320]{2,1,0:T(8,128)(2,1)S(1)}, bf16[16,8,320]{2,1,0:T(8,128)(2,1)S(1)}, u32[]{:S(2)}, u32[]{:S(2)}) collective-permute-start(bf16[16,8,320]{2,1,0:T(8,128)(2,1)S(1)} %get-tuple-element.182), channel_id=1, source_target_pairs={{0,64},{64,0},{1,65},{65,1},{2,66},{66,2},{3,67},{67,3},{4,68},{68... | collective-permute-start | bytes 245768 | tf_op jit(solution)/shard_map/ppermute | solution.py:31
  156.5 14.7 %all-to-all-start = ((bf16[8,32,640]{2,1,0:T(8,128)(2,1)}), bf16[8,32,640]{2,1,0:T(8,128)(2,1)S(1)}, u32[]{:S(2)}, u32[]{:S(2)}) async-start(bf16[8,32,640]{2,1,0:T(8,128)(2,1)} %broadcast_select_fusion.3), calls=%async_computation | async-start | bytes 655360 | tf_op jit(solution)/shard_map/while/body/all_to_all | solution.py:497
  172.9 0.8 copy-start.18

commit v7 on v6

--- a/solution.py
+++ b/solution.py
@@ -296,7 +296,7 @@
     dn[...] = total[:352].reshape(11, 32, 640)
     dn_send[...] = total[352:].reshape(11, 32, 640).astype(BF)
     gsum = jnp.sum(total * rows[0].astype(F32), axis=0, keepdims=True) / gain[...]
-    tail[...] = split_gain(gsum)
+    tail[...] = joined(split_gain(gsum))
 
 
 def far_forward(meta, *arrays):
@@ -315,7 +315,7 @@
             out[8 * j : 8 * j + 8] = keep[:, side].astype(BF)
     for out in (mine, send):
         out[24] = jnp.zeros((40, 320), BF)
-        out[24, :8] = tail[...].astype(BF)
+        out[24, :8] = resplit(tail[...]).astype(BF)
 
 
 def far_grads(meta, turned, acts, tail):
@@ -410,36 +410,36 @@
         out[...] = parts[:, lax.rem(z + step, 4)].astype(out.dtype)
 
 
-def far_sums_kernel(meta, mine, got, keep, up, down, far, tail, parts):
+def far_sums_kernel(meta, mine, got, keep, up, down, far, parts):
     for j in range(3):
         x = mine[8 * j : 8 * j + 8].astype(F32) + got[8 * j : 8 * j + 8].astype(F32)
         parts[:, :, 5 * j : 5 * j + 5] = x.reshape(2, 4, 5, 8, 320)
-    parts[:, :, 15] = jnp.zeros((2, 4, 8, 320), F32)
-    spread(parts, meta[2], (keep, up, down, far))
-    tail[...] = joined(mine[24, :8]) + joined(got[24, :8])
-
-
-def far_z_kernel(own, down, up, far, out):
-    x = (own[...] + far[...].astype(F32)) + (down[...].astype(F32) + up[...].astype(F32))
-    out[...] = x.astype(BF)
-
-
-def over_y_kernel(meta, own, from_down, from_up, near, across, keep, up, down, far, parts):
-    for j in range(3):
-        x = own[j] + from_down[j].astype(F32) + from_up[j].astype(F32)
-        parts[:, :, 5 * j : 5 * j + 5] = x.reshape(2, 4, 5, 8, 320)
-    tail = resplit(near[...] + across[...])
+    tail = resplit(joined(mine[24, :8]) + joined(got[24, :8]))
     for k in range(2):
         for z in range(4):
             parts[k, z, 15] = tail
     spread(parts, meta[2], (keep, up, down, far))
 
 
-def over_z_kernel(meta, own, down, up, far, across, keep, give, sums):
+def far_z_kernel(own, down, up, far, out, tail):
+    x = (own[...] + far[...].astype(F32)) + (down[...].astype(F32) + up[...].astype(F32))
+    out[...] = x.astype(BF)
+    tail[...] = joined(x[0, 15])
+
+
+def over_y_kernel(meta, own, from_down, from_up, keep, up, down, far, parts):
+    for j in range(3):
+        x = own[j] + from_down[j].astype(F32) + from_up[j].astype(F32)
+        parts[:, :, 5 * j : 5 * j + 5] = x.reshape(2, 4, 5, 8, 320)
+    parts[:, :, 15] = jnp.zeros((2, 4, 8, 320), F32)
+    spread(parts, meta[2], (keep, up, down, far))
+
+
+def over_z_kernel(meta, own, down, up, far, across, gain, gain2, keep, give, sums):
     sums[...] = (own[...] + far[...].astype(F32)) + (down[...].astype(F32) + up[...].astype(F32))
     for k in range(2):
         sums[k, :15] += across[k, :15].astype(F32)
-        sums[k, 15] = resplit(joined(sums[k, 15]))
+        sums[k, 15] = resplit(gain[...] + gain2[...])
     keep[...] = sums[meta[3]]
     give[...] = sums[1 - meta[3]].astype(BF)
 
@@ -470,21 +470,16 @@
     )
     from_down = ring(up, "y", 1)
     from_up = ring(down, "y", -1)
-    far_own, *far_sent, tail = local(
-        far_sums_kernel, 6, (*parts, row), (far_mine, far_got), whole, (meta,)
-    )
-    tail = tail + swap(tail, "xl")
+    far_own, *far_sent = local(far_sums_kernel, 6, parts, (far_mine, far_got), whole, (meta,))
     came = over_ring(*far_sent)
-    (across,) = local(far_z_kernel, 3, ((part, BF),), (far_own, *came))
+    across, tail = local(far_z_kernel, 3, ((part, BF), row), (far_own, *came))
     across = ring(across, "y", 2)
     tail = tail + lax.ppermute(tail, "y", [(0, 1), (1, 0), (2, 3), (3, 2)])
-    across_y = lax.ppermute(tail, "y", [(0, 3), (3, 0), (1, 2), (2, 1)])
-    own, *sent = local(
-        over_y_kernel, 6, parts, (own, from_down, from_up, tail, across_y), whole, (meta,)
-    )
+    tail2 = lax.ppermute(tail, "y", [(0, 3), (3, 0), (1, 2), (2, 1)])
+    own, *sent = local(over_y_kernel, 6, parts, (own, from_down, from_up), whole, (meta,))
     came = over_ring(*sent)
     keep, give = local(
-        over_z_kernel, 4, ((part[1:], F32), (part[1:], BF)), (own, *came, across),
+        over_z_kernel, 4, ((part[1:], F32), (part[1:], BF)), (own, *came, across, tail, tail2),
         [(part, F32)], (meta,),
     )
     got = swap(give, "xh")
@@ -535,6 +530,7 @@
     near_mine, near_send = near_grads(meta, turned, near_acts)
     near_got = swap(near_send, "c")
     dn, dn_send, far_acts, tail = far_forward(meta, both, gain, near_dn, first, second)
+    tail = tail + swap(tail, "xl")
     got = swap(dn_send, "xl")
     far_mine, far_send = far_grads(meta, turned, far_acts, tail)
     far_got = swap(far_send, "c")

time: 174 us -> 184 us (1.057)
  the two profiles are of different devices: /device:TPU:0 before, /device:TPU:24 now
where the time goes in v7:
time: 184 us; the launch traced here: 183 us
  waiting for transfers between devices  86.3 us (47%)
  starting transfers between devices  42.6 us (23%)
  Pallas kernels  40.4 us (22%)
  local copies, waits for them, and re-layouts  9.3 us (5%)
  other arithmetic  2.54 us (1%)
    ppermute x13, waiting for transfers between devices, ring(): return lax.ppermute(x, axis, [(i, (i + step) % 4) for i in range(4)])  38.8 us
    ppermute x9, waiting for transfers between devices, swap(): return lax.ppermute(x, axis, [(0, 1), (1, 0)])  29.9 us
    pallas_call x12, Pallas kernels, local(): pl.pallas_call(kernel, out_shape=tuple((jax.ShapeDtypeStruct(s, d) for s,...  28.2 us
    ppermute x13, starting transfers between devices, ring(): return lax.ppermute(x, axis, [(i, (i + step) % 4) for i in range(4)])  21.4 us
    all_to_all x2, starting transfers between devices, route(): return lax.all_to_all(packed, CHIP, 0, 0, tiled=True)  13.5 us
    all_to_all x2, waiting for transfers between devices, route(): return lax.all_to_all(packed, CHIP, 0, 0, tiled=True)  8.96 us
    ppermute x9, starting transfers between devices, swap(): return lax.ppermute(x, axis, [(0, 1), (1, 0)])  7.68 us
    pallas_call x1, Pallas kernels, index_work(): pl.pallas_call(index_kernel, out_shape=(i22, i22, i11, i11, jax.ShapeDtyp...  6.05 us
  transfers between devices with their start and end apart: 26, of which 18 were waited for; matrix products, arithmetic and copies ran while one was open for 1% of the time, Pallas kernels for 15%

profile of v7, /device:TPU:24, one launch (start us, length us, event | category | flops | bytes accessed | tf_op | source)
XLA Modules:
  0.0 183.1 jit_solution(7859110273133351399)
XLA Ops:
  0.8 1.7 halves.1
  2.6 1.9 %collective-permute-start.3 = (bf16[3,160,640]{2,1,0:T(8,128)(2,1)S(1)}, bf16[3,160,640]{2,1,0:T(8,128)(2,1)S(1)}, u32[]{:S(2)}, u32[]{:S(2)}) collective-permute-start(bf16[3,160,640]{2,1,0:T(8,128)(2,1)S(1)} %halves.1), channel_id=1, source_target_pairs={{0,6},{2,0},{4,2},{6,4},{1,7},{3,1},{5,3},{7,5},{8,14},{10,8},{12,... | collective-permute-start | bytes 1843208 | tf_op jit(solution)/shard_map/ppermute | solution.py:35
  5.2 1.6 prologue.1.grad
  6.8 1.6 collective-permute-start
  8.4 9.7 %collective-permute-done.1.below = bf16[3,160,640]{2,1,0:T(8,128)(2,1)S(1)} collective-permute-done((bf16[3,160,640]{2,1,0:T(8,128)(2,1)S(1)}, bf16[3,160,640]{2,1,0:T(8,128)(2,1)S(1)}, u32[]{:S(2)}, u32[]{:S(2)}) %collective-permute-start.1) | collective-permute-done | bytes 614432 | tf_op jit(solution)/shard_map/ppermute | solution.py:35
  18.1 1.3 collective-permute-done.3.above
  20.2 1.3 collective-permute-done.4.above2
  21.5 4.4 %shard_map.137 = (f32[352,640]{1,0:T(8,128)S(1)}, bf16[3,352,960]{2,1,0:T(8,128)(2,1)S(1)}, bf16[3,960,640]{2,1,0:T(8,128)(2,1)S(1)}) custom-call(s32[4]{0:T(128)S(1)} %pad_add_fusion.meta, bf16[2,352,640]{2,1,0:T(8,128)(2,1)S(1)} %bitcast.27, bf16[320,640]{1,0:T(8,128)(2,1)S(1)} %bitcast.30, bf16[320,640]{1,0:T(8,128)(2,1)S(1)} %bitcast.32, ...), custom_call_target="tpu_custom_call" | custom-call | tf_op jit(solution)/shard_map/pallas_call | solution.py:186
  25.9 2.2 %collective-permute-done = bf16[2,11,32,640]{3,2,1,0:T(8,128)(2,1)S(1)} collective-permute-done((bf16[2,11,32,640]{3,2,1,0:T(8,128)(2,1)S(1)}, bf16[2,11,32,640]{3,2,1,0:T(8,128)(2,1)S(1)}, u32[]{:S(2)}, u32[]{:S(2)}) %collective-permute-start) | collective-permute-done | bytes 901152 | tf_op jit(solution)/shard_map/ppermute | solution.py:31
  28.1 3.9 %shard_map.138 = (f32[704,640]{1,0:T(8,128)S(1)}, bf16[3,704,960]{2,1,0:T(8,128)(2,1)S(1)}, bf16[2,704,640]{2,1,0:T(8,128)(2,1)S(1)}, bf16[2,640,704]{2,1,0:T(8,128)(2,1)S(1)}) custom-call(bf16[2,352,640]{2,1,0:T(8,128)(2,1)S(1)} %bitcast.28, bf16[2,352,640]{2,1,0:T(8,128)(2,1)S(1)} %bitcast.35, f32[352,640]{1,0:T(8,128)S(1)} %get-tuple-element.153.own_dn, ...), custom_call_target="tpu_custom_call" | custom-call | tf_op jit(solution)/shard_map/pallas_call | solution.py:186
  32.0 5.7 %shard_map.141 = (bf16[3,3,8,40,320]{4,3,2,1,0:T(8,128)(2,1)S(1)}, bf16[3,3,8,40,320]{4,3,2,1,0:T(8,128)(2,1)}) custom-call(s32[4]{0:T(128)S(1)} %pad_add_fusion.meta, bf16[2,640,704]{2,1,0:T(8,128)(2,1)S(1)} %get-tuple-element.162.turned, bf16[3,704,960]{2,1,0:T(8,128)(2,1)S(1)} %get-tuple-element.163.acts), custom_call_target="tpu_custom_call" | custom-call | tf_op jit(solution)/shard_map/pallas_call | solution.py:186
  37.7 1.6 collective-permute-start.5
  39.7 14.2 %collective-permute-done.5.first = bf16[3,160,640]{2,1,0:T(8,128)(2,1)S(1)} collective-permute-done((bf16[3,160,640]{2,1,0:T(8,128)(2,1)S(1)}, bf16[3,160,640]{2,1,0:T(8,128)(2,1)S(1)}, u32[]{:S(2)}, u32[]{:S(2)}) %collective-permute-start.5) | collective-permute-done | bytes 614432 | tf_op jit(solution)/shard_map/ppermute | solution.py:35
  54.0 2.5 %collective-permute-done.6.second = bf16[3,160,640]{2,1,0:T(8,128)(2,1)S(1)} collective-permute-done((bf16[3,160,640]{2,1,0:T(8,128)(2,1)S(1)}, bf16[3,160,640]{2,1,0:T(8,128)(2,1)S(1)}, u32[]{:S(2)}, u32[]{:S(2)}) %collective-permute-start.6) | collective-permute-done | bytes 614432 | tf_op jit(solution)/shard_map/ppermute | solution.py:35
  56.5 3.7 %shard_map.139 = (f32[11,32,640]{2,1,0:T(8,128)S(1)}, bf16[11,32,640]{2,1,0:T(8,128)(2,1)S(1)}, bf16[3,704,320]{2,1,0:T(8,128)(2,1)S(1)}, f32[8,320]{1,0:T(8,128)S(1)}) custom-call(s32[4]{0:T(128)S(1)} %pad_add_fusion.meta, bf16[2,704,640]{2,1,0:T(8,128)(2,1)S(1)} %get-tuple-element.156.rows, f32[1,640]{1,0:T(1,128)S(1)} %broadcast_in_dim.67.gain, ...), custom_call_target="tpu_custom_call" | custom-call | tf_op jit(solution)/shard_map/pallas_call | solution.py:186
  60.2 1.6 collective-permute-start.7
  61.7 10.1 %collective-permute-done.7.got = bf16[11,32,640]{2,1,0:T(8,128)(2,1)S(1)} collective-permute-done((bf16[11,32,640]{2,1,0:T(8,128)(2,1)S(1)}, bf16[11,32,640]{2,1,0:T(8,128)(2,1)S(1)}, u32[]{:S(2)}, u32[]{:S(2)}) %collective-permute-start.7) | collective-permute-done | bytes 450592 | tf_op jit(solution)/shard_map/ppermute | solution.py:31
  71.9 1.2 shard_map.140.own
  73.2 6.1 %routes.1 = (s32[22]{0:T(128)S(1)}, s32[22]{0:T(128)S(1)}, s32[11]{0:T(128)S(1)}, s32[11]{0:T(128)S(1)}, s32[1]{0:T(128)}) custom-call(s32[4]{0:T(128)S(1)} %pad_add_fusion.meta, s32[16]{0:T(128)S(1)} %copy-done.14, s32[176]{0:T(256)S(1)} %copy-done.15), custom_call_target="tpu_custom_call" | custom-call | tf_op jit(solution)/shard_map/routes/pallas_call | solution.py:101
  79.3 1.5 pack.1
  82.3 7.8 %all-to-all-start.1 = ((bf16[32,32,640]{2,1,0:T(8,128)(2,1)}), bf16[32,32,640]{2,1,0:T(8,128)(2,1)S(1)}, u32[]{:S(2)}, u32[]{:S(2)}) async-start(bf16[32,32,640]{2,1,0:T(8,128)(2,1)} %pack.1), calls=%async_computation.1 | async-start | bytes 2621440 | tf_op jit(solution)/shard_map/all_to_all | solution.py:492
  90.8 15.5 %collective-permute-done.15 = f32[8,320]{1,0:T(8,128)S(1)} collective-permute-done((f32[8,320]{1,0:T(8,128)S(1)}, f32[8,320]{1,0:T(8,128)S(1)}, u32[]{:S(2)}, u32[]{:S(2)}) %collective-permute-start.15) | collective-permute-done | bytes 10272 | tf_op jit(solution)/shard_map/ppermute | solution.py:31
  106.3 1.4 copy-done.11
  107.7 2.3 %shard_map.144 = (bf16[25,40,320]{2,1,0:T(8,128)(2,1)S(1)}, bf16[25,40,320]{2,1,0:T(8,128)(2,1)S(1)}) custom-call(s32[4]{0:T(128)S(1)} %pad_add_fusion.meta, bf16[2,640,704]{2,1,0:T(8,128)(2,1)S(1)} %get-tuple-element.162.turned, bf16[3,704,320]{2,1,0:T(8,128)(2,1)S(1)} %copy-done.11, f32[8,320]{1,0:T(8,128)S(1)} %add.57.tail), custom_call_target="tpu_custom_call" | custom-call | tf_op jit(solution)/shard_map/pallas_call | solution.py:186
  110.1 2.1 %shard_map.142 = (f32[3,8,40,320]{3,2,1,0:T(8,128)S(1)}, bf16[3,8,40,320]{3,2,1,0:T(8,128)(2,1)S(1)}, bf16[3,8,40,320]{3,2,1,0:T(8,128)(2,1)S(1)}) custom-call(bf16[3,3,8,40,320]{4,3,2,1,0:T(8,128)(2,1)S(1)} %copy-done.3, bf16[3,3,8,40,320]{4,3,2,1,0:T(8,128)(2,1)} %collective-permute-done.9.got), custom_call_target="tpu_custom_call" | custom-call | tf_op jit(solution)/shard_map/pallas_call | solution.py:186
  112.9 1.5 collective-permute-start.11
  115.2 1.8 collective-permute-start.17
  117.1 1.5 collective-permute-start.18
  118.5 2.0 %collective-permute-start.19 = (bf16[2,16,8,320]{3,2,1,0:T(8,128)(2,1)S(1)}, bf16[2,16,8,320]{3,2,1,0:T(8,128)(2,1)S(1)}, u32[]{:S(2)}, u32[]{:S(2)}) collective-permute-start(bf16[2,16,8,320]{3,2,1,0:T(8,128)(2,1)S(1)} %get-tuple-element.180), channel_id=1, source_target_pairs={{0,32},{16,48},{32,0},{48,16},{1,33},{17,49},{33,1},{49,17},{2,34}... | collective-permute-start | bytes 491528 | tf_op jit(solution)/shard_map/ppermute | solution.py:35
  120.6 2.7 %collective-permute-done.17.down = bf16[2,16,8,320]{3,2,1,0:T(8,128)(2,1)S(1)} collective-permute-done((bf16[2,16,8,320]{3,2,1,0:T(8,128)(2,1)S(1)}, bf16[2,16,8,320]{3,2,1,0:T(8,128)(2,1)S(1)}, u32[]{:S(2)}, u32[]{:S(2)}) %collective-permute-start.17) | collective-permute-done | bytes 163872 | tf_op jit(solution)/shard_map/ppermute | solution.py:35
  123.3 1.6 collective-permute-done.18.up
  124.8 3.8 %collective-permute-done.19.far = bf16[2,16,8,320]{3,2,1,0:T(8,128)(2,1)S(1)} collective-permute-done((bf16[2,16,8,320]{3,2,1,0:T(8,128)(2,1)S(1)}, bf16[2,16,8,320]{3,2,1,0:T(8,128)(2,1)S(1)}, u32[]{:S(2)}, u32[]{:S(2)}) %collective-permute-start.19) | collective-permute-done | bytes 163872 | tf_op jit(solution)/shard_map/ppermute | solution.py:35
  129.8 1.4 collective-permute-done.10.from_down
  131.2 1.5 collective-permute-done.11.from_up
  132.7 1.7 shard_map.143
  135.2 6.0 %collective-permute-start.12 = (bf16[2,16,8,320]{3,2,1,0:T(8,128)(2,1)}, bf16[2,16,8,320]{3,2,1,0:T(8,128)(2,1)S(1)}, u32[]{:S(2)}, u32[]{:S(2)}) collective-permute-start(bf16[2,16,8,320]{3,2,1,0:T(8,128)(2,1)} %get-tuple-element.170), channel_id=1, source_target_pairs={{0,16},{16,32},{32,48},{48,0},{1,17},{17,33},{33,49},{49,1},{2,18}... | collective-permute-start | bytes 491528 | tf_op jit(solution)/shard_map/ppermute | solution.py:35
  141.2 1.2 collective-permute-start.13
  142.4 2.3 %collective-permute-start.14 = (bf16[2,16,8,320]{3,2,1,0:T(8,128)(2,1)}, bf16[2,16,8,320]{3,2,1,0:T(8,128)(2,1)S(1)}, u32[]{:S(2)}, u32[]{:S(2)}) collective-permute-start(bf16[2,16,8,320]{3,2,1,0:T(8,128)(2,1)} %get-tuple-element.172), channel_id=1, source_target_pairs={{0,32},{16,48},{32,0},{48,16},{1,33},{17,49},{33,1},{49,17},{2,34}... | collective-permute-start | bytes 491528 | tf_op jit(solution)/shard_map/ppermute | solution.py:35
  144.7 3.7 %collective-permute-done.21 = f32[8,320]{1,0:T(8,128)S(1)} collective-permute-done((f32[8,320]{1,0:T(8,128)S(1)}, f32[8,320]{1,0:T(8,128)S(1)}, u32[]{:S(2)}, u32[]{:S(2)}) %collective-permute-start.21) | collective-permute-done | bytes 10272 | tf_op jit(solution)/shard_map/ppermute | solution.py:477
  148.4 4.9 %collective-permute-done.22.gain2 = f32[8,320]{1,0:T(8,128)S(1)} collective-permute-done((f32[8,320]{1,0:T(8,128)S(1)}, f32[8,320]{1,0:T(8,128)S(1)}, u32[]{:S(2)}, u32[]{:S(2)}) %collective-permute-start.22) | collective-permute-done | bytes 10272 | tf_op jit(solution)/shard_map/ppermute | solution.py:478
  153.3 1.0 copy-done.13
  155.1 3.7 %collective-permute-start.23 = (bf16[16,8,320]{2,1,0:T(8,128)(2,1)S(1)}, bf16[16,8,320]{2,1,0:T(8,128)(2,1)S(1)}, u32[]{:S(2)}, u32[]{:S(2)}) collective-permute-start(bf16[16,8,320]{2,1,0:T(8,128)(2,1)S(1)} %get-tuple-element.184), channel_id=1, source_target_pairs={{0,64},{64,0},{1,65},{65,1},{2,66},{66,2},{3,67},{67,3},{4,68},{68... | collective-permute-start | bytes 245768 | tf_op jit(solution)/shard_map/ppermute | solution.py:31
  158.8 1.1 pad_maximum_fusion
  159.8 1.4 unpack.1
  162.7 19.7 %while.12 = (s32[]{:T(128)}, bf16[11,32,640]{2,1,0:T(8,128)(2,1)S(1)}, s32[1]{0:T(128)}, s32[11]{0:T(128)S(1)}, s32[11]{0:T(128)S(1)}, /*index=5*/s32[22]{0:T(12...) while((s32[]{:T(128)}, bf16[11,32,640]{2,1,0:T(8,128)(2,1)S(1)}, s32[1]{0:T(128)}, ...), condition=%wide.region_2.3_spmd, body=%wide.region_0.2_spmd.sunk | while | flops 617372 | bytes 4555640 | solution.py:509
  163.4 1.8 gather_fusion
  166.1 5.7 %all-to-all-start = ((bf16[8,32,640]{2,1,0:T(8,128)(2,1)}), bf16[8,32,640]{2,1,0:T(8,128)(2,1)S(1)}, u32[]{:S(2)}, u32[]{:S(2)}) async-start(bf16[8,32,640]{2,1,0:T(8,128)(2,1)} %broadcast_select_fusion.3), calls=%async_computation | async-start | bytes 655360 | tf_op jit(solution)/shard_map/while/body/all_to_all | solution.py:492
  171.8 9.0 %all-to-all-done = bf16[8,32,640]{2,1,0:T(8,128)(2,1)S(1)} async-done(((bf16[8,32,640]{2,1,0:T(8,128)(2,1)}), bf16[8,32,640]{2,1,0:T(8,128)(2,1)S(1)}, u32[]{:S(2)}, u32[]{:S(2)}) %all-to-all-start) | async-done | bytes 327712 | tf_op jit(solution)/shard_map/while/body/all_to_all | solution.py:492
  (75 shorter events, 13.0 us)
Async XLA Ops:
  0.6 20.8 %copy-start.7 = (bf16[640,320]{0,1:T(8,128)(2,1)S(1)}, bf16[640,320]{0,1:T(8,128)(2,1)}, u32[]{:S(2)}) copy-start(bf16[640,320]{0,1:T(8,128)(2,1)} %param.18) | copy-start | bytes 1228804
  0.6 20.8 %copy-start.8 = (bf16[640,320]{0,1:T(8,128)(2,1)S(1)}, bf16[640,320]{0,1:T(8,128)(2,1)}, u32[]{:S(2)}) copy-start(bf16[640,320]{0,1:T(8,128)(2,1)} %param.19) | copy-start | bytes 1228804
  0.7 20.8 %copy-start.9 = (bf16[640,320]{0,1:T(8,128)(2,1)S(1)}, bf16[640,320]{0,1:T(8,128)(2,1)}, u32[]{:S(2)}) copy-start(bf16[640,320]{0,1:T(8,128)(2,1)} %param.20) | copy-start | bytes 1228804
  2.5 15.7 %collective-permute-start.1 = (bf16[3,160,640]{2,1,0:T(8,128)(2,1)S(1)}, bf16[3,160,640]{2,1,0:T(8,128)(2,1)S(1)}, u32[]{:S(2)}, u32[]{:S(2)}) collective-permute-start(bf16[3,160,640]{2,1,0:T(8,128)(2,1)S(1)} %halves.1), channel_id=1, source_target_pairs={{0,2},{2,4},{4,6},{6,0},{1,3},{3,5},{5,7},{7,1},{8,10},{10,12},{12... | collective-permute-start | bytes 1843208 | tf_op jit(solution)/shard_map/ppermute | solution.py:35
  2.6 16.8 %collective-permute-start.3 = (bf16[3,160,640]{2,1,0:T(8,128)(2,1)S(1)}, bf16[3,160,640]{2,1,0:T(8,128)(2,1)S(1)}, u32[]{:S(2)}, u32[]{:S(2)}) collective-permute-start(bf16[3,160,640]{2,1,0:T(8,128)(2,1)S(1)} %halves.1), channel_id=1, source_target_pairs={{0,6},{2,0},{4,2},{6,4},{1,7},{3,1},{5,3},{7,5},{8,14},{10,8},{12,... | collective-permute-start | bytes 1843208 | tf_op jit(solution)/shard_map/ppermute | solution.py:35
  6.8 21.3 %collective-permute-start = (bf16[2,11,32,640]{3,2,1,0:T(8,128)(2,1)S(1)}, bf16[2,11,32,640]{3,2,1,0:T(8,128)(2,1)S(1)}, u32[]{:S(2)}, u32[]{:S(2)}) collective-permute-start(bf16[2,11,32,640]{3,2,1,0:T(8,128)(2,1)S(1)} %prologue.1.grad), channel_id=1, source_target_pairs={{0,1},{1,0},{2,3},{3,2},{4,5},{5,4},{6,7},{7,6},{8,9},{9,8},{10,11... | collective-permute-start | bytes 2703368 | tf_op jit(solution)/shard_map/ppermute | solution.py:31
  18.1 2.0 %collective-permute-start.2 = (bf16[3,160,640]{2,1,0:T(8,128)(2,1)S(1)}, bf16[3,160,640]{2,1,0:T(8,128)(2,1)S(1)}, u32[]{:S(2)}, u32[]{:S(2)}) collective-permute-start(bf16[3,160,640]{2,1,0:T(8,128)(2,1)S(1)} %collective-permute-done.1.below), channel_id=1, source_target_pairs={{0,8},{8,0},{1,9},{9,1},{2,10},{10,2},{3,11},{11,3},{4,12},{12,4},... | collective-permute-start | bytes 1843208 | tf_op jit(solution)/shard_map/ppermute | solution.py:31
  19.4 2.0 %collective-permute-start.4 = (bf16[3,160,640]{2,1,0:T(8,128)(2,1)S(1)}, bf16[3,160,640]{2,1,0:T(8,128)(2,1)S(1)}, u32[]{:S(2)}, u32[]{:S(2)}) collective-permute-start(bf16[3,160,640]{2,1,0:T(8,128)(2,1)S(1)} %collective-permute-done.3.above), channel_id=1, source_target_pairs={{0,8},{8,0},{1,9},{9,1},{2,10},{10,2},{3,11},{11,3},{4,12},{12,4},... | collective-permute-start | bytes 1843208 | tf_op jit(solution)/shard_map/ppermute | solution.py:31
  37.7 22.4 %copy-start.2 = (bf16[3,3,8,40,320]{4,3,2,1,0:T(8,128)(2,1)}, bf16[3,3,8,40,320]{4,3,2,1,0:T(8,128)(2,1)S(1)}, u32[]{:S(2)}) copy-start(bf16[3,3,8,40,320]{4,3,2,1,0:T(8,128)(2,1)S(1)} %get-tuple-element.164.mine) | copy-start | bytes 5529604
  37.7 72.4 %collective-permute-start.9 = (bf16[3,3,8,40,320]{4,3,2,1,0:T(8,128)(2,1)}, bf16[3,3,8,40,320]{4,3,2,1,0:T(8,128)(2,1)}, u32[]{:S(2)}, u32[]{:S(2)}) collective-permute-start(bf16[3,3,8,40,320]{4,3,2,1,0:T(8,128)(2,1)} %get-tuple-element.165), channel_id=1, source_target_pairs={{0,8},{8,0},{1,9},{9,1},{2,10},{10,2},{3,11},{11,3},{4,12},{12,4},... | collective-permute-start | bytes 5529608 | tf_op jit(solution)/shard_map/ppermute | solution.py:31
  37.7 16.3 %collective-permute-start.5 = (bf16[3,160,640]{2,1,0:T(8,128)(2,1)S(1)}, bf16[3,160,640]{2,1,0:T(8,128)(2,1)S(1)}, u32[]{:S(2)}, u32[]{:S(2)}) collective-permute-start(bf16[3,160,640]{2,1,0:T(8,128)(2,1)S(1)} %collective-permute-done.1.below), channel_id=1, source_target_pairs={{0,2},{2,4},{4,6},{6,0},{1,3},{3,5},{5,7},{7,1},{8,10},{10,12},{12... | collective-permute-start | bytes 1843208 | tf_op jit(solution)/shard_map/ppermute | solution.py:35
  39.3 17.2 %collective-permute-start.6 = (bf16[3,160,640]{2,1,0:T(8,128)(2,1)S(1)}, bf16[3,160,640]{2,1,0:T(8,128)(2,1)S(1)}, u32[]{:S(2)}, u32[]{:S(2)}) collective-permute-start(bf16[3,160,640]{2,1,0:T(8,128)(2,1)S(1)} %collective-permute-done.4.above2), channel_id=1, source_target_pairs={{0,6},{2,0},{4,2},{6,4},{1,7},{3,1},{5,3},{7,5},{8,14},{10,8},{12,... | collective-permute-start | bytes 1843208 | tf_op jit(solution)/shard_map/ppermute | solution.py:35
  56.5 15.4 %copy-start.6 = (bf16[11,32,640]{2,1,0:T(8,128)(2,1)S(1)}, bf16[11,32,640]{2,1,0:T(8,128)(2,1)}, u32[]{:S(2)}) copy-start(bf16[11,32,640]{2,1,0:T(8,128)(2,1)} %lat.3) | copy-start | bytes 1351684
  56.5 15.4 %copy-start.14 = (s32[16]{0:T(128)S(1)}, s32[16]{0:T(128)}, u32[]{:S(2)}) copy-start(s32[16]{0:T(128)} %trunc.5) | copy-start | bytes 196
  60.1 19.1 %copy-start.10 = (bf16[3,704,320]{2,1,0:T(8,128)(2,1)}, bf16[3,704,320]{2,1,0:T(8,128)(2,1)S(1)}, u32[]{:S(2)}) copy-start(bf16[3,704,320]{2,1,0:T(8,128)(2,1)S(1)} %get-tuple-element.173.acts) | copy-start | bytes 4055044
  60.2 13.1 %copy-start.15 = (s32[176]{0:T(256)S(1)}, s32[176]{0:T(256)}, u32[]{:S(2)}) copy-start(s32[176]{0:T(256)} %tmap.1) | copy-start | bytes 2116
  60.2 11.7 %collective-permute-start.7 = (bf16[11,32,640]{2,1,0:T(8,128)(2,1)S(1)}, bf16[11,32,640]{2,1,0:T(8,128)(2,1)S(1)}, u32[]{:S(2)}, u32[]{:S(2)}) collective-permute-start(bf16[11,32,640]{2,1,0:T(8,128)(2,1)S(1)} %get-tuple-element.159), channel_id=1, source_target_pairs={{0,1},{1,0},{2,3},{3,2},{4,5},{5,4},{6,7},{7,6},{8,9},{9,8},{10,11... | collective-permute-start | bytes 1351688 | tf_op jit(solution)/shard_map/ppermute | solution.py:31
  73.1 6.2 %collective-permute-start.8 = (bf16[11,32,640]{2,1,0:T(8,128)(2,1)S(1)}, bf16[11,32,640]{2,1,0:T(8,128)(2,1)S(1)}, u32[]{:S(2)}, u32[]{:S(2)}) collective-permute-start(bf16[11,32,640]{2,1,0:T(8,128)(2,1)S(1)} %shard_map.140.own), channel_id=1, source_target_pairs={{0,8},{8,0},{1,9},{9,1},{2,10},{10,2},{3,11},{11,3},{4,12},{12,4},... | collective-permute-start | bytes 1351688 | tf_op jit(solution)/shard_map/ppermute | solution.py:31
  80.8 0.8 copy-start
  81.6 0.8 copy-start.4
  82.3 77.5 %all-to-all-start.1 = ((bf16[32,32,640]{2,1,0:T(8,128)(2,1)}), bf16[32,32,640]{2,1,0:T(8,128)(2,1)S(1)}, u32[]{:S(2)}, u32[]{:S(2)}) async-start(bf16[32,32,640]{2,1,0:T(8,128)(2,1)} %pack.1), calls=%async_computation.1 | async-start | bytes 2621440 | tf_op jit(solution)/shard_map/all_to_all | solution.py:492
  90.1 20.0 %copy-start.3 = (bf16[3,3,8,40,320]{4,3,2,1,0:T(8,128)(2,1)S(1)}, bf16[3,3,8,40,320]{4,3,2,1,0:T(8,128)(2,1)}, u32[]{:S(2)}) copy-start(bf16[3,3,8,40,320]{4,3,2,1,0:T(8,128)(2,1)} %copy-done.2) | copy-start | bytes 5529604
  90.1 16.1 %collective-permute-start.15 = (f32[8,320]{1,0:T(8,128)S(1)}, f32[8,320]{1,0:T(8,128)S(1)}, u32[]{:S(2)}, u32[]{:S(2)}) collective-permute-start(f32[8,320]{1,0:T(8,128)S(1)} %get-tuple-element.174), channel_id=1, source_target_pairs={{0,1},{1,0},{2,3},{3,2},{4,5},{5,4},{6,7},{7,6},{8,9},{9,8},{10,11... | collective-permute-start | bytes 30728 | tf_op jit(solution)/shard_map/ppermute | solution.py:31
  106.3 1.4 copy-start.11
  110.0 4.3 %collective-permute-start.16 = (bf16[25,40,320]{2,1,0:T(8,128)(2,1)S(1)}, bf16[25,40,320]{2,1,0:T(8,128)(2,1)S(1)}, u32[]{:S(2)}, u32[]{:S(2)}) collective-permute-start(bf16[25,40,320]{2,1,0:T(8,128)(2,1)S(1)} %get-tuple-element.176), channel_id=1, source_target_pairs={{0,8},{8,0},{1,9},{9,1},{2,10},{10,2},{3,11},{11,3},{4,12},{12,4},... | collective-permute-start | bytes 1920008 | tf_op jit(solution)/shard_map/ppermute | solution.py:31
  112.3 18.9 %collective-permute-start.10 = (bf16[3,8,40,320]{3,2,1,0:T(8,128)(2,1)S(1)}, bf16[3,8,40,320]{3,2,1,0:T(8,128)(2,1)S(1)}, u32[]{:S(2)}, u32[]{:S(2)}) collective-permute-start(bf16[3,8,40,320]{3,2,1,0:T(8,128)(2,1)S(1)} %get-tuple-element.167), channel_id=1, source_target_pairs={{0,2},{2,4},{4,6},{6,0},{1,3},{3,5},{5,7},{7,1},{8,10},{10,12},{12... | collective-permute-start | bytes 1843208 | tf_op jit(solution)/shard_map/ppermute | solution.py:35
  112.9 19.8 %collective-permute-start.11 = (bf16[3,8,40,320]{3,2,1,0:T(8,128)(2,1)S(1)}, bf16[3,8,40,320]{3,2,1,0:T(8,128)(2,1)S(1)}, u32[]{:S(2)}, u32[]{:S(2)}) collective-permute-start(bf16[3,8,40,320]{3,2,1,0:T(8,128)(2,1)S(1)} %get-tuple-element.168), channel_id=1, source_target_pairs={{0,6},{2,0},{4,2},{6,4},{1,7},{3,1},{5,3},{7,5},{8,14},{10,8},{12,... | collective-permute-start | bytes 1843208 | tf_op jit(solution)/shard_map/ppermute | solution.py:35
  115.2 8.0 %collective-permute-start.17 = (bf16[2,16,8,320]{3,2,1,0:T(8,128)(2,1)S(1)}, bf16[2,16,8,320]{3,2,1,0:T(8,128)(2,1)S(1)}, u32[]{:S(2)}, u32[]{:S(2)}) collective-permute-start(bf16[2,16,8,320]{3,2,1,0:T(8,128)(2,1)S(1)} %get-tuple-element.178), channel_id=1, source_target_pairs={{0,16},{16,32},{32,48},{48,0},{1,17},{17,33},{33,49},{49,1},{2,18}... | collective-permute-start | bytes 491528 | tf_op jit(solution)/shard_map/ppermute | solution.py:35
  117.1 7.8 %collective-permute-start.18 = (bf16[2,16,8,320]{3,2,1,0:T(8,128)(2,1)S(1)}, bf16[2,16,8,320]{3,2,1,0:T(8,128)(2,1)S(1)}, u32[]{:S(2)}, u32[]{:S(2)}) collective-permute-start(bf16[2,16,8,320]{3,2,1,0:T(8,128)(2,1)S(1)} %get-tuple-element.179), channel_id=1, source_target_pairs={{0,48},{16,0},{32,16},{48,32},{1,49},{17,1},{33,17},{49,33},{2,50}... | collective-permute-start | bytes 491528 | tf_op jit(solution)/shard_map/ppermute | solution.py:35
  118.5 10.1 %collective-permute-start.19 = (bf16[2,16,8,320]{3,2,1,0:T(8,128)(2,1)S(1)}, bf16[2,16,8,320]{3,2,1,0:T(8,128)(2,1)S(1)}, u32[]{:S(2)}, u32[]{:S(2)}) collective-permute-start(bf16[2,16,8,320]{3,2,1,0:T(8,128)(2,1)S(1)} %get-tuple-element.180), channel_id=1, source_target_pairs={{0,32},{16,48},{32,0},{48,16},{1,33},{17,49},{33,1},{49,17},{2,34}... | collective-permute-start | bytes 491528 | tf_op jit(solution)/shard_map/ppermute | solution.py:35
  129.4 23.9 %collective-permute-start.20 = (bf16[2,16,8,320]{3,2,1,0:T(8,128)(2,1)}, bf16[2,16,8,320]{3,2,1,0:T(8,128)(2,1)S(1)}, u32[]{:S(2)}, u32[]{:S(2)}) collective-permute-start(bf16[2,16,8,320]{3,2,1,0:T(8,128)(2,1)} %get-tuple-element.181), channel_id=1, source_target_pairs={{0,4},{2,6},{4,0},{6,2},{1,5},{3,7},{5,1},{7,3},{8,12},{10,14},{12... | collective-permute-start | bytes 491528 | tf_op jit(solution)/shard_map/ppermute | solution.py:35
  132.7 26.1 %copy-start.1 = (bf16[11,32,640]{2,1,0:T(8,128)(2,1)S(1)}, bf16[11,32,640]{2,1,0:T(8,128)(2,1)}, u32[]{:S(2)}) copy-start(bf16[11,32,640]{2,1,0:T(8,128)(2,1)} %copy-done) | copy-start | bytes 1351684
  132.7 26.1 %copy-start.5 = (bf16[11,32,640]{2,1,0:T(8,128)(2,1)S(1)}, bf16[11,32,640]{2,1,0:T(8,128)(2,1)}, u32[]{:S(2)}) copy-start(bf16[11,32,640]{2,1,0:T(8,128)(2,1)} %copy-done.4) | copy-start | bytes 1351684
  134.5 0.8 copy-start.12
  135.2 18.1 %collective-permute-start.12 = (bf16[2,16,8,320]{3,2,1,0:T(8,128)(2,1)}, bf16[2,16,8,320]{3,2,1,0:T(8,128)(2,1)S(1)}, u32[]{:S(2)}, u32[]{:S(2)}) collective-permute-start(bf16[2,16,8,320]{3,2,1,0:T(8,128)(2,1)} %get-tuple-element.170), channel_id=1, source_target_pairs={{0,16},{16,32},{32,48},{48,0},{1,17},{17,33},{33,49},{49,1},{2,18}... | collective-permute-start | bytes 491528 | tf_op jit(solution)/shard_map/ppermute | solution.py:35
  141.2 12.1 %collective-permute-start.13 = (bf16[2,16,8,320]{3,2,1,0:T(8,128)(2,1)}, bf16[2,16,8,320]{3,2,1,0:T(8,128)(2,1)S(1)}, u32[]{:S(2)}, u32[]{:S(2)}) collective-permute-start(bf16[2,16,8,320]{3,2,1,0:T(8,128)(2,1)} %get-tuple-element.171), channel_id=1, source_target_pairs={{0,48},{16,0},{32,16},{48,32},{1,49},{17,1},{33,17},{49,33},{2,50}... | collective-permute-start | bytes 491528 | tf_op jit(solution)/shard_map/ppermute | solution.py:35
  142.4 10.9 %collective-permute-start.14 = (bf16[2,16,8,320]{3,2,1,0:T(8,128)(2,1)}, bf16[2,16,8,320]{3,2,1,0:T(8,128)(2,1)S(1)}, u32[]{:S(2)}, u32[]{:S(2)}) collective-permute-start(bf16[2,16,8,320]{3,2,1,0:T(8,128)(2,1)} %get-tuple-element.172), channel_id=1, source_target_pairs={{0,32},{16,48},{32,0},{48,16},{1,33},{17,49},{33,1},{49,17},{2,34}... | collective-permute-start | bytes 491528 | tf_op jit(solution)/shard_map/ppermute | solution.py:35
  144.7 3.7 %collective-permute-start.21 = (f32[8,320]{1,0:T(8,128)S(1)}, f32[8,320]{1,0:T(8,128)S(1)}, u32[]{:S(2)}, u32[]{:S(2)}) collective-permute-start(f32[8,320]{1,0:T(8,128)S(1)} %get-tuple-element.182), channel_id=1, source_target_pairs={{0,2},{2,0},{4,6},{6,4},{1,3},{3,1},{5,7},{7,5},{8,10},{10,8},{12,... | collective-permute-start | bytes 30728 | tf_op jit(solution)/shard_map/ppermute | solution.py:477
  148.4 4.9 %collective-permute-start.22 = (f32[8,320]{1,0:T(8,128)S(1)}, f32[8,320]{1,0:T(8,128)S(1)}, u32[]{:S(2)}, u32[]{:S(2)}) collective-permute-start(f32[8,320]{1,0:T(8,128)S(1)} %add.58.gain), channel_id=1, source_target_pairs={{0,6},{6,0},{2,4},{4,2},{1,7},{7,1},{3,5},{5,3},{8,14},{14,8},{10,... | collective-permute-start | bytes 30728 | tf_op jit(solution)/shard_map/ppermute | solution.py:478
  153.3 1.0 copy-start.13
  155.1 6.3 %collective-permute-start.23 = (bf16[16,8,320]{2,1,0:T(8,128)(2,1)S(1)}, bf16[16,8,320]{2,1,0:T(8,128)(2,1)S(1)}, u32[]{:S(2)}, u32[]{:S(2)}) collective-permute-start(bf16[16,8,320]{2,1,0:T(8,128)(2,1)S(1)} %get-tuple-element.184), channel_id=1, source_target_pairs={{0,64},{64,0},{1,65},{65,1},{2,66},{66,2},{3,67},{67,3},{4,68},{68... | collective-permute-start | bytes 245768 | tf_op jit(solution)/shard_map/ppermute | solution.py:31
  166.1 14.7 %all-to-all-start = ((bf16[8,32,640]{2,1,0:T(8,128)(2,1)}), bf16[8,32,640]{2,1,0:T(8,128)(2,1)S(1)}, u32[]{:S(2)}, u32[]{:S(2)}) async-start(bf16[8,32,640]{2,1,0:T(8,128)(2,1)} %broadcast_select_fusion.3), calls=%async_computation | async-start | bytes 655360 | tf_op jit(solution)/shard_map/while/body/all_to_all | solution.py:492
  182.4 0.8 copy-start.16
